TPU v7x, 256 devices: a whole 4x4x8 slice. The times are simulated.
256 devices in a mesh: lat: 16 (over z, core), lon: 8 (over x, y_hi), ens: 2 (over y_lo).
Axes of the slice: x: 4, y: 4 (y_hi: 2, y_lo: 2; y = y_hi * 2 + y_lo), z: 8, core: 2. Of those that a mesh axis runs over, the one named last changes fastest.
Arguments:
- state: bfloat16 [4, 96, 192, 768], P('ens', 'lat', 'lon'), parts along dimension 0, may hold values from -6 to 6
- spec_weight1: float32 [2, 8, 96, 96], P(None, 'lon'), may hold values from -0.4375 to 0.4375
- spec_bias1: float32 [2, 8, 96], P(None, 'lon'), may hold values from -0.6 to 0.6
- spec_weight2: float32 [2, 8, 96, 96], P(None, 'lon'), may hold values from -0.4375 to 0.4375
- spec_bias2: float32 [2, 8, 96], P(None, 'lon'), may hold values from -0.12 to 0.12
- norm1_gain: float32 [768], replicated, may hold values from 0.5 to 1.5
- norm1_bias: float32 [768], replicated, may hold values from -0.6 to 0.6
- norm2_gain: float32 [768], replicated, may hold values from 0.5 to 1.5
- norm2_bias: float32 [768], replicated, may hold values from -0.6 to 0.6
- fc1_weight: bfloat16 [768, 3072], replicated, may hold values from -0.21875 to 0.21875
- fc1_bias: float32 [3072], replicated, may hold values from -0.6 to 0.6
- fc2_weight: bfloat16 [3072, 768], replicated, may hold values from -0.109375 to 0.109375
- fc2_bias: float32 [768], replicated, may hold values from -0.6 to 0.6
- cotangent: bfloat16 [4, 96, 192, 768], P('ens', 'lat', 'lon'), parts along dimension 0, may hold values from -6 to 6
Outputs:
- advanced: bfloat16 [4, 96, 192, 768], P('ens', 'lat', 'lon'), parts along dimension 0
- sensitivity: bfloat16 [4, 96, 192, 768], P('ens', 'lat', 'lon'), parts along dimension 0
There are 2 independent parts, one for each index of `ens`. A program takes and returns all parts, laid end to end along the dimension named above; an argument that names none is the same for every part. Nothing has to cross between parts.
All inputs are finite; a program needn't handle non-finite values.
Results may differ from a plain program's by a relative error of at most 0.0085.
Values may be sent and summed in bfloat16 or wider, within the bound.
No kernel may reach another device: no remote copies, remote signals or barrier semaphores. Data moves between devices by JAX's collectives and lax.ppermute only.
A program may use at most 128 MiB of HBM per device.

v0:
```python
import functools
import math

import jax
import jax.numpy as jnp
import numpy as np
from jax import lax
from jax.experimental import pallas as pl
from jax.experimental.pallas import tpu as pltpu
from jax.sharding import PartitionSpec as P

EPSILON = 1e-06
THRESHOLD = 0.01
LATS, LONS = 16, 8
HEIGHT, WIDTH, FEATURES, HIDDEN = 96, 192, 768, 3072
ROWS, COLS = HEIGHT // LATS, WIDTH // LONS
BLOCK = FEATURES // LONS
STATES = 2
GROUPS = STATES * ROWS
TOKENS = GROUPS * COLS
LANES = GROUPS * BLOCK
TILES = LANES // 128
WIRE = TILES * GROUPS
STRIDE = 109
CHUNK = 512
F32, BF16 = jnp.float32, jnp.bfloat16


def split_table(table):
    high = table.astype(BF16)
    return np.stack([high, (table - high.astype(np.float64)).astype(BF16)])


def width_tables():
    part, q, d = np.meshgrid(np.arange(2), np.arange(ROWS), np.arange(LATS), indexing="ij")
    part, freq = part.reshape(-1, 1), (q + ROWS * d).reshape(-1, 1)
    w = np.arange(WIDTH).reshape(1, -1)
    angle = 2.0 * math.pi * (freq * w % WIDTH) / WIDTH
    parity = np.where(w % 2 == 0, 1.0, -1.0)
    scale = 1.0 / math.sqrt(WIDTH)
    forward = np.where(part == 0, np.cos(angle), np.where(freq == 0, parity, -np.sin(angle)))
    twice = np.where(freq == 0, 1.0, 2.0)
    return forward * scale, (forward * twice * scale).T


def height_tables():
    p = np.arange(HEIGHT).reshape(-1, 1, 1)
    r = np.arange(ROWS).reshape(1, -1, 1)
    s = np.arange(LATS).reshape(1, 1, -1)
    angle = 2.0 * math.pi * (p * (ROWS * s + r) % HEIGHT) / HEIGHT
    c, n = np.cos(angle) / math.sqrt(HEIGHT), np.sin(angle) / math.sqrt(HEIGHT)
    zero = np.zeros_like(c)

    def join(rows):
        return np.concatenate([np.stack(row, axis=2).reshape(HEIGHT, -1) for row in rows], axis=0)

    plain = join([[c, n], [c, n], [-n, c], [n, -c]])
    packed = join([[c, zero], [zero, c], [-n, zero], [zero, -n]])

    def join_back(rows):
        return np.concatenate(
            [np.concatenate([v.reshape(HEIGHT, -1).T for v in row], axis=1) for row in rows], axis=0
        )

    h = 0.5
    plain_back = join_back([[h * c, h * c, -h * n, h * n], [h * n, h * n, h * c, -h * c]])
    packed_back = join_back([[c, zero, -n, zero], [zero, c, zero, -n]])
    return np.stack([plain, packed]), np.stack([plain_back, packed_back])


def dot(a, b):
    return lax.dot_general(a, b, (((1,), (0,)), ((), ())), preferred_element_type=F32)


def dot_t(a, b):
    return lax.dot_general(a, b, (((1,), (1,)), ((), ())), preferred_element_type=F32)


def lane_index(rows):
    return lax.broadcasted_iota(jnp.int32, (rows, 128), 1)


def unpack4(t0, t1, t2):
    lane = lane_index(t0.shape[0])
    b1 = jnp.where(lane < 32, pltpu.roll(t0, 32, 1), pltpu.roll(t1, 32, 1))
    b2 = jnp.where(lane < 64, pltpu.roll(t1, 64, 1), pltpu.roll(t2, 64, 1))
    return t0, b1, b2, pltpu.roll(t2, 96, 1)


def pack4(b0, b1, b2, b3):
    lane = lane_index(b0.shape[0])
    r1, r2, r3 = pltpu.roll(b1, 96, 1), pltpu.roll(b2, 64, 1), pltpu.roll(b3, 32, 1)
    return (
        jnp.where(lane < 96, b0, r1),
        jnp.where(lane < 64, r1, r2),
        jnp.where(lane < 32, r2, r3),
    )


def norm(values):
    average = jnp.mean(values, axis=-1, keepdims=True)
    centred = values - average
    inverse = lax.rsqrt(jnp.mean(centred * centred, axis=-1, keepdims=True) + EPSILON)
    return centred * inverse, inverse


def norm_backward(gradient, gain, normed, inverse):
    scaled = gradient * gain
    return inverse * (
        scaled
        - jnp.mean(scaled, axis=-1, keepdims=True)
        - normed * jnp.mean(scaled * normed, axis=-1, keepdims=True)
    )


def gelu_pair(values):
    cumulative = 0.5 * (1.0 + lax.erf(values * 0.7071067811865476))
    density = jnp.exp(-0.5 * values * values) * 0.3989422804014327
    return values * cumulative, cumulative + values * density


def scatter_blocks(blocks, pair, values):
    tiles = [values[:, 128 * i : 128 * i + 128] for i in range(6)]
    for j, b in enumerate((*unpack4(*tiles[:3]), *unpack4(*tiles[3:]))):
        blocks[j, 2 * pair] = b[:COLS]
        blocks[j, 2 * pair + 1] = b[COLS:]


def send_blocks(blocks, wire):
    for j in range(LONS):
        for g in range(GROUPS // 4):
            tiles = pack4(*(blocks[j, 4 * g + n] for n in range(4)))
            for i, t in enumerate(tiles):
                at = 384 * g + 128 * i
                wire[j, :, at : at + 128] = t.astype(BF16)


def receive_blocks(wire, blocks):
    for j in range(LONS):
        for g in range(GROUPS // 4):
            at = 384 * g
            tiles = [wire[j, :, at + 128 * i : at + 128 * i + 128].astype(F32) for i in range(3)]
            for n, b in enumerate(unpack4(*tiles)):
                blocks[j, 4 * g + n] = b


def gather_blocks(blocks, pair):
    parts = [jnp.concatenate([blocks[j, 2 * pair], blocks[j, 2 * pair + 1]], axis=0) for j in range(LONS)]
    return jnp.concatenate([*pack4(*parts[:4]), *pack4(*parts[4:])], axis=1)


def begin_kernel(state, gain, shift, lowered, wire, blocks):
    for pair in range(GROUPS // 2):
        rows = slice(48 * pair, 48 * pair + 48)
        normed, _ = norm(state[rows, :].astype(F32))
        value = (normed * gain[...] + shift[...]).astype(BF16)
        lowered[rows, :] = value
        scatter_blocks(blocks, pair, value.astype(F32))
    send_blocks(blocks, wire)


def wire_out(scratch, wire):
    for d in range(LATS):
        wire[d] = scratch[STRIDE * d : STRIDE * d + WIRE, :].astype(BF16)


def wire_in(wire, scratch):
    for d in range(LATS):
        scratch[STRIDE * d : STRIDE * d + WIRE, :] = wire[d].astype(F32)


def peers(row):
    return pl.ds(row, LATS, stride=STRIDE)


def width_kernel(field, table, wire, scratch):
    product = dot(table[0], field[...]) + dot(table[1], field[...])
    for e in range(GROUPS):
        for i in range(TILES):
            scratch[peers(GROUPS * i + e), :] = product[16 * e : 16 * e + 16, 128 * i : 128 * i + 128]
    wire_out(scratch, wire)


def width_back_kernel(wire, table, field, scratch, gathered):
    wire_in(wire, scratch)
    for e in range(GROUPS):
        for i in range(TILES):
            piece = scratch[peers(GROUPS * i + e), :]
            gathered[16 * e : 16 * e + 16, 128 * i : 128 * i + 128] = piece.astype(BF16)
    field[...] = (dot(table[0], gathered[...]) + dot(table[1], gathered[...])).astype(BF16)


def spectrum_in(wire, scratch, columns):
    wire_in(wire, scratch)
    for part in range(2):
        for q in range(ROWS):
            e = ROWS * part + q
            for g in range(GROUPS // 4):
                tiles = [scratch[peers(GROUPS * (3 * g + i) + e), :] for i in range(3)]
                for n, b in enumerate(unpack4(*tiles)):
                    state, r = divmod(4 * g + n, ROWS)
                    at = 16 * (2 * r + part)
                    columns[q, at : at + 16, 128 * state : 128 * state + 128] = b.astype(BF16)


def spectrum_out(backs, scratch, wire):
    for part in range(2):
        for q in range(ROWS):
            e = ROWS * part + q
            for g in range(GROUPS // 4):
                blocks = []
                for n in range(4):
                    state, r = divmod(4 * g + n, ROWS)
                    at = 16 * (ROWS * part + r)
                    blocks.append(backs[q, at : at + 16, 128 * state : 128 * state + 128])
                for i, t in enumerate(pack4(*blocks)):
                    scratch[peers(GROUPS * (3 * g + i) + e), :] = t
    wire_out(scratch, wire)


def build_weight(weight, square, out):
    square[...] = jnp.zeros_like(square)
    square[0:BLOCK, 0:BLOCK] = weight[0]
    square[0:BLOCK, 128 : 128 + BLOCK] = weight[1]
    square[128 : 128 + BLOCK, 0:BLOCK] = -weight[1]
    square[128 : 128 + BLOCK, 128 : 128 + BLOCK] = weight[0]
    full = square[...]
    high = full.astype(BF16)
    out[0] = high
    out[1] = (full - high.astype(F32)).astype(BF16)


def build_bias(bias, out):
    out[...] = jnp.zeros_like(out)
    out[0:1, 0:BLOCK] = bias[0:1, :]
    out[0:1, 128 : 128 + BLOCK] = bias[1:2, :]


def to_points(spectrum):
    half = 2 * HEIGHT
    return jnp.concatenate(
        [
            jnp.concatenate([spectrum[:half, at : at + 128], spectrum[half:, at : at + 128]], axis=1)
            for at in (0, 128)
        ],
        axis=0,
    )


def from_points(points):
    half = 2 * HEIGHT
    return jnp.concatenate(
        [
            jnp.concatenate([points[at : at + half, :128], points[at : at + half, 128:]], axis=0)
            for at in (0, half)
        ],
        axis=1,
    )


def filter_kernel(
    wire, forward, inverse, weight1, bias1, weight2, bias2,
    wire_back, slopes, squares,
    scratch, columns, backs, square, w1, w2, c1, c2,
):
    build_weight(weight1, square, w1)
    build_weight(weight2, square, w2)
    build_bias(bias1, c1)
    build_bias(bias2, c2)
    spectrum_in(wire, scratch, columns)
    first = jnp.where(lax.axis_index("lat") == 0, 1, 0)

    def column(q, which):
        field = columns[q]
        spectrum = dot(forward[which, 0], field) + dot(forward[which, 1], field)
        points = to_points(spectrum.astype(BF16))
        pre = dot(points, w1[0]) + dot(points, w1[1]) + c1[...]
        active, slope = gelu_pair(pre)
        slopes[q] = slope.astype(BF16)
        active = active.astype(BF16)
        post = dot(active, w2[0]) + dot(active, w2[1]) + c2[...]
        bend = jnp.tanh(post * (1.0 / THRESHOLD))
        squares[q] = (bend * bend).astype(BF16)
        shrunk = from_points((post - THRESHOLD * bend).astype(BF16))
        backs[q] = dot(inverse[which, 0], shrunk) + dot(inverse[which, 1], shrunk)

    column(0, first)

    @pl.loop(1, ROWS)
    def _(q):
        column(q, 0)

    spectrum_out(backs, scratch, wire_back)


def adjoint_kernel(
    wire, forward, inverse, weight1, weight2, slopes, squares,
    wire_back,
    scratch, columns, backs, square, w1, w2,
):
    build_weight(weight1, square, w1)
    build_weight(weight2, square, w2)
    spectrum_in(wire, scratch, columns)
    first = jnp.where(lax.axis_index("lat") == 0, 1, 0)

    def column(q, which):
        field = columns[q]
        spectrum = dot(forward[which, 0], field) + dot(forward[which, 1], field)
        points = (to_points(spectrum) * squares[q].astype(F32)).astype(BF16)
        active = dot_t(points, w2[0]) + dot_t(points, w2[1])
        pre = (active * slopes[q].astype(F32)).astype(BF16)
        result = dot_t(pre, w1[0]) + dot_t(pre, w1[1])
        shrunk = from_points(result.astype(BF16))
        backs[q] = dot(inverse[which, 0], shrunk) + dot(inverse[which, 1], shrunk)

    column(0, first)

    @pl.loop(1, ROWS)
    def _(q):
        column(q, 0)

    spectrum_out(backs, scratch, wire_back)


def token_kernel(
    wire, state, lowered, cotangent, gain, shift, fc1, bias1, fc2, bias2,
    advanced, grad_mixed, wire_next,
    blocks, mixed, rows_in, total, grad_total,
):
    step = pl.program_id(0)

    @pl.when(step == 0)
    def _():
        receive_blocks(wire, blocks)
        for pair in range(GROUPS // 2):
            rows = slice(48 * pair, 48 * pair + 48)
            value = gather_blocks(blocks, pair)
            value = value + lowered[rows, :].astype(F32) + state[rows, :].astype(F32)
            value = value.astype(BF16)
            mixed[rows, :] = value
            normed, _ = norm(value.astype(F32))
            rows_in[rows, :] = (normed * gain[...] + shift[...]).astype(BF16)
        total[...] = jnp.zeros_like(total)
        grad_total[...] = jnp.zeros_like(grad_total)

    hidden_pre = dot(rows_in[...], fc1[...]) + bias1[...]
    hidden, slope = gelu_pair(hidden_pre)
    total[...] += dot(hidden.astype(BF16), fc2[...])
    grad_hidden = dot_t(cotangent[...], fc2[...])
    grad_pre = (grad_hidden * slope).astype(BF16)
    grad_total[...] += dot_t(grad_pre, fc1[...])

    @pl.when(step == pl.num_programs(0) - 1)
    def _():
        for pair in range(GROUPS // 2):
            rows = slice(48 * pair, 48 * pair + 48)
            value = mixed[rows, :].astype(F32)
            normed, scale = norm(value)
            advanced[rows, :] = (total[rows, :] + bias2[...] + value).astype(BF16)
            grad = cotangent[rows, :].astype(F32) + norm_backward(
                grad_total[rows, :], gain[...], normed, scale
            )
            grad = grad.astype(BF16)
            grad_mixed[rows, :] = grad
            scatter_blocks(blocks, pair, grad.astype(F32))
        send_blocks(blocks, wire_next)


def finish_kernel(wire, grad_mixed, state, gain, sensitivity, blocks):
    receive_blocks(wire, blocks)
    for pair in range(GROUPS // 2):
        rows = slice(48 * pair, 48 * pair + 48)
        grad = grad_mixed[rows, :].astype(F32)
        normed, scale = norm(state[rows, :].astype(F32))
        grad_lowered = gather_blocks(blocks, pair) + grad
        sensitivity[rows, :] = (grad + norm_backward(grad_lowered, gain[...], normed, scale)).astype(BF16)


def array(shape, dtype=BF16):
    return jax.ShapeDtypeStruct(shape, dtype)


LON_WIRE = array((LONS, COLS, LANES))
LAT_WIRE = array((LATS, WIRE, 128))
BLOCKS = pltpu.VMEM((LONS, GROUPS, COLS, 128), F32)
PEERS = pltpu.VMEM((LATS * STRIDE + 7, 128), F32)
COLUMNS = pltpu.VMEM((ROWS, 2 * HEIGHT, 256), BF16)
BACKS = pltpu.VMEM((ROWS, 2 * HEIGHT, 256), F32)
SQUARE = pltpu.VMEM((256, 256), F32)
WEIGHT = pltpu.VMEM((2, 256, 256), BF16)
POINTS = array((ROWS, 4 * HEIGHT, 256))
PARAMS = pltpu.CompilerParams(vmem_limit_bytes=48 * 1024 * 1024)


def call(kernel, out_shape, scratch, name):
    return pl.pallas_call(kernel, out_shape=out_shape, scratch_shapes=scratch, name=name, compiler_params=PARAMS)


def exchange(value, axis):
    return lax.all_to_all(value, axis, split_axis=0, concat_axis=0, tiled=True)


def to_lat(wire, table):
    field = exchange(wire, "lon").reshape(WIDTH, LANES)
    wire = call(width_kernel, LAT_WIRE, [PEERS], "width")(field, table)
    return exchange(wire, "lat")


def to_lon(wire, table):
    wire = exchange(wire, "lat")
    field = call(
        width_back_kernel, array((WIDTH, LANES)), [PEERS, pltpu.VMEM((WIDTH, LANES), BF16)], "width_back"
    )(wire, table)
    return exchange(field.reshape(LON_WIRE.shape), "lon")


def shards(
    state, spec_weight1, spec_bias1, spec_weight2, spec_bias2, norm1_gain, norm1_bias, norm2_gain, norm2_bias,
    fc1_weight, fc1_bias, fc2_weight, fc2_bias, cotangent,
):
    width_forward, width_inverse = (jnp.asarray(split_table(t)) for t in width_tables())
    height_forward, height_inverse = (
        jnp.asarray(np.stack([split_table(v) for v in t])) for t in height_tables()
    )
    tokens = state.reshape(TOKENS, FEATURES)
    cot = cotangent.reshape(TOKENS, FEATURES)
    gain1, shift1 = norm1_gain.reshape(1, -1), norm1_bias.reshape(1, -1)
    gain2, shift2 = norm2_gain.reshape(1, -1), norm2_bias.reshape(1, -1)
    weight1, weight2 = spec_weight1.reshape(2, BLOCK, BLOCK), spec_weight2.reshape(2, BLOCK, BLOCK)
    bias1, bias2 = spec_bias1.reshape(2, BLOCK), spec_bias2.reshape(2, BLOCK)

    token_array = array((TOKENS, FEATURES))
    lowered, wire = call(begin_kernel, (token_array, LON_WIRE), [BLOCKS], "begin")(tokens, gain1, shift1)
    wire = to_lat(wire, width_forward)
    bias = pltpu.VMEM((1, 256), F32)
    wire, slopes, squares = call(
        filter_kernel,
        (LAT_WIRE, POINTS, POINTS),
        [PEERS, COLUMNS, BACKS, SQUARE, WEIGHT, WEIGHT, bias, bias],
        "filter",
    )(wire, height_forward, height_inverse, weight1, bias1, weight2, bias2)
    wire = to_lon(wire, width_inverse)

    whole = lambda *shape: pl.BlockSpec(shape, lambda i: (0,) * len(shape))
    token_spec = whole(TOKENS, FEATURES)
    wire_spec = whole(*LON_WIRE.shape)
    advanced, grad_mixed, wire = pl.pallas_call(
        token_kernel,
        grid=(HIDDEN // CHUNK,),
        in_specs=[
            wire_spec,
            token_spec,
            token_spec,
            token_spec,
            whole(1, FEATURES),
            whole(1, FEATURES),
            pl.BlockSpec((FEATURES, CHUNK), lambda i: (0, i)),
            pl.BlockSpec((1, CHUNK), lambda i: (0, i)),
            pl.BlockSpec((CHUNK, FEATURES), lambda i: (i, 0)),
            whole(1, FEATURES),
        ],
        out_specs=(token_spec, token_spec, wire_spec),
        out_shape=(token_array, token_array, LON_WIRE),
        scratch_shapes=[
            BLOCKS,
            pltpu.VMEM((TOKENS, FEATURES), BF16),
            pltpu.VMEM((TOKENS, FEATURES), BF16),
            pltpu.VMEM((TOKENS, FEATURES), F32),
            pltpu.VMEM((TOKENS, FEATURES), F32),
        ],
        name="token",
        compiler_params=PARAMS,
    )(
        wire, tokens, lowered, cot, gain2, shift2,
        fc1_weight, fc1_bias.reshape(1, -1), fc2_weight, fc2_bias.reshape(1, -1),
    )

    wire = to_lat(wire, width_forward)
    wire = call(adjoint_kernel, LAT_WIRE, [PEERS, COLUMNS, BACKS, SQUARE, WEIGHT, WEIGHT], "adjoint")(
        wire, height_forward, height_inverse, weight1, weight2, slopes, squares
    )
    wire = to_lon(wire, width_inverse)
    sensitivity = call(finish_kernel, token_array, [BLOCKS], "finish")(wire, grad_mixed, tokens, gain1)
    return advanced.reshape(state.shape), sensitivity.reshape(state.shape)


def solution(mesh):
    field = P("ens", "lat", "lon", None)
    block, bias = P(None, "lon", None, None), P(None, "lon", None)
    return jax.shard_map(
        shards,
        mesh=mesh,
        in_specs=(field, block, bias, block, bias, *[P()] * 8, field),
        out_specs=(field, field),
        check_vma=False,
    )
```

profile of v0, /device:TPU:1, one launch (start us, length us, event | category | flops | bytes accessed | tf_op | source)
XLA Modules:
  0.0 184.7 jit_solution(4504440128967292243)
XLA Ops:
  0.6 0.7 reshape.59.gain
  1.3 0.7 reshape.60.shift
  2.0 1.0 copy-done
  3.1 1.2 begin.1
  4.2 0.0 copy-start.10
  4.3 16.3 %all_to_all.40 = bf16[8,24,1152]{2,1,0:T(8,128)(2,1)S(1)} all-to-all(bf16[8,24,1152]{2,1,0:T(8,128)(2,1)S(1)} %get-tuple-element.10), channel_id=1, replica_groups=mesh['lat'=16,'lon'=8,'ens'=2] {'lon'}, dimensions={0} | all-to-all | bytes 884736 | tf_op jit(solution)/shard_map/all_to_all | solution.py:400
  20.5 0.9 copy-done.6
  21.5 0.4 width.2
  21.9 26.5 %all_to_all.41.wire = bf16[16,108,128]{2,1,0:T(8,128)(2,1)S(1)} all-to-all(bf16[16,108,128]{2,1,0:T(8,128)(2,1)S(1)} %width.2), channel_id=1, replica_groups=mesh['lat'=16,'lon'=8,'ens'=2] {'lat'}, dimensions={0} | all-to-all | bytes 884736 | tf_op jit(solution)/shard_map/all_to_all | solution.py:400
  48.4 1.1 copy-done.2
  49.6 1.1 copy-done.4
  50.6 0.9 copy-done.12
  51.5 0.9 copy-done.14
  52.4 0.7 copy-done.17
  53.1 0.7 copy-done.18
  53.8 8.0 %filter.1 = (bf16[16,108,128]{2,1,0:T(8,128)(2,1)S(1)}, bf16[6,384,256]{2,1,0:T(8,128)(2,1)S(1)}, bf16[6,384,256]{2,1,0:T(8,128)(2,1)S(1)}) custom-call(bf16[16,108,128]{2,1,0:T(8,128)(2,1)S(1)} %all_to_all.41.wire, bf16[2,2,384,192]{3,2,1,0:T(8,128)(2,1)S(1)} %copy-done.2, bf16[2,2,192,384]{3,2,1,0:T(8,128)(2,1)S(1)} %copy-done.4, ...), custom_call_target="tpu_custom_call" | custom-call | tf_op jit(solution)/shard_map/filter/pallas_call | solution.py:436
  61.8 18.6 %all_to_all.42.wire = bf16[16,108,128]{2,1,0:T(8,128)(2,1)S(1)} all-to-all(bf16[16,108,128]{2,1,0:T(8,128)(2,1)S(1)} %get-tuple-element.11), channel_id=1, replica_groups=mesh['lat'=16,'lon'=8,'ens'=2] {'lat'}, dimensions={0} | all-to-all | bytes 884736 | tf_op jit(solution)/shard_map/all_to_all | solution.py:400
  80.3 1.3 width_back.2
  81.6 3.5 %all-to-all-start.3 = ((bf16[8,24,1152]{2,1,0:T(8,128)(2,1)}), bf16[8,24,1152]{2,1,0:T(8,128)(2,1)S(1)}, u32[]{:S(2)}, u32[]{:S(2)}) async-start(bf16[8,24,1152]{2,1,0:T(8,128)(2,1)} %bitcast.6), calls=%async_computation.3 | async-start | bytes 884736 | tf_op jit(solution)/shard_map/all_to_all | solution.py:400
  85.2 9.5 %all-to-all-done.3.wire = bf16[8,24,1152]{2,1,0:T(8,128)(2,1)S(1)} async-done(((bf16[8,24,1152]{2,1,0:T(8,128)(2,1)}), bf16[8,24,1152]{2,1,0:T(8,128)(2,1)S(1)}, u32[]{:S(2)}, u32[]{:S(2)}) %all-to-all-start.3) | async-done | bytes 442400 | tf_op jit(solution)/shard_map/all_to_all | solution.py:400
  94.7 1.0 copy-done.9
  95.7 1.0 copy-done.11
  96.7 0.0 copy-start.15
  96.7 13.2 %token_.1 = (bf16[288,768]{1,0:T(8,128)(2,1)}, bf16[288,768]{1,0:T(8,128)(2,1)S(1)}, bf16[8,24,1152]{2,1,0:T(8,128)(2,1)S(1)}) custom-call(bf16[8,24,1152]{2,1,0:T(8,128)(2,1)S(1)} %all-to-all-done.3.wire, bf16[288,768]{1,0:T(8,128)(2,1)S(1)} %bitcast.14, bf16[288,768]{1,0:T(8,128)(2,1)S(1)} %copy-done.11, bf16[288,768]{1,0:T(8,128)(2,1)S(1)} %bitcast.19, ...), custom_call_target="tpu_custom_call" | custom-call | tf_op jit(solution)/shard_map/token/pallas_call | solution.py:447
  109.9 12.7 %all_to_all.43 = bf16[8,24,1152]{2,1,0:T(8,128)(2,1)S(1)} all-to-all(bf16[8,24,1152]{2,1,0:T(8,128)(2,1)S(1)} %get-tuple-element.14), channel_id=1, replica_groups=mesh['lat'=16,'lon'=8,'ens'=2] {'lon'}, dimensions={0} | all-to-all | bytes 884736 | tf_op jit(solution)/shard_map/all_to_all | solution.py:400
  122.6 0.4 width.3
  123.0 20.1 %all_to_all.44.wire = bf16[16,108,128]{2,1,0:T(8,128)(2,1)S(1)} all-to-all(bf16[16,108,128]{2,1,0:T(8,128)(2,1)S(1)} %width.3), channel_id=1, replica_groups=mesh['lat'=16,'lon'=8,'ens'=2] {'lat'}, dimensions={0} | all-to-all | bytes 884736 | tf_op jit(solution)/shard_map/all_to_all | solution.py:400
  143.2 7.4 %adjoint.1 = bf16[16,108,128]{2,1,0:T(8,128)(2,1)S(1)} custom-call(bf16[16,108,128]{2,1,0:T(8,128)(2,1)S(1)} %all_to_all.44.wire, bf16[2,2,384,192]{3,2,1,0:T(8,128)(2,1)S(1)} %copy-done.3, bf16[2,2,192,384]{3,2,1,0:T(8,128)(2,1)S(1)} %copy-done.5, f32[2,96,96]{2,1,0:T(8,128)S(1)} %bitcast.21, f32[2,96,96]{2,1,0:T(8,128)S(1)} %bitcast.23, ...), custom_call_target="tpu_custom_call" | custom-call | tf_op jit(solution)/shard_map/adjoint/pallas_call | solution.py:479
  150.5 18.6 %all_to_all.45.wire = bf16[16,108,128]{2,1,0:T(8,128)(2,1)S(1)} all-to-all(bf16[16,108,128]{2,1,0:T(8,128)(2,1)S(1)} %adjoint.1), channel_id=1, replica_groups=mesh['lat'=16,'lon'=8,'ens'=2] {'lat'}, dimensions={0} | all-to-all | bytes 884736 | tf_op jit(solution)/shard_map/all_to_all | solution.py:400
  169.1 0.5 width_back.3
  169.6 12.8 %all_to_all.46.wire = bf16[8,24,1152]{2,1,0:T(8,128)(2,1)S(1)} all-to-all(bf16[8,24,1152]{2,1,0:T(8,128)(2,1)S(1)} %bitcast.17), channel_id=1, replica_groups=mesh['lat'=16,'lon'=8,'ens'=2] {'lon'}, dimensions={0} | all-to-all | bytes 884736 | tf_op jit(solution)/shard_map/all_to_all | solution.py:400
  182.4 2.3 %finish.1 = bf16[288,768]{1,0:T(8,128)(2,1)} custom-call(bf16[8,24,1152]{2,1,0:T(8,128)(2,1)S(1)} %all_to_all.46.wire, bf16[288,768]{1,0:T(8,128)(2,1)S(1)} %get-tuple-element.17.grad_mixed, bf16[288,768]{1,0:T(8,128)(2,1)S(1)} %bitcast.15, f32[1,768]{1,0:T(1,128)S(1)} %reshape.59.gain), custom_call_target="tpu_custom_call" | custom-call | tf_op jit(solution)/shard_map/finish/pallas_call | solution.py:483
  (35 shorter events, 0.1 us)
Async XLA Ops:
  0.6 94.1 %copy-start.16 = (f32[3072]{0:T(1024)S(1)}, f32[3072]{0:T(1024)}, u32[]{:S(2)}) copy-start(f32[3072]{0:T(1024)} %param.28) | copy-start | bytes 36868
  2.0 1.0 copy-start
  3.0 77.3 %copy-start.8 = (bf16[2,192,192]{2,1,0:T(8,128)(2,1)S(1)}, bf16[2,192,192]{2,1,0:T(8,128)(2,1)}, u32[]{:S(2)}) copy-start(bf16[2,192,192]{2,1,0:T(8,128)(2,1)} %constant.9.clone.table) | copy-start | bytes 442372
  3.0 82.1 %copy-start.19 = (f32[768]{0:T(1024)S(1)}, f32[768]{0:T(1024)}, u32[]{:S(2)}) copy-start(f32[768]{0:T(1024)} %param.25) | copy-start | bytes 9220
  3.0 82.1 %copy-start.20 = (f32[768]{0:T(1024)S(1)}, f32[768]{0:T(1024)}, u32[]{:S(2)}) copy-start(f32[768]{0:T(1024)} %param.26) | copy-start | bytes 9220
  3.0 82.1 %copy-start.21 = (f32[768]{0:T(1024)S(1)}, f32[768]{0:T(1024)}, u32[]{:S(2)}) copy-start(f32[768]{0:T(1024)} %param.30) | copy-start | bytes 9220
  3.0 91.6 %copy-start.1 = (bf16[2,6,24,768]{3,2,1,0:T(8,128)(2,1)S(1)}, bf16[2,6,24,768]{3,2,1,0:T(8,128)(2,1)}, u32[]{:S(2)}) copy-start(bf16[2,6,24,768]{3,2,1,0:T(8,128)(2,1)} %param.18) | copy-start | bytes 1327108
  4.2 44.2 %copy-start.10 = (bf16[288,768]{1,0:T(8,128)(2,1)}, bf16[288,768]{1,0:T(8,128)(2,1)S(1)}, u32[]{:S(2)}) copy-start(bf16[288,768]{1,0:T(8,128)(2,1)S(1)} %get-tuple-element.12.lowered) | copy-start | bytes 1327108
  20.5 0.9 copy-start.6
  48.4 1.1 copy-start.2
  49.6 1.1 copy-start.4
  50.6 0.9 copy-start.12
  51.5 0.9 copy-start.14
  52.4 0.7 copy-start.17
  53.1 0.7 copy-start.18
  81.6 13.1 %all-to-all-start.3 = ((bf16[8,24,1152]{2,1,0:T(8,128)(2,1)}), bf16[8,24,1152]{2,1,0:T(8,128)(2,1)S(1)}, u32[]{:S(2)}, u32[]{:S(2)}) async-start(bf16[8,24,1152]{2,1,0:T(8,128)(2,1)} %bitcast.6), calls=%async_computation.3 | async-start | bytes 884736 | tf_op jit(solution)/shard_map/all_to_all | solution.py:400
  94.7 1.0 copy-start.9
  95.7 1.0 copy-start.11
  96.7 25.9 %copy-start.7 = (bf16[2,192,192]{2,1,0:T(8,128)(2,1)S(1)}, bf16[2,192,192]{2,1,0:T(8,128)(2,1)}, u32[]{:S(2)}) copy-start(bf16[2,192,192]{2,1,0:T(8,128)(2,1)} %constant.8.clone.table) | copy-start | bytes 442372
  96.7 46.4 %copy-start.3 = (bf16[2,2,384,192]{3,2,1,0:T(8,128)(2,1)S(1)}, bf16[2,2,384,192]{3,2,1,0:T(8,128)(2,1)}, u32[]{:S(2)}) copy-start(bf16[2,2,384,192]{3,2,1,0:T(8,128)(2,1)} %constant.10.clone.forward) | copy-start | bytes 1769476
  96.7 46.4 %copy-start.5 = (bf16[2,2,192,384]{3,2,1,0:T(8,128)(2,1)S(1)}, bf16[2,2,192,384]{3,2,1,0:T(8,128)(2,1)}, u32[]{:S(2)}) copy-start(bf16[2,2,192,384]{3,2,1,0:T(8,128)(2,1)} %constant.11.clone.inverse) | copy-start | bytes 1769476
  96.7 46.4 %copy-start.13 = (f32[2,1,96,96]{3,2,1,0:T(8,128)S(1)}, f32[2,1,96,96]{3,2,1,0:T(8,128)}, u32[]{:S(2)}) copy-start(f32[2,1,96,96]{3,2,1,0:T(8,128)} %param.19) | copy-start | bytes 221188
  96.7 46.4 %copy-start.15 = (f32[2,1,96,96]{3,2,1,0:T(8,128)S(1)}, f32[2,1,96,96]{3,2,1,0:T(8,128)}, u32[]{:S(2)}) copy-start(f32[2,1,96,96]{3,2,1,0:T(8,128)} %param.21) | copy-start | bytes 221188
where the time goes:
time: 186 us; the launch traced here: 185 us
  blocking collectives  126 us (68%)
  Pallas kernels  34.6 us (19%)
  local copies, waits for them, and re-layouts  10.8 us (6%)
  waiting for transfers between devices  9.51 us (5%)
  starting transfers between devices  3.47 us (2%)
    all_to_all x7, blocking collectives, exchange(): return lax.all_to_all(value, axis, split_axis=0, concat_axis=0, tiled=True)  126 us
    pallas_call x1, Pallas kernels, shards(): pl.pallas_call(token_kernel, grid=(HIDDEN // CHUNK,), in_specs=[wire_spec...  13.2 us
    all_to_all x1, waiting for transfers between devices, exchange(): return lax.all_to_all(value, axis, split_axis=0, concat_axis=0, tiled=True)  9.51 us
    unnamed x44, local copies, waits for them, and re-layouts  9.36 us
    pallas_call x1, Pallas kernels, shards(): call(filter_kernel, (LAT_WIRE, POINTS, POINTS), [PEERS, COLUMNS, BACKS, S...  7.98 us
    pallas_call x1, Pallas kernels, shards(): call(adjoint_kernel, LAT_WIRE, [PEERS, COLUMNS, BACKS, SQUARE, WEIGHT, WE...  7.37 us
  transfers between devices with their start and end apart: 1, of which 1 were waited for; matrix products, arithmetic and copies ran while one was open for 0% of the time, Pallas kernels for 0%

commit v1 on v0

--- a/solution.py
+++ b/solution.py
@@ -1,4 +1,3 @@
-import functools
 import math
 
 import jax
@@ -23,6 +22,8 @@
 WIRE = TILES * GROUPS
 STRIDE = 109
 CHUNK = 512
+CHUNKS = HIDDEN // CHUNK
+UNROLL = 2
 F32, BF16 = jnp.float32, jnp.bfloat16
 
 
@@ -40,7 +41,7 @@
     scale = 1.0 / math.sqrt(WIDTH)
     forward = np.where(part == 0, np.cos(angle), np.where(freq == 0, parity, -np.sin(angle)))
     twice = np.where(freq == 0, 1.0, 2.0)
-    return forward * scale, (forward * twice * scale).T
+    return split_table(forward * scale), split_table((forward * twice * scale).T)
 
 
 def height_tables():
@@ -65,7 +66,7 @@
     h = 0.5
     plain_back = join_back([[h * c, h * c, -h * n, h * n], [h * n, h * n, h * c, -h * c]])
     packed_back = join_back([[c, zero, -n, zero], [zero, c, zero, -n]])
-    return np.stack([plain, packed]), np.stack([plain_back, packed_back])
+    return tuple(np.stack([split_table(t) for t in pair]) for pair in ((plain, packed), (plain_back, packed_back)))
 
 
 def dot(a, b):
@@ -97,6 +98,10 @@
     )
 
 
+def row(vector):
+    return vector[...].reshape(1, -1)
+
+
 def norm(values):
     average = jnp.mean(values, axis=-1, keepdims=True)
     centred = values - average
@@ -149,14 +154,31 @@
     return jnp.concatenate([*pack4(*parts[:4]), *pack4(*parts[4:])], axis=1)
 
 
-def begin_kernel(state, gain, shift, lowered, wire, blocks):
+def fetch(sem, *pairs):
+    copies = [pltpu.make_async_copy(source, target, sem.at[n]) for n, (source, target) in enumerate(pairs)]
+    for c in copies:
+        c.start()
+
+    def wait(*numbers):
+        for n in numbers:
+            copies[n].wait()
+
+    return wait
+
+
+def begin_kernel(states, gains, shifts, lowereds, wire, state, gain, shift, lowered, blocks, sem):
+    wait = fetch(sem, (states, state), (gains, gain), (shifts, shift))
+    wait(0, 1, 2)
+    gain, shift = row(gain), row(shift)
     for pair in range(GROUPS // 2):
         rows = slice(48 * pair, 48 * pair + 48)
         normed, _ = norm(state[rows, :].astype(F32))
-        value = (normed * gain[...] + shift[...]).astype(BF16)
+        value = (normed * gain + shift).astype(BF16)
         lowered[rows, :] = value
         scatter_blocks(blocks, pair, value.astype(F32))
+    keep = fetch(sem, (lowered, lowereds))
     send_blocks(blocks, wire)
+    keep(0)
 
 
 def wire_out(scratch, wire):
@@ -173,7 +195,8 @@
     return pl.ds(row, LATS, stride=STRIDE)
 
 
-def width_kernel(field, table, wire, scratch):
+def width_kernel(field, tables, wire, scratch, table, sem):
+    fetch(sem, (tables, table))(0)
     product = dot(table[0], field[...]) + dot(table[1], field[...])
     for e in range(GROUPS):
         for i in range(TILES):
@@ -181,12 +204,14 @@
     wire_out(scratch, wire)
 
 
-def width_back_kernel(wire, table, field, scratch, gathered):
+def width_back_kernel(wire, tables, field, scratch, gathered, table, sem):
+    wait = fetch(sem, (tables, table))
     wire_in(wire, scratch)
     for e in range(GROUPS):
         for i in range(TILES):
             piece = scratch[peers(GROUPS * i + e), :]
             gathered[16 * e : 16 * e + 16, 128 * i : 128 * i + 128] = piece.astype(BF16)
+    wait(0)
     field[...] = (dot(table[0], gathered[...]) + dot(table[1], gathered[...])).astype(BF16)
 
 
@@ -258,19 +283,31 @@
     )
 
 
+def is_packed(q):
+    return jnp.where((q == 0) & (lax.axis_index("lat") == 0), 1, 0)
+
+
 def filter_kernel(
-    wire, forward, inverse, weight1, bias1, weight2, bias2,
-    wire_back, slopes, squares,
-    scratch, columns, backs, square, w1, w2, c1, c2,
+    wire, forwards, inverses, weight1s, bias1s, weight2s, bias2s,
+    wire_back, slopes_out, squares_out,
+    forward, inverse, weight1, bias1, weight2, bias2, slopes, squares,
+    scratch, columns, backs, square, w1, w2, c1, c2, sem, sem_out,
 ):
+    wait = fetch(
+        sem, (weight1s, weight1), (bias1s, bias1), (weight2s, weight2), (bias2s, bias2),
+        (forwards, forward), (inverses, inverse),
+    )
+    spectrum_in(wire, scratch, columns)
+    wait(0, 1, 2, 3)
     build_weight(weight1, square, w1)
     build_weight(weight2, square, w2)
     build_bias(bias1, c1)
     build_bias(bias2, c2)
-    spectrum_in(wire, scratch, columns)
-    first = jnp.where(lax.axis_index("lat") == 0, 1, 0)
-
-    def column(q, which):
+    wait(4, 5)
+
+    @pl.loop(0, ROWS, unroll=UNROLL)
+    def _(q):
+        which = is_packed(q)
         field = columns[q]
         spectrum = dot(forward[which, 0], field) + dot(forward[which, 1], field)
         points = to_points(spectrum.astype(BF16))
@@ -284,26 +321,30 @@
         shrunk = from_points((post - THRESHOLD * bend).astype(BF16))
         backs[q] = dot(inverse[which, 0], shrunk) + dot(inverse[which, 1], shrunk)
 
-    column(0, first)
-
-    @pl.loop(1, ROWS)
-    def _(q):
-        column(q, 0)
-
+    keep = fetch(sem_out, (slopes, slopes_out), (squares, squares_out))
     spectrum_out(backs, scratch, wire_back)
+    keep(0, 1)
 
 
 def adjoint_kernel(
-    wire, forward, inverse, weight1, weight2, slopes, squares,
+    wire, forwards, inverses, weight1s, weight2s, slopes_in, squares_in,
     wire_back,
-    scratch, columns, backs, square, w1, w2,
+    forward, inverse, weight1, weight2, slopes, squares,
+    scratch, columns, backs, square, w1, w2, sem,
 ):
+    wait = fetch(
+        sem, (weight1s, weight1), (weight2s, weight2), (forwards, forward), (inverses, inverse),
+        (slopes_in, slopes), (squares_in, squares),
+    )
+    spectrum_in(wire, scratch, columns)
+    wait(0, 1)
     build_weight(weight1, square, w1)
     build_weight(weight2, square, w2)
-    spectrum_in(wire, scratch, columns)
-    first = jnp.where(lax.axis_index("lat") == 0, 1, 0)
-
-    def column(q, which):
+    wait(2, 3, 4, 5)
+
+    @pl.loop(0, ROWS, unroll=UNROLL)
+    def _(q):
+        which = is_packed(q)
         field = columns[q]
         spectrum = dot(forward[which, 0], field) + dot(forward[which, 1], field)
         points = (to_points(spectrum) * squares[q].astype(F32)).astype(BF16)
@@ -313,87 +354,179 @@
         shrunk = from_points(result.astype(BF16))
         backs[q] = dot(inverse[which, 0], shrunk) + dot(inverse[which, 1], shrunk)
 
-    column(0, first)
-
-    @pl.loop(1, ROWS)
-    def _(q):
-        column(q, 0)
-
     spectrum_out(backs, scratch, wire_back)
 
 
+def pieces(n):
+    return pl.ds(CHUNK * n if isinstance(n, int) else pl.multiple_of(CHUNK * n, CHUNK), CHUNK)
+
+
+def chunk_copies(sem, copy):
+    one = lambda n: pltpu.make_async_copy(*copy(pieces(n)), sem.at[n])
+    return lambda n: one(n).start(), lambda n: one(n).wait()
+
+
+def gradient_kernel(cotangents, fc2s, grad_hiddens, cotangent, fc2, grad_hidden, sem, sem_in, sem_out):
+    wait = fetch(sem, (cotangents, cotangent))
+    start_in, wait_in = chunk_copies(sem_in, lambda c: (fc2s.at[c, :], fc2.at[c, :]))
+    start_out, wait_out = chunk_copies(sem_out, lambda c: (grad_hidden.at[:, c], grad_hiddens.at[:, c]))
+    pl.loop(0, CHUNKS)(start_in)
+    wait(0)
+
+    @pl.loop(0, CHUNKS)
+    def _(n):
+        wait_in(n)
+        grad_hidden[:, pieces(n)] = dot_t(cotangent[...], fc2[pieces(n), :])
+        start_out(n)
+
+    pl.loop(0, CHUNKS)(wait_out)
+
+
 def token_kernel(
-    wire, state, lowered, cotangent, gain, shift, fc1, bias1, fc2, bias2,
-    advanced, grad_mixed, wire_next,
-    blocks, mixed, rows_in, total, grad_total,
+    wire, states, lowereds, cotangents, gains, shifts, fc1s, bias1s, grad_hiddens,
+    hiddens, mixeds, grad_mixeds, wire_next,
+    state, lowered, cotangent, gain, shift, fc1, bias1, grad_hidden, hidden, mixed, grad_mixed,
+    blocks, rows_in, grad_total, sem, sem_fc1, sem_grad, sem_hidden,
 ):
-    step = pl.program_id(0)
-
-    @pl.when(step == 0)
-    def _():
-        receive_blocks(wire, blocks)
-        for pair in range(GROUPS // 2):
-            rows = slice(48 * pair, 48 * pair + 48)
-            value = gather_blocks(blocks, pair)
-            value = value + lowered[rows, :].astype(F32) + state[rows, :].astype(F32)
-            value = value.astype(BF16)
-            mixed[rows, :] = value
-            normed, _ = norm(value.astype(F32))
-            rows_in[rows, :] = (normed * gain[...] + shift[...]).astype(BF16)
-        total[...] = jnp.zeros_like(total)
-        grad_total[...] = jnp.zeros_like(grad_total)
-
-    hidden_pre = dot(rows_in[...], fc1[...]) + bias1[...]
-    hidden, slope = gelu_pair(hidden_pre)
-    total[...] += dot(hidden.astype(BF16), fc2[...])
-    grad_hidden = dot_t(cotangent[...], fc2[...])
-    grad_pre = (grad_hidden * slope).astype(BF16)
-    grad_total[...] += dot_t(grad_pre, fc1[...])
-
-    @pl.when(step == pl.num_programs(0) - 1)
-    def _():
-        for pair in range(GROUPS // 2):
-            rows = slice(48 * pair, 48 * pair + 48)
-            value = mixed[rows, :].astype(F32)
-            normed, scale = norm(value)
-            advanced[rows, :] = (total[rows, :] + bias2[...] + value).astype(BF16)
-            grad = cotangent[rows, :].astype(F32) + norm_backward(
-                grad_total[rows, :], gain[...], normed, scale
-            )
-            grad = grad.astype(BF16)
-            grad_mixed[rows, :] = grad
-            scatter_blocks(blocks, pair, grad.astype(F32))
-        send_blocks(blocks, wire_next)
-
-
-def finish_kernel(wire, grad_mixed, state, gain, sensitivity, blocks):
+    wait = fetch(
+        sem, (states, state), (lowereds, lowered), (gains, gain), (shifts, shift), (bias1s, bias1),
+        (cotangents, cotangent),
+    )
+    start_fc1, wait_fc1 = chunk_copies(sem_fc1, lambda c: (fc1s.at[:, c], fc1.at[:, c]))
+    start_grad, wait_grad = chunk_copies(sem_grad, lambda c: (grad_hiddens.at[:, c], grad_hidden.at[:, c]))
+    start_hidden, wait_hidden = chunk_copies(sem_hidden, lambda c: (hidden.at[:, c], hiddens.at[:, c]))
+
+    @pl.loop(0, CHUNKS)
+    def _(n):
+        start_fc1(n)
+        start_grad(n)
+
     receive_blocks(wire, blocks)
+    wait(0, 1, 2, 3, 4)
+    for pair in range(GROUPS // 2):
+        rows = slice(48 * pair, 48 * pair + 48)
+        value = gather_blocks(blocks, pair)
+        value = value + lowered[rows, :].astype(F32) + state[rows, :].astype(F32)
+        value = value.astype(BF16)
+        mixed[rows, :] = value
+        normed, _ = norm(value.astype(F32))
+        rows_in[rows, :] = (normed * row(gain) + row(shift)).astype(BF16)
+    grad_total[...] = jnp.zeros_like(grad_total)
+
+    @pl.loop(0, CHUNKS, unroll=UNROLL)
+    def _(n):
+        wait_fc1(n)
+        hidden_pre = dot(rows_in[...], fc1[:, pieces(n)]) + bias1[:, pieces(n)]
+        value, slope = gelu_pair(hidden_pre)
+        hidden[:, pieces(n)] = value.astype(BF16)
+        start_hidden(n)
+        wait_grad(n)
+        grad_pre = (grad_hidden[:, pieces(n)] * slope).astype(BF16)
+        grad_total[...] += dot_t(grad_pre, fc1[:, pieces(n)])
+
+    wait(5)
+    for pair in range(GROUPS // 2):
+        rows = slice(48 * pair, 48 * pair + 48)
+        normed, scale = norm(mixed[rows, :].astype(F32))
+        grad = cotangent[rows, :].astype(F32) + norm_backward(grad_total[rows, :], row(gain), normed, scale)
+        grad = grad.astype(BF16)
+        grad_mixed[rows, :] = grad
+        scatter_blocks(blocks, pair, grad.astype(F32))
+    keep = fetch(sem, (mixed, mixeds), (grad_mixed, grad_mixeds))
+    send_blocks(blocks, wire_next)
+    pl.loop(0, CHUNKS)(wait_hidden)
+    keep(0, 1)
+
+
+def advance_kernel(
+    hiddens, fc2s, bias2s, mixeds, advanced, hidden, fc2, bias2, mixed, total, sem, sem_hidden, sem_fc2
+):
+    wait = fetch(sem, (bias2s, bias2), (mixeds, mixed))
+    start_hidden, wait_hidden = chunk_copies(sem_hidden, lambda c: (hiddens.at[:, c], hidden.at[:, c]))
+    start_fc2, wait_fc2 = chunk_copies(sem_fc2, lambda c: (fc2s.at[c, :], fc2.at[c, :]))
+
+    @pl.loop(0, CHUNKS)
+    def _(n):
+        start_hidden(n)
+        start_fc2(n)
+
+    wait(0, 1)
+    total[...] = mixed[...].astype(F32) + row(bias2)
+
+    @pl.loop(0, CHUNKS)
+    def _(n):
+        wait_hidden(n)
+        wait_fc2(n)
+        total[...] += dot(hidden[:, pieces(n)], fc2[pieces(n), :])
+
+    advanced[...] = total[...].astype(BF16)
+
+
+def finish_kernel(wire, grad_mixeds, states, gains, sensitivity, grad_mixed, state, gain, blocks, sem):
+    wait = fetch(sem, (grad_mixeds, grad_mixed), (states, state), (gains, gain))
+    receive_blocks(wire, blocks)
+    wait(0, 1, 2)
     for pair in range(GROUPS // 2):
         rows = slice(48 * pair, 48 * pair + 48)
         grad = grad_mixed[rows, :].astype(F32)
         normed, scale = norm(state[rows, :].astype(F32))
         grad_lowered = gather_blocks(blocks, pair) + grad
-        sensitivity[rows, :] = (grad + norm_backward(grad_lowered, gain[...], normed, scale)).astype(BF16)
-
-
-def array(shape, dtype=BF16):
+        sensitivity[rows, :] = (grad + norm_backward(grad_lowered, row(gain), normed, scale)).astype(BF16)
+
+
+def near(*shape, dtype=BF16):
     return jax.ShapeDtypeStruct(shape, dtype)
 
 
-LON_WIRE = array((LONS, COLS, LANES))
-LAT_WIRE = array((LATS, WIRE, 128))
-BLOCKS = pltpu.VMEM((LONS, GROUPS, COLS, 128), F32)
-PEERS = pltpu.VMEM((LATS * STRIDE + 7, 128), F32)
-COLUMNS = pltpu.VMEM((ROWS, 2 * HEIGHT, 256), BF16)
-BACKS = pltpu.VMEM((ROWS, 2 * HEIGHT, 256), F32)
-SQUARE = pltpu.VMEM((256, 256), F32)
-WEIGHT = pltpu.VMEM((2, 256, 256), BF16)
-POINTS = array((ROWS, 4 * HEIGHT, 256))
+def vmem(*shape, dtype=BF16):
+    return pltpu.VMEM(shape, dtype)
+
+
+def sems(n):
+    return pltpu.SemaphoreType.DMA((n,))
+
+
+LON_WIRE = near(LONS, COLS, LANES)
+LAT_WIRE = near(LATS, WIRE, 128)
+BLOCKS = vmem(LONS, GROUPS, COLS, 128, dtype=F32)
+PEERS = vmem(LATS * STRIDE, 128, dtype=F32)
+WIDTH_TABLE = vmem(2, WIDTH, WIDTH)
+HEIGHT_TABLES = (vmem(2, 2, 4 * HEIGHT, 2 * HEIGHT), vmem(2, 2, 2 * HEIGHT, 4 * HEIGHT))
+WEIGHT, BIAS = vmem(2, BLOCK, BLOCK, dtype=F32), vmem(2, BLOCK, dtype=F32)
+POINTS = (ROWS, 4 * HEIGHT, 256)
+SPECTRAL = (
+    PEERS,
+    vmem(ROWS, 2 * HEIGHT, 256),
+    vmem(ROWS, 2 * HEIGHT, 256, dtype=F32),
+    vmem(256, 256, dtype=F32),
+    vmem(2, 256, 256),
+    vmem(2, 256, 256),
+)
+WIDE_BIAS = vmem(1, 256, dtype=F32)
+TOKEN, UNITS = (TOKENS, FEATURES), (TOKENS, HIDDEN)
+VECTOR = vmem(FEATURES, dtype=F32)
 PARAMS = pltpu.CompilerParams(vmem_limit_bytes=48 * 1024 * 1024)
-
-
-def call(kernel, out_shape, scratch, name):
-    return pl.pallas_call(kernel, out_shape=out_shape, scratch_shapes=scratch, name=name, compiler_params=PARAMS)
+NEAR, FAR = pl.BlockSpec(), pl.BlockSpec(memory_space=pltpu.HBM)
+
+
+def far(value):
+    return pltpu.with_memory_space_constraint(value, pltpu.HBM)
+
+
+def call(kernel, out_shape, scratch, near_operands, far_operands, flops=0):
+    single = not isinstance(out_shape, tuple)
+    shapes = (out_shape,) if single else out_shape
+    specs = tuple(NEAR if isinstance(o, jax.ShapeDtypeStruct) else FAR for o in shapes)
+    return pl.pallas_call(
+        kernel,
+        out_shape=out_shape,
+        in_specs=[NEAR] * len(near_operands) + [FAR] * len(far_operands),
+        out_specs=specs[0] if single else specs,
+        scratch_shapes=scratch,
+        name=kernel.__name__,
+        compiler_params=PARAMS,
+        cost_estimate=pl.CostEstimate(flops=flops, bytes_accessed=0, transcendentals=0),
+    )(*near_operands, *map(far, far_operands))
 
 
 def exchange(value, axis):
@@ -402,15 +535,12 @@
 
 def to_lat(wire, table):
     field = exchange(wire, "lon").reshape(WIDTH, LANES)
-    wire = call(width_kernel, LAT_WIRE, [PEERS], "width")(field, table)
-    return exchange(wire, "lat")
+    return exchange(call(width_kernel, LAT_WIRE, [PEERS, WIDTH_TABLE, sems(1)], [field], [table]), "lat")
 
 
 def to_lon(wire, table):
-    wire = exchange(wire, "lat")
-    field = call(
-        width_back_kernel, array((WIDTH, LANES)), [PEERS, pltpu.VMEM((WIDTH, LANES), BF16)], "width_back"
-    )(wire, table)
+    scratch = [PEERS, vmem(WIDTH, LANES), WIDTH_TABLE, sems(1)]
+    field = call(width_back_kernel, near(WIDTH, LANES), scratch, [exchange(wire, "lat")], [table])
     return exchange(field.reshape(LON_WIRE.shape), "lon")
 
 
@@ -418,69 +548,76 @@
     state, spec_weight1, spec_bias1, spec_weight2, spec_bias2, norm1_gain, norm1_bias, norm2_gain, norm2_bias,
     fc1_weight, fc1_bias, fc2_weight, fc2_bias, cotangent,
 ):
-    width_forward, width_inverse = (jnp.asarray(split_table(t)) for t in width_tables())
-    height_forward, height_inverse = (
-        jnp.asarray(np.stack([split_table(v) for v in t])) for t in height_tables()
-    )
-    tokens = state.reshape(TOKENS, FEATURES)
-    cot = cotangent.reshape(TOKENS, FEATURES)
-    gain1, shift1 = norm1_gain.reshape(1, -1), norm1_bias.reshape(1, -1)
-    gain2, shift2 = norm2_gain.reshape(1, -1), norm2_bias.reshape(1, -1)
+    width_forward, width_inverse = map(jnp.asarray, width_tables())
+    height_forward, height_inverse = map(jnp.asarray, height_tables())
+    tokens = state.reshape(TOKEN)
+    cot = cotangent.reshape(TOKEN)
     weight1, weight2 = spec_weight1.reshape(2, BLOCK, BLOCK), spec_weight2.reshape(2, BLOCK, BLOCK)
     bias1, bias2 = spec_bias1.reshape(2, BLOCK), spec_bias2.reshape(2, BLOCK)
-
-    token_array = array((TOKENS, FEATURES))
-    lowered, wire = call(begin_kernel, (token_array, LON_WIRE), [BLOCKS], "begin")(tokens, gain1, shift1)
+    matmul = 2 * TOKENS * FEATURES * HIDDEN
+
+    lowered, wire = call(
+        begin_kernel,
+        (pltpu.HBM(TOKEN, BF16), LON_WIRE),
+        [vmem(*TOKEN), VECTOR, VECTOR, vmem(*TOKEN), BLOCKS, sems(3)],
+        [],
+        [tokens, norm1_gain, norm1_bias],
+    )
     wire = to_lat(wire, width_forward)
-    bias = pltpu.VMEM((1, 256), F32)
+    grad_hidden = call(
+        gradient_kernel,
+        pltpu.HBM(UNITS, F32),
+        [vmem(*TOKEN), vmem(HIDDEN, FEATURES), vmem(*UNITS, dtype=F32), sems(1), sems(CHUNKS), sems(CHUNKS)],
+        [],
+        [cot, fc2_weight],
+        matmul,
+    )
     wire, slopes, squares = call(
         filter_kernel,
-        (LAT_WIRE, POINTS, POINTS),
-        [PEERS, COLUMNS, BACKS, SQUARE, WEIGHT, WEIGHT, bias, bias],
-        "filter",
-    )(wire, height_forward, height_inverse, weight1, bias1, weight2, bias2)
+        (LAT_WIRE, pltpu.HBM(POINTS, BF16), pltpu.HBM(POINTS, BF16)),
+        [*HEIGHT_TABLES, WEIGHT, BIAS, WEIGHT, BIAS, vmem(*POINTS), vmem(*POINTS)]
+        + [*SPECTRAL, WIDE_BIAS, WIDE_BIAS, sems(6), sems(2)],
+        [wire],
+        [height_forward, height_inverse, weight1, bias1, weight2, bias2],
+    )
     wire = to_lon(wire, width_inverse)
 
-    whole = lambda *shape: pl.BlockSpec(shape, lambda i: (0,) * len(shape))
-    token_spec = whole(TOKENS, FEATURES)
-    wire_spec = whole(*LON_WIRE.shape)
-    advanced, grad_mixed, wire = pl.pallas_call(
+    hidden, mixed, grad_mixed, wire = call(
         token_kernel,
-        grid=(HIDDEN // CHUNK,),
-        in_specs=[
-            wire_spec,
-            token_spec,
-            token_spec,
-            token_spec,
-            whole(1, FEATURES),
-            whole(1, FEATURES),
-            pl.BlockSpec((FEATURES, CHUNK), lambda i: (0, i)),
-            pl.BlockSpec((1, CHUNK), lambda i: (0, i)),
-            pl.BlockSpec((CHUNK, FEATURES), lambda i: (i, 0)),
-            whole(1, FEATURES),
-        ],
-        out_specs=(token_spec, token_spec, wire_spec),
-        out_shape=(token_array, token_array, LON_WIRE),
-        scratch_shapes=[
-            BLOCKS,
-            pltpu.VMEM((TOKENS, FEATURES), BF16),
-            pltpu.VMEM((TOKENS, FEATURES), BF16),
-            pltpu.VMEM((TOKENS, FEATURES), F32),
-            pltpu.VMEM((TOKENS, FEATURES), F32),
-        ],
-        name="token",
-        compiler_params=PARAMS,
-    )(
-        wire, tokens, lowered, cot, gain2, shift2,
-        fc1_weight, fc1_bias.reshape(1, -1), fc2_weight, fc2_bias.reshape(1, -1),
+        (pltpu.HBM(UNITS, BF16), pltpu.HBM(TOKEN, BF16), pltpu.HBM(TOKEN, BF16), LON_WIRE),
+        [vmem(*TOKEN), vmem(*TOKEN), vmem(*TOKEN), VECTOR, VECTOR, vmem(FEATURES, HIDDEN)]
+        + [vmem(1, HIDDEN, dtype=F32), vmem(*UNITS, dtype=F32), vmem(*UNITS), vmem(*TOKEN), vmem(*TOKEN)]
+        + [BLOCKS, vmem(*TOKEN), vmem(*TOKEN, dtype=F32), sems(6), sems(CHUNKS), sems(CHUNKS), sems(CHUNKS)],
+        [wire],
+        [tokens, lowered, cot, norm2_gain, norm2_bias, fc1_weight, fc1_bias.reshape(1, -1), grad_hidden],
+        2 * matmul,
     )
 
     wire = to_lat(wire, width_forward)
-    wire = call(adjoint_kernel, LAT_WIRE, [PEERS, COLUMNS, BACKS, SQUARE, WEIGHT, WEIGHT], "adjoint")(
-        wire, height_forward, height_inverse, weight1, weight2, slopes, squares
+    advanced = call(
+        advance_kernel,
+        near(*TOKEN),
+        [vmem(*UNITS), vmem(HIDDEN, FEATURES), VECTOR, vmem(*TOKEN), vmem(*TOKEN, dtype=F32)]
+        + [sems(2), sems(CHUNKS), sems(CHUNKS)],
+        [],
+        [hidden, fc2_weight, fc2_bias, mixed],
+        matmul,
+    )
+    wire = call(
+        adjoint_kernel,
+        LAT_WIRE,
+        [*HEIGHT_TABLES, WEIGHT, WEIGHT, vmem(*POINTS), vmem(*POINTS), *SPECTRAL, sems(6)],
+        [wire],
+        [height_forward, height_inverse, weight1, weight2, slopes, squares],
     )
     wire = to_lon(wire, width_inverse)
-    sensitivity = call(finish_kernel, token_array, [BLOCKS], "finish")(wire, grad_mixed, tokens, gain1)
+    sensitivity = call(
+        finish_kernel,
+        near(*TOKEN),
+        [vmem(*TOKEN), vmem(*TOKEN), VECTOR, BLOCKS, sems(3)],
+        [wire],
+        [grad_mixed, tokens, norm1_gain],
+    )
     return advanced.reshape(state.shape), sensitivity.reshape(state.shape)
 
 

time: 186 us -> 182 us (0.978)
  Pallas kernels: 34.6 us -> 51.6 us
  blocking collectives: 126 us -> 113 us
  local copies, waits for them, and re-layouts: 10.8 us -> 0 us
  starting transfers between devices: 3.47 us -> 6.96 us
    pallas_call x9 -> x11, Pallas kernels: 34.6 us -> 51.6 us  [call(): pl.pallas_call(kernel, out_shape=out_shape, in_specs=[NEAR] * len(near_op...]
    all_to_all x7 -> x6, blocking collectives: 126 us -> 113 us  [exchange(): return lax.all_to_all(value, axis, split_axis=0, concat_axis=0, tiled=True)]
    unnamed x44 -> x0, local copies, waits for them, and re-layouts: 9.36 us -> none
    all_to_all x1 -> x2, starting transfers between devices: 3.47 us -> 6.96 us  [exchange(): return lax.all_to_all(value, axis, split_axis=0, concat_axis=0, tiled=True)]
    all_to_all x1 -> x2, waiting for transfers between devices: 9.51 us -> 9.65 us  [exchange(): return lax.all_to_all(value, axis, split_axis=0, concat_axis=0, tiled=True)]
  transfers between devices with their start and end apart: 1 -> 2, of which waited for: 1 -> 2; matrix products, arithmetic and copies ran while one was open for 0% -> 0% of each run, Pallas kernels for 0% -> 5%
where the time goes in v1:
time: 182 us
  blocking collectives  113 us (62%)
  Pallas kernels  51.6 us (28%)
  waiting for transfers between devices  9.65 us (5%)
  starting transfers between devices  6.96 us (4%)
    all_to_all x6, blocking collectives, exchange(): return lax.all_to_all(value, axis, split_axis=0, concat_axis=0, tiled=True)  113 us
    pallas_call x11, Pallas kernels, call(): pl.pallas_call(kernel, out_shape=out_shape, in_specs=[NEAR] * len(near_op...  51.6 us
    all_to_all x2, waiting for transfers between devices, exchange(): return lax.all_to_all(value, axis, split_axis=0, concat_axis=0, tiled=True)  9.65 us
    all_to_all x2, starting transfers between devices, exchange(): return lax.all_to_all(value, axis, split_axis=0, concat_axis=0, tiled=True)  6.96 us
  transfers between devices with their start and end apart: 2, of which 2 were waited for; matrix products, arithmetic and copies ran while one was open for 0% of the time, Pallas kernels for 5%

profile of v1, /device:TPU:1, one launch (start us, length us, event | category | flops | bytes accessed | tf_op | source)
XLA Modules:
  0.0 181.7 jit_solution(13034847861389538576)
XLA Ops:
  0.6 2.7 %begin_kernel.1 = (bf16[288,768]{1,0:T(8,128)(2,1)}, bf16[8,24,1152]{2,1,0:T(8,128)(2,1)S(1)}) custom-call(bf16[288,768]{1,0:T(8,128)(2,1)} %bitcast.15, f32[768]{0:T(1024)} %gains.5, f32[768]{0:T(1024)} %shifts.2), custom_call_target="tpu_custom_call" | custom-call | tf_op jit(solution)/shard_map/begin_kernel/pallas_call | solution.py:520
  3.4 16.3 %all_to_all.40 = bf16[8,24,1152]{2,1,0:T(8,128)(2,1)S(1)} all-to-all(bf16[8,24,1152]{2,1,0:T(8,128)(2,1)S(1)} %get-tuple-element.11), channel_id=1, replica_groups=mesh['lat'=16,'lon'=8,'ens'=2] {'lon'}, dimensions={0} | all-to-all | bytes 884736 | tf_op jit(solution)/shard_map/all_to_all | solution.py:533
  19.7 1.4 width_kernel.2
  21.0 26.5 %all_to_all.41.wire = bf16[16,108,128]{2,1,0:T(8,128)(2,1)S(1)} all-to-all(bf16[16,108,128]{2,1,0:T(8,128)(2,1)S(1)} %width_kernel.2), channel_id=1, replica_groups=mesh['lat'=16,'lon'=8,'ens'=2] {'lat'}, dimensions={0} | all-to-all | bytes 884736 | tf_op jit(solution)/shard_map/all_to_all | solution.py:533
  47.6 9.6 %filter_kernel.1 = (bf16[16,108,128]{2,1,0:T(8,128)(2,1)S(1)}, bf16[6,384,256]{2,1,0:T(8,128)(2,1)}, bf16[6,384,256]{2,1,0:T(8,128)(2,1)}) custom-call(bf16[16,108,128]{2,1,0:T(8,128)(2,1)S(1)} %all_to_all.41.wire, bf16[2,2,384,192]{3,2,1,0:T(8,128)(2,1)} %constant.10.clone.forwards, bf16[2,2,192,384]{3,2,1,0:T(8,128)(2,1)} %constant.11.clone.inverses, ...), custom_call_target="tpu_custom_call" | custom-call | tf_op jit(solution)/shard_map/filter_kernel/pallas_call | solution.py:520
  57.2 18.6 %all_to_all.42.wire = bf16[16,108,128]{2,1,0:T(8,128)(2,1)S(1)} all-to-all(bf16[16,108,128]{2,1,0:T(8,128)(2,1)S(1)} %get-tuple-element.12), channel_id=1, replica_groups=mesh['lat'=16,'lon'=8,'ens'=2] {'lat'}, dimensions={0} | all-to-all | bytes 884736 | tf_op jit(solution)/shard_map/all_to_all | solution.py:533
  75.7 2.1 %width_back_kernel.2 = bf16[192,1152]{1,0:T(8,128)(2,1)} custom-call(bf16[16,108,128]{2,1,0:T(8,128)(2,1)S(1)} %all_to_all.42.wire, bf16[2,192,192]{2,1,0:T(8,128)(2,1)} %constant.9.clone.tables), custom_call_target="tpu_custom_call" | custom-call | tf_op jit(solution)/shard_map/width_back_kernel/pallas_call | solution.py:520
  77.9 3.5 %all-to-all-start.3 = ((bf16[8,24,1152]{2,1,0:T(8,128)(2,1)}), bf16[8,24,1152]{2,1,0:T(8,128)(2,1)S(1)}, u32[]{:S(2)}, u32[]{:S(2)}) async-start(bf16[8,24,1152]{2,1,0:T(8,128)(2,1)} %bitcast.6), calls=%async_computation.3 | async-start | bytes 884736 | tf_op jit(solution)/shard_map/all_to_all | solution.py:533
  81.3 4.8 %gradient_kernel.1.grad_hiddens = f32[288,3072]{1,0:T(8,128)} custom-call(bf16[288,768]{1,0:T(8,128)(2,1)} %bitcast.19, bf16[3072,768]{1,0:T(8,128)(2,1)} %fc2s.3), custom_call_target="tpu_custom_call" | custom-call | flops 1358954496 | tf_op jit(solution)/shard_map/gradient_kernel/pallas_call | solution.py:520
  86.1 4.8 %all-to-all-done.3.wire = bf16[8,24,1152]{2,1,0:T(8,128)(2,1)S(1)} async-done(((bf16[8,24,1152]{2,1,0:T(8,128)(2,1)}), bf16[8,24,1152]{2,1,0:T(8,128)(2,1)S(1)}, u32[]{:S(2)}, u32[]{:S(2)}) %all-to-all-start.3) | async-done | bytes 442400 | tf_op jit(solution)/shard_map/all_to_all | solution.py:533
  90.9 10.7 %token_kernel.1 = (bf16[288,3072]{1,0:T(8,128)(2,1)}, bf16[288,768]{1,0:T(8,128)(2,1)}, bf16[288,768]{1,0:T(8,128)(2,1)}, bf16[8,24,1152]{2,1,0:T(8,128)(2,1)S(1)}) custom-call(bf16[8,24,1152]{2,1,0:T(8,128)(2,1)S(1)} %all-to-all-done.3.wire, bf16[288,768]{1,0:T(8,128)(2,1)} %bitcast.16, bf16[288,768]{1,0:T(8,128)(2,1)} %get-tuple-element.13.lowereds, ...), custom_call_target="tpu_custom_call" | custom-call | flops 2717908992 | tf_op jit(solution)/shard_map/token_kernel/pallas_call | solution.py:520
  101.7 12.7 %all_to_all.43 = bf16[8,24,1152]{2,1,0:T(8,128)(2,1)S(1)} all-to-all(bf16[8,24,1152]{2,1,0:T(8,128)(2,1)S(1)} %get-tuple-element.16), channel_id=1, replica_groups=mesh['lat'=16,'lon'=8,'ens'=2] {'lon'}, dimensions={0} | all-to-all | bytes 884736 | tf_op jit(solution)/shard_map/all_to_all | solution.py:533
  114.4 1.4 width_kernel.3
  115.7 20.2 %all_to_all.44.wire = bf16[16,108,128]{2,1,0:T(8,128)(2,1)S(1)} all-to-all(bf16[16,108,128]{2,1,0:T(8,128)(2,1)S(1)} %width_kernel.3), channel_id=1, replica_groups=mesh['lat'=16,'lon'=8,'ens'=2] {'lat'}, dimensions={0} | all-to-all | bytes 884736 | tf_op jit(solution)/shard_map/all_to_all | solution.py:533
  135.9 8.8 %adjoint_kernel.1 = bf16[16,108,128]{2,1,0:T(8,128)(2,1)S(1)} custom-call(bf16[16,108,128]{2,1,0:T(8,128)(2,1)S(1)} %all_to_all.44.wire, bf16[2,2,384,192]{3,2,1,0:T(8,128)(2,1)} %constant.10.clone.forwards, bf16[2,2,192,384]{3,2,1,0:T(8,128)(2,1)} %constant.11.clone.inverses, f32[2,96,96]{2,1,0:T(8,128)} %bitcast.23, f32[2,96,96]{2,1,0:T(8,128)} %bitcast.25, ...), custom_call_target="tpu_custom_call" | custom-call | tf_op jit(solution)/shard_map/adjoint_kernel/pallas_call | solution.py:520
  144.7 18.5 %all_to_all.45.wire = bf16[16,108,128]{2,1,0:T(8,128)(2,1)S(1)} all-to-all(bf16[16,108,128]{2,1,0:T(8,128)(2,1)S(1)} %adjoint_kernel.1), channel_id=1, replica_groups=mesh['lat'=16,'lon'=8,'ens'=2] {'lat'}, dimensions={0} | all-to-all | bytes 884736 | tf_op jit(solution)/shard_map/all_to_all | solution.py:533
  163.2 2.1 %width_back_kernel.3 = bf16[192,1152]{1,0:T(8,128)(2,1)} custom-call(bf16[16,108,128]{2,1,0:T(8,128)(2,1)S(1)} %all_to_all.45.wire, bf16[2,192,192]{2,1,0:T(8,128)(2,1)} %constant.9.clone.tables), custom_call_target="tpu_custom_call" | custom-call | tf_op jit(solution)/shard_map/width_back_kernel/pallas_call | solution.py:520
  165.3 3.5 %all-to-all-start.7 = ((bf16[8,24,1152]{2,1,0:T(8,128)(2,1)}), bf16[8,24,1152]{2,1,0:T(8,128)(2,1)S(1)}, u32[]{:S(2)}, u32[]{:S(2)}) async-start(bf16[8,24,1152]{2,1,0:T(8,128)(2,1)} %bitcast.11), calls=%async_computation.7 | async-start | bytes 884736 | tf_op jit(solution)/shard_map/all_to_all | solution.py:533
  168.8 4.7 %advance_kernel.1 = bf16[288,768]{1,0:T(8,128)(2,1)} custom-call(bf16[288,3072]{1,0:T(8,128)(2,1)} %get-tuple-element.14.hiddens, bf16[3072,768]{1,0:T(8,128)(2,1)} %fc2s.3, f32[768]{0:T(1024)} %bias2s.1, bf16[288,768]{1,0:T(8,128)(2,1)} %get-tuple-element.15.mixeds), custom_call_target="tpu_custom_call" | custom-call | flops 1358954496 | tf_op jit(solution)/shard_map/advance_kernel/pallas_call | solution.py:520
  173.6 4.9 %all-to-all-done.7.wire = bf16[8,24,1152]{2,1,0:T(8,128)(2,1)S(1)} async-done(((bf16[8,24,1152]{2,1,0:T(8,128)(2,1)}), bf16[8,24,1152]{2,1,0:T(8,128)(2,1)S(1)}, u32[]{:S(2)}, u32[]{:S(2)}) %all-to-all-start.7) | async-done | bytes 442400 | tf_op jit(solution)/shard_map/all_to_all | solution.py:533
  178.4 3.3 %finish_kernel.1 = bf16[288,768]{1,0:T(8,128)(2,1)} custom-call(bf16[8,24,1152]{2,1,0:T(8,128)(2,1)S(1)} %all-to-all-done.7.wire, bf16[288,768]{1,0:T(8,128)(2,1)} %get-tuple-element.19.grad_mixeds, bf16[288,768]{1,0:T(8,128)(2,1)} %bitcast.17, f32[768]{0:T(1024)} %gains.5), custom_call_target="tpu_custom_call" | custom-call | tf_op jit(solution)/shard_map/finish_kernel/pallas_call | solution.py:520
Async XLA Ops:
  77.9 13.1 %all-to-all-start.3 = ((bf16[8,24,1152]{2,1,0:T(8,128)(2,1)}), bf16[8,24,1152]{2,1,0:T(8,128)(2,1)S(1)}, u32[]{:S(2)}, u32[]{:S(2)}) async-start(bf16[8,24,1152]{2,1,0:T(8,128)(2,1)} %bitcast.6), calls=%async_computation.3 | async-start | bytes 884736 | tf_op jit(solution)/shard_map/all_to_all | solution.py:533
  165.3 13.1 %all-to-all-start.7 = ((bf16[8,24,1152]{2,1,0:T(8,128)(2,1)}), bf16[8,24,1152]{2,1,0:T(8,128)(2,1)S(1)}, u32[]{:S(2)}, u32[]{:S(2)}) async-start(bf16[8,24,1152]{2,1,0:T(8,128)(2,1)} %bitcast.11), calls=%async_computation.7 | async-start | bytes 884736 | tf_op jit(solution)/shard_map/all_to_all | solution.py:533

commit v2 on v1

--- a/solution.py
+++ b/solution.py
@@ -66,7 +66,7 @@
     h = 0.5
     plain_back = join_back([[h * c, h * c, -h * n, h * n], [h * n, h * n, h * c, -h * c]])
     packed_back = join_back([[c, zero, -n, zero], [zero, c, zero, -n]])
-    return tuple(np.stack([split_table(t) for t in pair]) for pair in ((plain, packed), (plain_back, packed_back)))
+    return np.stack([plain, packed]).astype(BF16), np.stack([plain_back, packed_back]).astype(BF16)
 
 
 def dot(a, b):
@@ -166,19 +166,28 @@
     return wait
 
 
-def begin_kernel(states, gains, shifts, lowereds, wire, state, gain, shift, lowered, blocks, sem):
-    wait = fetch(sem, (states, state), (gains, gain), (shifts, shift))
-    wait(0, 1, 2)
-    gain, shift = row(gain), row(shift)
+def pair_rows(pair):
+    return slice(48 * pair, 48 * pair + 48)
+
+
+def begin_kernel(
+    states, gains, shifts, *rest
+):
+    sources, (lowered, wire), targets = rest[:KEPT], rest[KEPT : KEPT + 2], rest[KEPT + 2 : 2 * KEPT + 2]
+    state, gain, shift, blocks, sem, sem_kept = rest[2 * KEPT + 2 :]
+    vectors = [(gains, gain), (shifts, shift)]
+    wait = fetch(sem, *((states.at[pair_rows(n), :], state.at[pair_rows(n), :]) for n in range(GROUPS // 2)), *vectors)
+    wait_kept = fetch(sem_kept, *zip(sources, targets))
+    wait(6, 7)
     for pair in range(GROUPS // 2):
-        rows = slice(48 * pair, 48 * pair + 48)
+        rows = pair_rows(pair)
+        wait(pair)
         normed, _ = norm(state[rows, :].astype(F32))
-        value = (normed * gain + shift).astype(BF16)
+        value = (normed * row(gain) + row(shift)).astype(BF16)
         lowered[rows, :] = value
         scatter_blocks(blocks, pair, value.astype(F32))
-    keep = fetch(sem, (lowered, lowereds))
     send_blocks(blocks, wire)
-    keep(0)
+    wait_kept(*range(KEPT))
 
 
 def wire_out(scratch, wire):
@@ -195,8 +204,7 @@
     return pl.ds(row, LATS, stride=STRIDE)
 
 
-def width_kernel(field, tables, wire, scratch, table, sem):
-    fetch(sem, (tables, table))(0)
+def width_kernel(field, table, wire, scratch):
     product = dot(table[0], field[...]) + dot(table[1], field[...])
     for e in range(GROUPS):
         for i in range(TILES):
@@ -204,14 +212,12 @@
     wire_out(scratch, wire)
 
 
-def width_back_kernel(wire, tables, field, scratch, gathered, table, sem):
-    wait = fetch(sem, (tables, table))
+def width_back_kernel(wire, table, field, scratch, gathered):
     wire_in(wire, scratch)
     for e in range(GROUPS):
         for i in range(TILES):
             piece = scratch[peers(GROUPS * i + e), :]
             gathered[16 * e : 16 * e + 16, 128 * i : 128 * i + 128] = piece.astype(BF16)
-    wait(0)
     field[...] = (dot(table[0], gathered[...]) + dot(table[1], gathered[...])).astype(BF16)
 
 
@@ -249,10 +255,7 @@
     square[0:BLOCK, 128 : 128 + BLOCK] = weight[1]
     square[128 : 128 + BLOCK, 0:BLOCK] = -weight[1]
     square[128 : 128 + BLOCK, 128 : 128 + BLOCK] = weight[0]
-    full = square[...]
-    high = full.astype(BF16)
-    out[0] = high
-    out[1] = (full - high.astype(F32)).astype(BF16)
+    out[...] = square[...].astype(BF16)
 
 
 def build_bias(bias, out):
@@ -288,71 +291,50 @@
 
 
 def filter_kernel(
-    wire, forwards, inverses, weight1s, bias1s, weight2s, bias2s,
+    wire, forward, inverse, weight1, bias1, weight2, bias2,
     wire_back, slopes_out, squares_out,
-    forward, inverse, weight1, bias1, weight2, bias2, slopes, squares,
-    scratch, columns, backs, square, w1, w2, c1, c2, sem, sem_out,
+    slopes, squares, scratch, columns, backs, square, w1, w2, c1, c2, sem,
 ):
-    wait = fetch(
-        sem, (weight1s, weight1), (bias1s, bias1), (weight2s, weight2), (bias2s, bias2),
-        (forwards, forward), (inverses, inverse),
-    )
-    spectrum_in(wire, scratch, columns)
-    wait(0, 1, 2, 3)
     build_weight(weight1, square, w1)
     build_weight(weight2, square, w2)
     build_bias(bias1, c1)
     build_bias(bias2, c2)
-    wait(4, 5)
+    spectrum_in(wire, scratch, columns)
 
     @pl.loop(0, ROWS, unroll=UNROLL)
     def _(q):
         which = is_packed(q)
-        field = columns[q]
-        spectrum = dot(forward[which, 0], field) + dot(forward[which, 1], field)
-        points = to_points(spectrum.astype(BF16))
-        pre = dot(points, w1[0]) + dot(points, w1[1]) + c1[...]
-        active, slope = gelu_pair(pre)
+        points = to_points(dot(forward[which], columns[q]).astype(BF16))
+        active, slope = gelu_pair(dot(points, w1[...]) + c1[...])
         slopes[q] = slope.astype(BF16)
-        active = active.astype(BF16)
-        post = dot(active, w2[0]) + dot(active, w2[1]) + c2[...]
+        post = dot(active.astype(BF16), w2[...]) + c2[...]
         bend = jnp.tanh(post * (1.0 / THRESHOLD))
         squares[q] = (bend * bend).astype(BF16)
         shrunk = from_points((post - THRESHOLD * bend).astype(BF16))
-        backs[q] = dot(inverse[which, 0], shrunk) + dot(inverse[which, 1], shrunk)
-
-    keep = fetch(sem_out, (slopes, slopes_out), (squares, squares_out))
+        backs[q] = dot(inverse[which], shrunk)
+
+    keep = fetch(sem, (slopes, slopes_out), (squares, squares_out))
     spectrum_out(backs, scratch, wire_back)
     keep(0, 1)
 
 
 def adjoint_kernel(
-    wire, forwards, inverses, weight1s, weight2s, slopes_in, squares_in,
+    wire, forward, inverse, weight1, weight2, slopes, squares,
     wire_back,
-    forward, inverse, weight1, weight2, slopes, squares,
-    scratch, columns, backs, square, w1, w2, sem,
+    scratch, columns, backs, square, w1, w2,
 ):
-    wait = fetch(
-        sem, (weight1s, weight1), (weight2s, weight2), (forwards, forward), (inverses, inverse),
-        (slopes_in, slopes), (squares_in, squares),
-    )
-    spectrum_in(wire, scratch, columns)
-    wait(0, 1)
     build_weight(weight1, square, w1)
     build_weight(weight2, square, w2)
-    wait(2, 3, 4, 5)
+    spectrum_in(wire, scratch, columns)
 
     @pl.loop(0, ROWS, unroll=UNROLL)
     def _(q):
         which = is_packed(q)
-        field = columns[q]
-        spectrum = dot(forward[which, 0], field) + dot(forward[which, 1], field)
+        spectrum = dot(forward[which], columns[q])
         points = (to_points(spectrum) * squares[q].astype(F32)).astype(BF16)
-        active = dot_t(points, w2[0]) + dot_t(points, w2[1])
-        pre = (active * slopes[q].astype(F32)).astype(BF16)
-        result = dot_t(pre, w1[0]) + dot_t(pre, w1[1])
-        shrunk = from_points(result.astype(BF16))
-        backs[q] = dot(inverse[which, 0], shrunk) + dot(inverse[which, 1], shrunk)
+        pre = (dot_t(points, w2[...]) * slopes[q].astype(F32)).astype(BF16)
+        shrunk = from_points(dot_t(pre, w1[...]).astype(BF16))
+        backs[q] = dot(inverse[which], shrunk)
 
     spectrum_out(backs, scratch, wire_back)
 
@@ -366,8 +348,12 @@
     return lambda n: one(n).start(), lambda n: one(n).wait()
 
 
-def gradient_kernel(cotangents, fc2s, grad_hiddens, cotangent, fc2, grad_hidden, sem, sem_in, sem_out):
-    wait = fetch(sem, (cotangents, cotangent))
+def gradient_kernel(
+    states, lowereds, cotangents, fc2s,
+    grad_hiddens, base, cotangent,
+    state, lowered, fc2, grad_hidden, sem, sem_in, sem_out,
+):
+    wait = fetch(sem, (cotangents, cotangent), (states, state), (lowereds, lowered))
     start_in, wait_in = chunk_copies(sem_in, lambda c: (fc2s.at[c, :], fc2.at[c, :]))
     start_out, wait_out = chunk_copies(sem_out, lambda c: (grad_hidden.at[:, c], grad_hiddens.at[:, c]))
     pl.loop(0, CHUNKS)(start_in)
@@ -379,19 +365,18 @@
         grad_hidden[:, pieces(n)] = dot_t(cotangent[...], fc2[pieces(n), :])
         start_out(n)
 
+    wait(1, 2)
+    base[...] = lowered[...].astype(F32) + state[...].astype(F32)
     pl.loop(0, CHUNKS)(wait_out)
 
 
 def token_kernel(
-    wire, states, lowereds, cotangents, gains, shifts, fc1s, bias1s, grad_hiddens,
+    wire, base, cotangent, gains, shifts, fc1s, bias1s, grad_hiddens,
     hiddens, mixeds, grad_mixeds, wire_next,
-    state, lowered, cotangent, gain, shift, fc1, bias1, grad_hidden, hidden, mixed, grad_mixed,
+    gain, shift, fc1, bias1, grad_hidden, hidden, mixed, grad_mixed,
     blocks, rows_in, grad_total, sem, sem_fc1, sem_grad, sem_hidden,
 ):
-    wait = fetch(
-        sem, (states, state), (lowereds, lowered), (gains, gain), (shifts, shift), (bias1s, bias1),
-        (cotangents, cotangent),
-    )
+    wait = fetch(sem, (gains, gain), (shifts, shift), (bias1s, bias1))
     start_fc1, wait_fc1 = chunk_copies(sem_fc1, lambda c: (fc1s.at[:, c], fc1.at[:, c]))
     start_grad, wait_grad = chunk_copies(sem_grad, lambda c: (grad_hiddens.at[:, c], grad_hidden.at[:, c]))
     start_hidden, wait_hidden = chunk_copies(sem_hidden, lambda c: (hidden.at[:, c], hiddens.at[:, c]))
@@ -402,12 +387,10 @@
         start_grad(n)
 
     receive_blocks(wire, blocks)
-    wait(0, 1, 2, 3, 4)
+    wait(0, 1, 2)
     for pair in range(GROUPS // 2):
-        rows = slice(48 * pair, 48 * pair + 48)
-        value = gather_blocks(blocks, pair)
-        value = value + lowered[rows, :].astype(F32) + state[rows, :].astype(F32)
-        value = value.astype(BF16)
+        rows = pair_rows(pair)
+        value = (gather_blocks(blocks, pair) + base[rows, :]).astype(BF16)
         mixed[rows, :] = value
         normed, _ = norm(value.astype(F32))
         rows_in[rows, :] = (normed * row(gain) + row(shift)).astype(BF16)
@@ -424,9 +407,8 @@
         grad_pre = (grad_hidden[:, pieces(n)] * slope).astype(BF16)
         grad_total[...] += dot_t(grad_pre, fc1[:, pieces(n)])
 
-    wait(5)
     for pair in range(GROUPS // 2):
-        rows = slice(48 * pair, 48 * pair + 48)
+        rows = pair_rows(pair)
         normed, scale = norm(mixed[rows, :].astype(F32))
         grad = cotangent[rows, :].astype(F32) + norm_backward(grad_total[rows, :], row(gain), normed, scale)
         grad = grad.astype(BF16)
@@ -439,9 +421,11 @@
 
 
 def advance_kernel(
-    hiddens, fc2s, bias2s, mixeds, advanced, hidden, fc2, bias2, mixed, total, sem, sem_hidden, sem_fc2
+    hiddens, fc2s, bias2s, mixeds, grad_mixeds, states,
+    advanced, normed, scale, grad_mixed,
+    hidden, fc2, bias2, mixed, state, total, sem, sem_hidden, sem_fc2,
 ):
-    wait = fetch(sem, (bias2s, bias2), (mixeds, mixed))
+    wait = fetch(sem, (bias2s, bias2), (mixeds, mixed), (grad_mixeds, grad_mixed), (states, state))
     start_hidden, wait_hidden = chunk_copies(sem_hidden, lambda c: (hiddens.at[:, c], hidden.at[:, c]))
     start_fc2, wait_fc2 = chunk_copies(sem_fc2, lambda c: (fc2s.at[c, :], fc2.at[c, :]))
 
@@ -450,7 +434,10 @@
         start_hidden(n)
         start_fc2(n)
 
-    wait(0, 1)
+    wait(0, 1, 2, 3)
+    for pair in range(GROUPS // 2):
+        rows = pair_rows(pair)
+        normed[rows, :], scale[rows, :] = norm(state[rows, :].astype(F32))
     total[...] = mixed[...].astype(F32) + row(bias2)
 
     @pl.loop(0, CHUNKS)
@@ -462,16 +449,21 @@
     advanced[...] = total[...].astype(BF16)
 
 
-def finish_kernel(wire, grad_mixeds, states, gains, sensitivity, grad_mixed, state, gain, blocks, sem):
-    wait = fetch(sem, (grad_mixeds, grad_mixed), (states, state), (gains, gain))
+def finish_kernel(wire, normed, scale, grad_mixed, gains, sensitivity, gain, blocks, out, sem, sem_out):
+    wait = fetch(sem, (gains, gain))
     receive_blocks(wire, blocks)
-    wait(0, 1, 2)
+    wait(0)
+    copies = []
     for pair in range(GROUPS // 2):
-        rows = slice(48 * pair, 48 * pair + 48)
+        rows = pair_rows(pair)
         grad = grad_mixed[rows, :].astype(F32)
-        normed, scale = norm(state[rows, :].astype(F32))
         grad_lowered = gather_blocks(blocks, pair) + grad
-        sensitivity[rows, :] = (grad + norm_backward(grad_lowered, row(gain), normed, scale)).astype(BF16)
+        grad = grad + norm_backward(grad_lowered, row(gain), normed[rows, :], scale[rows, :])
+        out[rows, :] = grad.astype(BF16)
+        copies.append(pltpu.make_async_copy(out.at[rows, :], sensitivity.at[rows, :], sem_out.at[pair]))
+        copies[-1].start()
+    for c in copies:
+        c.wait()
 
 
 def near(*shape, dtype=BF16):
@@ -490,43 +482,41 @@
 LAT_WIRE = near(LATS, WIRE, 128)
 BLOCKS = vmem(LONS, GROUPS, COLS, 128, dtype=F32)
 PEERS = vmem(LATS * STRIDE, 128, dtype=F32)
-WIDTH_TABLE = vmem(2, WIDTH, WIDTH)
-HEIGHT_TABLES = (vmem(2, 2, 4 * HEIGHT, 2 * HEIGHT), vmem(2, 2, 2 * HEIGHT, 4 * HEIGHT))
-WEIGHT, BIAS = vmem(2, BLOCK, BLOCK, dtype=F32), vmem(2, BLOCK, dtype=F32)
 POINTS = (ROWS, 4 * HEIGHT, 256)
 SPECTRAL = (
     PEERS,
     vmem(ROWS, 2 * HEIGHT, 256),
     vmem(ROWS, 2 * HEIGHT, 256, dtype=F32),
     vmem(256, 256, dtype=F32),
-    vmem(2, 256, 256),
-    vmem(2, 256, 256),
+    vmem(256, 256),
+    vmem(256, 256),
 )
 WIDE_BIAS = vmem(1, 256, dtype=F32)
 TOKEN, UNITS = (TOKENS, FEATURES), (TOKENS, HIDDEN)
 VECTOR = vmem(FEATURES, dtype=F32)
 PARAMS = pltpu.CompilerParams(vmem_limit_bytes=48 * 1024 * 1024)
-NEAR, FAR = pl.BlockSpec(), pl.BlockSpec(memory_space=pltpu.HBM)
-
-
-def far(value):
-    return pltpu.with_memory_space_constraint(value, pltpu.HBM)
-
-
-def call(kernel, out_shape, scratch, near_operands, far_operands, flops=0):
+KEPT = 8
+
+
+def place(space):
+    return pl.BlockSpec() if space is None else pl.BlockSpec(memory_space=space)
+
+
+def call(kernel, out_shape, scratch, operands, places, flops=0):
     single = not isinstance(out_shape, tuple)
     shapes = (out_shape,) if single else out_shape
-    specs = tuple(NEAR if isinstance(o, jax.ShapeDtypeStruct) else FAR for o in shapes)
+    specs = tuple(place(None if isinstance(o, jax.ShapeDtypeStruct) else o.memory_space) for o in shapes)
+    spaces = [{"f": pltpu.HBM, "h": pltpu.VMEM, "n": None}[p] for p in places]
     return pl.pallas_call(
         kernel,
         out_shape=out_shape,
-        in_specs=[NEAR] * len(near_operands) + [FAR] * len(far_operands),
+        in_specs=[place(m) for m in spaces],
         out_specs=specs[0] if single else specs,
         scratch_shapes=scratch,
         name=kernel.__name__,
         compiler_params=PARAMS,
         cost_estimate=pl.CostEstimate(flops=flops, bytes_accessed=0, transcendentals=0),
-    )(*near_operands, *map(far, far_operands))
+    )(*(v if m is None else pltpu.with_memory_space_constraint(v, m) for v, m in zip(operands, spaces, strict=True)))
 
 
 def exchange(value, axis):
@@ -535,12 +525,12 @@
 
 def to_lat(wire, table):
     field = exchange(wire, "lon").reshape(WIDTH, LANES)
-    return exchange(call(width_kernel, LAT_WIRE, [PEERS, WIDTH_TABLE, sems(1)], [field], [table]), "lat")
+    return exchange(call(width_kernel, LAT_WIRE, [PEERS], [field, table], "nh"), "lat")
 
 
 def to_lon(wire, table):
-    scratch = [PEERS, vmem(WIDTH, LANES), WIDTH_TABLE, sems(1)]
-    field = call(width_back_kernel, near(WIDTH, LANES), scratch, [exchange(wire, "lat")], [table])
+    scratch = [PEERS, vmem(WIDTH, LANES)]
+    field = call(width_back_kernel, near(WIDTH, LANES), scratch, [exchange(wire, "lat"), table], "nh")
     return exchange(field.reshape(LON_WIRE.shape), "lon")
 
 
@@ -548,75 +538,79 @@
     state, spec_weight1, spec_bias1, spec_weight2, spec_bias2, norm1_gain, norm1_bias, norm2_gain, norm2_bias,
     fc1_weight, fc1_bias, fc2_weight, fc2_bias, cotangent,
 ):
-    width_forward, width_inverse = map(jnp.asarray, width_tables())
-    height_forward, height_inverse = map(jnp.asarray, height_tables())
     tokens = state.reshape(TOKEN)
     cot = cotangent.reshape(TOKEN)
-    weight1, weight2 = spec_weight1.reshape(2, BLOCK, BLOCK), spec_weight2.reshape(2, BLOCK, BLOCK)
-    bias1, bias2 = spec_bias1.reshape(2, BLOCK), spec_bias2.reshape(2, BLOCK)
     matmul = 2 * TOKENS * FEATURES * HIDDEN
-
-    lowered, wire = call(
+    kept = [
+        *map(jnp.asarray, (*width_tables(), *height_tables())),
+        spec_weight1.reshape(2, BLOCK, BLOCK),
+        spec_bias1.reshape(2, BLOCK),
+        spec_weight2.reshape(2, BLOCK, BLOCK),
+        spec_bias2.reshape(2, BLOCK),
+    ]
+
+    lowered, wire, *kept = call(
         begin_kernel,
-        (pltpu.HBM(TOKEN, BF16), LON_WIRE),
-        [vmem(*TOKEN), VECTOR, VECTOR, vmem(*TOKEN), BLOCKS, sems(3)],
-        [],
-        [tokens, norm1_gain, norm1_bias],
-    )
+        (near(*TOKEN), LON_WIRE, *(vmem(*k.shape, dtype=k.dtype) for k in kept)),
+        [vmem(*TOKEN), VECTOR, VECTOR, BLOCKS, sems(8), sems(KEPT)],
+        [tokens, norm1_gain, norm1_bias, *kept],
+        "fff" + "f" * KEPT,
+    )
+    width_forward, width_inverse, height_forward, height_inverse, weight1, bias1, weight2, bias2 = kept
     wire = to_lat(wire, width_forward)
-    grad_hidden = call(
-        gradient_kernel,
-        pltpu.HBM(UNITS, F32),
-        [vmem(*TOKEN), vmem(HIDDEN, FEATURES), vmem(*UNITS, dtype=F32), sems(1), sems(CHUNKS), sems(CHUNKS)],
-        [],
-        [cot, fc2_weight],
-        matmul,
-    )
     wire, slopes, squares = call(
         filter_kernel,
         (LAT_WIRE, pltpu.HBM(POINTS, BF16), pltpu.HBM(POINTS, BF16)),
-        [*HEIGHT_TABLES, WEIGHT, BIAS, WEIGHT, BIAS, vmem(*POINTS), vmem(*POINTS)]
-        + [*SPECTRAL, WIDE_BIAS, WIDE_BIAS, sems(6), sems(2)],
-        [wire],
-        [height_forward, height_inverse, weight1, bias1, weight2, bias2],
+        [vmem(*POINTS), vmem(*POINTS), *SPECTRAL, WIDE_BIAS, WIDE_BIAS, sems(2)],
+        [wire, height_forward, height_inverse, weight1, bias1, weight2, bias2],
+        "nhhhhhh",
+    )
+    grad_hidden, base, cot = call(
+        gradient_kernel,
+        (pltpu.HBM(UNITS, F32), vmem(*TOKEN, dtype=F32), vmem(*TOKEN)),
+        [vmem(*TOKEN), vmem(*TOKEN), vmem(HIDDEN, FEATURES), vmem(*UNITS, dtype=F32)]
+        + [sems(3), sems(CHUNKS), sems(CHUNKS)],
+        [tokens, lowered, cot, fc2_weight],
+        "fnff",
+        matmul,
     )
     wire = to_lon(wire, width_inverse)
 
     hidden, mixed, grad_mixed, wire = call(
         token_kernel,
         (pltpu.HBM(UNITS, BF16), pltpu.HBM(TOKEN, BF16), pltpu.HBM(TOKEN, BF16), LON_WIRE),
-        [vmem(*TOKEN), vmem(*TOKEN), vmem(*TOKEN), VECTOR, VECTOR, vmem(FEATURES, HIDDEN)]
-        + [vmem(1, HIDDEN, dtype=F32), vmem(*UNITS, dtype=F32), vmem(*UNITS), vmem(*TOKEN), vmem(*TOKEN)]
-        + [BLOCKS, vmem(*TOKEN), vmem(*TOKEN, dtype=F32), sems(6), sems(CHUNKS), sems(CHUNKS), sems(CHUNKS)],
-        [wire],
-        [tokens, lowered, cot, norm2_gain, norm2_bias, fc1_weight, fc1_bias.reshape(1, -1), grad_hidden],
+        [VECTOR, VECTOR, vmem(FEATURES, HIDDEN), vmem(1, HIDDEN, dtype=F32), vmem(*UNITS, dtype=F32)]
+        + [vmem(*UNITS), vmem(*TOKEN), vmem(*TOKEN), BLOCKS, vmem(*TOKEN), vmem(*TOKEN, dtype=F32)]
+        + [sems(3), sems(CHUNKS), sems(CHUNKS), sems(CHUNKS)],
+        [wire, base, cot, norm2_gain, norm2_bias, fc1_weight, fc1_bias.reshape(1, -1), grad_hidden],
+        "nhhfffff",
         2 * matmul,
     )
 
     wire = to_lat(wire, width_forward)
-    advanced = call(
-        advance_kernel,
-        near(*TOKEN),
-        [vmem(*UNITS), vmem(HIDDEN, FEATURES), VECTOR, vmem(*TOKEN), vmem(*TOKEN, dtype=F32)]
-        + [sems(2), sems(CHUNKS), sems(CHUNKS)],
-        [],
-        [hidden, fc2_weight, fc2_bias, mixed],
-        matmul,
-    )
     wire = call(
         adjoint_kernel,
         LAT_WIRE,
-        [*HEIGHT_TABLES, WEIGHT, WEIGHT, vmem(*POINTS), vmem(*POINTS), *SPECTRAL, sems(6)],
-        [wire],
-        [height_forward, height_inverse, weight1, weight2, slopes, squares],
+        [*SPECTRAL],
+        [wire, height_forward, height_inverse, weight1, weight2, slopes, squares],
+        "nhhhhnn",
+    )
+    advanced, normed, scale, grad_mixed = call(
+        advance_kernel,
+        (near(*TOKEN), vmem(*TOKEN, dtype=F32), vmem(TOKENS, 1, dtype=F32), vmem(*TOKEN)),
+        [vmem(*UNITS), vmem(HIDDEN, FEATURES), VECTOR, vmem(*TOKEN), vmem(*TOKEN), vmem(*TOKEN, dtype=F32)]
+        + [sems(4), sems(CHUNKS), sems(CHUNKS)],
+        [hidden, fc2_weight, fc2_bias, mixed, grad_mixed, tokens],
+        "ffffff",
+        matmul,
     )
     wire = to_lon(wire, width_inverse)
     sensitivity = call(
         finish_kernel,
-        near(*TOKEN),
-        [vmem(*TOKEN), vmem(*TOKEN), VECTOR, BLOCKS, sems(3)],
-        [wire],
-        [grad_mixed, tokens, norm1_gain],
+        pltpu.HBM(TOKEN, BF16),
+        [VECTOR, BLOCKS, vmem(*TOKEN), sems(1), sems(GROUPS // 2)],
+        [wire, normed, scale, grad_mixed, norm1_gain],
+        "nhhhf",
     )
     return advanced.reshape(state.shape), sensitivity.reshape(state.shape)
 

time: 182 us -> 171 us (0.940)
  Pallas kernels: 51.6 us -> 40.5 us
    pallas_call x11, Pallas kernels: 51.6 us -> 40.5 us  [call(): pl.pallas_call(kernel, out_shape=out_shape, in_specs=[place(m) for m in s...]
  transfers between devices with their start and end apart: 2 -> 2, of which waited for: 2 -> 2; matrix products, arithmetic and copies ran while one was open for 0% -> 0% of each run, Pallas kernels for 5% -> 6%
where the time goes in v2:
time: 171 us; the launch traced here: 170 us
  blocking collectives  113 us (66%)
  Pallas kernels  40.5 us (24%)
  waiting for transfers between devices  9.1 us (5%)
  starting transfers between devices  6.94 us (4%)
    all_to_all x6, blocking collectives, exchange(): return lax.all_to_all(value, axis, split_axis=0, concat_axis=0, tiled=True)  113 us
    pallas_call x11, Pallas kernels, call(): pl.pallas_call(kernel, out_shape=out_shape, in_specs=[place(m) for m in s...  40.5 us
    all_to_all x2, waiting for transfers between devices, exchange(): return lax.all_to_all(value, axis, split_axis=0, concat_axis=0, tiled=True)  9.1 us
    all_to_all x2, starting transfers between devices, exchange(): return lax.all_to_all(value, axis, split_axis=0, concat_axis=0, tiled=True)  6.94 us
  transfers between devices with their start and end apart: 2, of which 2 were waited for; matrix products, arithmetic and copies ran while one was open for 0% of the time, Pallas kernels for 6%

profile of v2, /device:TPU:1, one launch (start us, length us, event | category | flops | bytes accessed | tf_op | source)
XLA Modules:
  0.0 170.2 jit_solution(11050865282708174535)
XLA Ops:
  0.6 3.3 %begin_kernel.1 = (bf16[288,768]{1,0:T(8,128)(2,1)S(1)}, bf16[8,24,1152]{2,1,0:T(8,128)(2,1)S(1)}, bf16[2,192,192]{2,1,0:T(8,128)(2,1)S(1)}, bf16[2,192,192]{2,1...) custom-call(bf16[288,768]{1,0:T(8,128)(2,1)} %bitcast.15, ...), custom_call_target="tpu_custom_call" | custom-call | tf_op jit(solution)/shard_map/begin_kernel/pallas_call | solution.py:510
  4.0 16.3 %all_to_all.40 = bf16[8,24,1152]{2,1,0:T(8,128)(2,1)S(1)} all-to-all(bf16[8,24,1152]{2,1,0:T(8,128)(2,1)S(1)} %get-tuple-element.26), channel_id=1, replica_groups=mesh['lat'=16,'lon'=8,'ens'=2] {'lon'}, dimensions={0} | all-to-all | bytes 884736 | tf_op jit(solution)/shard_map/all_to_all | solution.py:523
  20.2 0.4 width_kernel.2
  20.7 26.5 %all_to_all.41.wire = bf16[16,108,128]{2,1,0:T(8,128)(2,1)S(1)} all-to-all(bf16[16,108,128]{2,1,0:T(8,128)(2,1)S(1)} %width_kernel.2), channel_id=1, replica_groups=mesh['lat'=16,'lon'=8,'ens'=2] {'lat'}, dimensions={0} | all-to-all | bytes 884736 | tf_op jit(solution)/shard_map/all_to_all | solution.py:523
  47.2 6.3 %filter_kernel.1 = (bf16[16,108,128]{2,1,0:T(8,128)(2,1)S(1)}, bf16[6,384,256]{2,1,0:T(8,128)(2,1)}, bf16[6,384,256]{2,1,0:T(8,128)(2,1)}) custom-call(bf16[16,108,128]{2,1,0:T(8,128)(2,1)S(1)} %all_to_all.41.wire, bf16[2,384,192]{2,1,0:T(8,128)(2,1)S(1)} %get-tuple-element.28.forward, bf16[2,192,384]{2,1,0:T(8,128)(2,1)S(1)} %get-tuple-element.29.inverse, ...), custom_call_target="tpu_custom_call" | custom-call | tf_op jit(solution)/shard_map/filter_kernel/pallas_call | solution.py:510
  53.5 18.6 %all_to_all.42.wire = bf16[16,108,128]{2,1,0:T(8,128)(2,1)S(1)} all-to-all(bf16[16,108,128]{2,1,0:T(8,128)(2,1)S(1)} %get-tuple-element.34), channel_id=1, replica_groups=mesh['lat'=16,'lon'=8,'ens'=2] {'lat'}, dimensions={0} | all-to-all | bytes 884736 | tf_op jit(solution)/shard_map/all_to_all | solution.py:523
  72.1 1.3 width_back_kernel.2
  73.3 3.5 %all-to-all-start.3 = ((bf16[8,24,1152]{2,1,0:T(8,128)(2,1)}), bf16[8,24,1152]{2,1,0:T(8,128)(2,1)S(1)}, u32[]{:S(2)}, u32[]{:S(2)}) async-start(bf16[8,24,1152]{2,1,0:T(8,128)(2,1)} %bitcast.6), calls=%async_computation.3 | async-start | bytes 884736 | tf_op jit(solution)/shard_map/all_to_all | solution.py:523
  76.8 5.0 %gradient_kernel.1 = (f32[288,3072]{1,0:T(8,128)}, f32[288,768]{1,0:T(8,128)S(1)}, bf16[288,768]{1,0:T(8,128)(2,1)S(1)}) custom-call(bf16[288,768]{1,0:T(8,128)(2,1)} %bitcast.16, bf16[288,768]{1,0:T(8,128)(2,1)S(1)} %get-tuple-element.36.lowereds, bf16[288,768]{1,0:T(8,128)(2,1)} %bitcast.18, bf16[3072,768]{1,0:T(8,128)(2,1)} %fc2s.3), custom_call_target="tpu_custom_call" | custom-call | flops 1358954496 | tf_op jit(solution)/shard_map/gradient_kernel/pallas_call | solution.py:510
  81.8 4.6 %all-to-all-done.3.wire = bf16[8,24,1152]{2,1,0:T(8,128)(2,1)S(1)} async-done(((bf16[8,24,1152]{2,1,0:T(8,128)(2,1)}), bf16[8,24,1152]{2,1,0:T(8,128)(2,1)S(1)}, u32[]{:S(2)}, u32[]{:S(2)}) %all-to-all-start.3) | async-done | bytes 442400 | tf_op jit(solution)/shard_map/all_to_all | solution.py:523
  86.4 10.3 %token_kernel.1 = (bf16[288,3072]{1,0:T(8,128)(2,1)}, bf16[288,768]{1,0:T(8,128)(2,1)}, bf16[288,768]{1,0:T(8,128)(2,1)}, bf16[8,24,1152]{2,1,0:T(8,128)(2,1)S(1)}) custom-call(bf16[8,24,1152]{2,1,0:T(8,128)(2,1)S(1)} %all-to-all-done.3.wire, f32[288,768]{1,0:T(8,128)S(1)} %get-tuple-element.37.base, bf16[288,768]{1,0:T(8,128)(2,1)S(1)} %get-tuple-element.38.cotangent, ...), custom_call_target="tpu_custom_call" | custom-call | flops 2717908992 | tf_op jit(solution)/shard_map/token_kernel/pallas_call | solution.py:510
  96.7 0.0 copy-start
  96.7 0.0 copy-start.1
  96.7 12.8 %all_to_all.43 = bf16[8,24,1152]{2,1,0:T(8,128)(2,1)S(1)} all-to-all(bf16[8,24,1152]{2,1,0:T(8,128)(2,1)S(1)} %get-tuple-element.44), channel_id=1, replica_groups=mesh['lat'=16,'lon'=8,'ens'=2] {'lon'}, dimensions={0} | all-to-all | bytes 884736 | tf_op jit(solution)/shard_map/all_to_all | solution.py:523
  109.5 0.4 width_kernel.3
  110.0 20.1 %all_to_all.44.wire = bf16[16,108,128]{2,1,0:T(8,128)(2,1)S(1)} all-to-all(bf16[16,108,128]{2,1,0:T(8,128)(2,1)S(1)} %width_kernel.3), channel_id=1, replica_groups=mesh['lat'=16,'lon'=8,'ens'=2] {'lat'}, dimensions={0} | all-to-all | bytes 884736 | tf_op jit(solution)/shard_map/all_to_all | solution.py:523
  130.1 0.0 copy-done
  130.1 0.0 copy-done.1
  130.1 4.6 %adjoint_kernel.1 = bf16[16,108,128]{2,1,0:T(8,128)(2,1)S(1)} custom-call(bf16[16,108,128]{2,1,0:T(8,128)(2,1)S(1)} %all_to_all.44.wire, bf16[2,384,192]{2,1,0:T(8,128)(2,1)S(1)} %get-tuple-element.28.forward, bf16[2,192,384]{2,1,0:T(8,128)(2,1)S(1)} %get-tuple-element.29.inverse, f32[2,96,96]{2,1,0:T(8,128)S(1)} %get-tuple-element.30.weight1, ...), custom_call_target="tpu_custom_call" | custom-call | tf_op jit(solution)/shard_map/adjoint_kernel/pallas_call | solution.py:510
  134.7 18.6 %all_to_all.45.wire = bf16[16,108,128]{2,1,0:T(8,128)(2,1)S(1)} all-to-all(bf16[16,108,128]{2,1,0:T(8,128)(2,1)S(1)} %adjoint_kernel.1), channel_id=1, replica_groups=mesh['lat'=16,'lon'=8,'ens'=2] {'lat'}, dimensions={0} | all-to-all | bytes 884736 | tf_op jit(solution)/shard_map/all_to_all | solution.py:523
  153.3 1.3 width_back_kernel.3
  154.6 3.5 %all-to-all-start.7 = ((bf16[8,24,1152]{2,1,0:T(8,128)(2,1)}), bf16[8,24,1152]{2,1,0:T(8,128)(2,1)S(1)}, u32[]{:S(2)}, u32[]{:S(2)}) async-start(bf16[8,24,1152]{2,1,0:T(8,128)(2,1)} %bitcast.11), calls=%async_computation.7 | async-start | bytes 884736 | tf_op jit(solution)/shard_map/all_to_all | solution.py:523
  158.1 5.0 %advance_kernel.1 = (bf16[288,768]{1,0:T(8,128)(2,1)}, f32[288,768]{1,0:T(8,128)S(1)}, f32[288,1]{1,0:T(8,128)S(1)}, bf16[288,768]{1,0:T(8,128)(2,1)S(1)}) custom-call(bf16[288,3072]{1,0:T(8,128)(2,1)} %get-tuple-element.40.hiddens, bf16[3072,768]{1,0:T(8,128)(2,1)} %fc2s.3, f32[768]{0:T(1024)} %bias2s.1, bf16[288,768]{1,0:T(8,128)(2,1)} %get-tuple-element.41.mixeds, ...), custom_call_target="tpu_custom_call" | custom-call | flops 1358954496 | tf_op jit(solution)/shard_map/advance_kernel/pallas_call | solution.py:510
  163.1 4.5 %all-to-all-done.7.wire = bf16[8,24,1152]{2,1,0:T(8,128)(2,1)S(1)} async-done(((bf16[8,24,1152]{2,1,0:T(8,128)(2,1)}), bf16[8,24,1152]{2,1,0:T(8,128)(2,1)S(1)}, u32[]{:S(2)}, u32[]{:S(2)}) %all-to-all-start.7) | async-done | bytes 442400 | tf_op jit(solution)/shard_map/all_to_all | solution.py:523
  167.7 2.6 %finish_kernel.1 = bf16[288,768]{1,0:T(8,128)(2,1)} custom-call(bf16[8,24,1152]{2,1,0:T(8,128)(2,1)S(1)} %all-to-all-done.7.wire, f32[288,768]{1,0:T(8,128)S(1)} %get-tuple-element.47.normed, f32[288,1]{1,0:T(8,128)S(1)} %get-tuple-element.48.scale, bf16[288,768]{1,0:T(8,128)(2,1)S(1)} %get-tuple-element.49.grad_mixed, f32[768]{0:T(1024)} %gains.5), custom_call_target="tpu_custom_call" | custom-call | tf_op jit(solution)/shard_map/finish_kernel/pallas_call | solution.py:510
Async XLA Ops:
  73.3 13.1 %all-to-all-start.3 = ((bf16[8,24,1152]{2,1,0:T(8,128)(2,1)}), bf16[8,24,1152]{2,1,0:T(8,128)(2,1)S(1)}, u32[]{:S(2)}, u32[]{:S(2)}) async-start(bf16[8,24,1152]{2,1,0:T(8,128)(2,1)} %bitcast.6), calls=%async_computation.3 | async-start | bytes 884736 | tf_op jit(solution)/shard_map/all_to_all | solution.py:523
  96.7 33.4 %copy-start = (bf16[6,384,256]{2,1,0:T(8,128)(2,1)S(1)}, bf16[6,384,256]{2,1,0:T(8,128)(2,1)}, u32[]{:S(2)}) copy-start(bf16[6,384,256]{2,1,0:T(8,128)(2,1)} %get-tuple-element.45.slopes) | copy-start | bytes 3538948
  96.7 33.4 %copy-start.1 = (bf16[6,384,256]{2,1,0:T(8,128)(2,1)S(1)}, bf16[6,384,256]{2,1,0:T(8,128)(2,1)}, u32[]{:S(2)}) copy-start(bf16[6,384,256]{2,1,0:T(8,128)(2,1)} %get-tuple-element.46.squares) | copy-start | bytes 3538948
  154.6 13.1 %all-to-all-start.7 = ((bf16[8,24,1152]{2,1,0:T(8,128)(2,1)}), bf16[8,24,1152]{2,1,0:T(8,128)(2,1)S(1)}, u32[]{:S(2)}, u32[]{:S(2)}) async-start(bf16[8,24,1152]{2,1,0:T(8,128)(2,1)} %bitcast.11), calls=%async_computation.7 | async-start | bytes 884736 | tf_op jit(solution)/shard_map/all_to_all | solution.py:523

commit v3 on v2

--- a/solution.py
+++ b/solution.py
@@ -21,9 +21,10 @@
 TILES = LANES // 128
 WIRE = TILES * GROUPS
 STRIDE = 109
-CHUNK = 512
+CHUNK = 1536
+BATCH = 6
+BATCHES = GROUPS // BATCH
 CHUNKS = HIDDEN // CHUNK
-UNROLL = 2
 F32, BF16 = jnp.float32, jnp.bfloat16
 
 
@@ -124,11 +125,11 @@
     return values * cumulative, cumulative + values * density
 
 
-def scatter_blocks(blocks, pair, values):
+def scatter_blocks(blocks, batch, values):
     tiles = [values[:, 128 * i : 128 * i + 128] for i in range(6)]
     for j, b in enumerate((*unpack4(*tiles[:3]), *unpack4(*tiles[3:]))):
-        blocks[j, 2 * pair] = b[:COLS]
-        blocks[j, 2 * pair + 1] = b[COLS:]
+        for n in range(BATCH):
+            blocks[j, BATCH * batch + n] = b[COLS * n : COLS * n + COLS]
 
 
 def send_blocks(blocks, wire):
@@ -149,8 +150,9 @@
                 blocks[j, 4 * g + n] = b
 
 
-def gather_blocks(blocks, pair):
-    parts = [jnp.concatenate([blocks[j, 2 * pair], blocks[j, 2 * pair + 1]], axis=0) for j in range(LONS)]
+def gather_blocks(blocks, batch):
+    groups = range(BATCH * batch, BATCH * batch + BATCH)
+    parts = [jnp.concatenate([blocks[j, k] for k in groups], axis=0) for j in range(LONS)]
     return jnp.concatenate([*pack4(*parts[:4]), *pack4(*parts[4:])], axis=1)
 
 
@@ -166,28 +168,24 @@
     return wait
 
 
-def pair_rows(pair):
-    return slice(48 * pair, 48 * pair + 48)
-
-
-def begin_kernel(
-    states, gains, shifts, *rest
-):
-    sources, (lowered, wire), targets = rest[:KEPT], rest[KEPT : KEPT + 2], rest[KEPT + 2 : 2 * KEPT + 2]
-    state, gain, shift, blocks, sem, sem_kept = rest[2 * KEPT + 2 :]
-    vectors = [(gains, gain), (shifts, shift)]
-    wait = fetch(sem, *((states.at[pair_rows(n), :], state.at[pair_rows(n), :]) for n in range(GROUPS // 2)), *vectors)
-    wait_kept = fetch(sem_kept, *zip(sources, targets))
-    wait(6, 7)
-    for pair in range(GROUPS // 2):
-        rows = pair_rows(pair)
-        wait(pair)
-        normed, _ = norm(state[rows, :].astype(F32))
+def batch_rows(batch):
+    size = BATCH * COLS
+    return slice(size * batch, size * batch + size)
+
+
+def begin_kernel(states, gains, shifts, wire, state, gain, shift, blocks, sem):
+    fetch(sem, (states, state), (gains, gain), (shifts, shift))(0, 1, 2)
+    for batch in range(BATCHES):
+        normed, _ = norm(state[batch_rows(batch), :].astype(F32))
         value = (normed * row(gain) + row(shift)).astype(BF16)
-        lowered[rows, :] = value
-        scatter_blocks(blocks, pair, value.astype(F32))
+        scatter_blocks(blocks, batch, value.astype(F32))
     send_blocks(blocks, wire)
-    wait_kept(*range(KEPT))
+
+
+def keep_kernel(*refs):
+    sem = refs[-1]
+    half = len(refs) // 2
+    fetch(sem, *zip(refs[:half], refs[half:-1], strict=True))(*range(half))
 
 
 def wire_out(scratch, wire):
@@ -287,7 +285,7 @@
 
 
 def is_packed(q):
-    return jnp.where((q == 0) & (lax.axis_index("lat") == 0), 1, 0)
+    return jnp.where(lax.axis_index("lat") == 0, 1, 0) if q == 0 else 0
 
 
 def filter_kernel(
@@ -301,8 +299,7 @@
     build_bias(bias2, c2)
     spectrum_in(wire, scratch, columns)
 
-    @pl.loop(0, ROWS, unroll=UNROLL)
-    def _(q):
+    for q in range(ROWS):
         which = is_packed(q)
         points = to_points(dot(forward[which], columns[q]).astype(BF16))
         active, slope = gelu_pair(dot(points, w1[...]) + c1[...])
@@ -327,8 +324,7 @@
     build_weight(weight2, square, w2)
     spectrum_in(wire, scratch, columns)
 
-    @pl.loop(0, ROWS, unroll=UNROLL)
-    def _(q):
+    for q in range(ROWS):
         which = is_packed(q)
         spectrum = dot(forward[which], columns[q])
         points = (to_points(spectrum) * squares[q].astype(F32)).astype(BF16)
@@ -349,34 +345,38 @@
 
 
 def gradient_kernel(
-    states, lowereds, cotangents, fc2s,
-    grad_hiddens, base, cotangent,
-    state, lowered, fc2, grad_hidden, sem, sem_in, sem_out,
+    cotangents, states, gain1s, shift1s, gain2s, shift2s, bias1s, fc2s,
+    grad_hiddens, base, cotangent, gain2, shift2, bias1,
+    state, gain1, shift1, fc2, grad_hidden, sem, sem_in, sem_out,
 ):
-    wait = fetch(sem, (cotangents, cotangent), (states, state), (lowereds, lowered))
+    wait = fetch(
+        sem, (cotangents, cotangent), (states, state), (gain1s, gain1), (shift1s, shift1),
+        (gain2s, gain2), (shift2s, shift2), (bias1s, bias1),
+    )
     start_in, wait_in = chunk_copies(sem_in, lambda c: (fc2s.at[c, :], fc2.at[c, :]))
     start_out, wait_out = chunk_copies(sem_out, lambda c: (grad_hidden.at[:, c], grad_hiddens.at[:, c]))
     pl.loop(0, CHUNKS)(start_in)
-    wait(0)
+    wait(*range(7))
+    for batch in range(BATCHES):
+        rows = batch_rows(batch)
+        value = state[rows, :].astype(F32)
+        normed, _ = norm(value)
+        base[rows, :] = (normed * row(gain1) + row(shift1)).astype(BF16).astype(F32) + value
 
     @pl.loop(0, CHUNKS)
     def _(n):
         wait_in(n)
-        grad_hidden[:, pieces(n)] = dot_t(cotangent[...], fc2[pieces(n), :])
+        grad_hidden[:, pieces(n)] = dot_t(cotangent[...], fc2[pieces(n), :]).astype(BF16)
         start_out(n)
 
-    wait(1, 2)
-    base[...] = lowered[...].astype(F32) + state[...].astype(F32)
     pl.loop(0, CHUNKS)(wait_out)
 
 
 def token_kernel(
-    wire, base, cotangent, gains, shifts, fc1s, bias1s, grad_hiddens,
-    hiddens, mixeds, grad_mixeds, wire_next,
-    gain, shift, fc1, bias1, grad_hidden, hidden, mixed, grad_mixed,
-    blocks, rows_in, grad_total, sem, sem_fc1, sem_grad, sem_hidden,
+    wire, base, cotangent, gain, shift, bias1, fc1s, grad_hiddens,
+    hiddens, mixeds, grad_mixed, wire_next,
+    fc1, grad_hidden, hidden, mixed, blocks, rows_in, grad_total, sem, sem_fc1, sem_grad, sem_hidden,
 ):
-    wait = fetch(sem, (gains, gain), (shifts, shift), (bias1s, bias1))
     start_fc1, wait_fc1 = chunk_copies(sem_fc1, lambda c: (fc1s.at[:, c], fc1.at[:, c]))
     start_grad, wait_grad = chunk_copies(sem_grad, lambda c: (grad_hiddens.at[:, c], grad_hidden.at[:, c]))
     start_hidden, wait_hidden = chunk_copies(sem_hidden, lambda c: (hidden.at[:, c], hiddens.at[:, c]))
@@ -387,16 +387,16 @@
         start_grad(n)
 
     receive_blocks(wire, blocks)
-    wait(0, 1, 2)
-    for pair in range(GROUPS // 2):
-        rows = pair_rows(pair)
-        value = (gather_blocks(blocks, pair) + base[rows, :]).astype(BF16)
+    for batch in range(BATCHES):
+        rows = batch_rows(batch)
+        value = (gather_blocks(blocks, batch) + base[rows, :]).astype(BF16)
         mixed[rows, :] = value
         normed, _ = norm(value.astype(F32))
         rows_in[rows, :] = (normed * row(gain) + row(shift)).astype(BF16)
+    keep = fetch(sem, (mixed, mixeds))
     grad_total[...] = jnp.zeros_like(grad_total)
 
-    @pl.loop(0, CHUNKS, unroll=UNROLL)
+    @pl.loop(0, CHUNKS)
     def _(n):
         wait_fc1(n)
         hidden_pre = dot(rows_in[...], fc1[:, pieces(n)]) + bias1[:, pieces(n)]
@@ -404,28 +404,27 @@
         hidden[:, pieces(n)] = value.astype(BF16)
         start_hidden(n)
         wait_grad(n)
-        grad_pre = (grad_hidden[:, pieces(n)] * slope).astype(BF16)
+        grad_pre = (grad_hidden[:, pieces(n)].astype(F32) * slope).astype(BF16)
         grad_total[...] += dot_t(grad_pre, fc1[:, pieces(n)])
 
-    for pair in range(GROUPS // 2):
-        rows = pair_rows(pair)
+    for batch in range(BATCHES):
+        rows = batch_rows(batch)
         normed, scale = norm(mixed[rows, :].astype(F32))
         grad = cotangent[rows, :].astype(F32) + norm_backward(grad_total[rows, :], row(gain), normed, scale)
         grad = grad.astype(BF16)
         grad_mixed[rows, :] = grad
-        scatter_blocks(blocks, pair, grad.astype(F32))
-    keep = fetch(sem, (mixed, mixeds), (grad_mixed, grad_mixeds))
+        scatter_blocks(blocks, batch, grad.astype(F32))
     send_blocks(blocks, wire_next)
+    keep(0)
     pl.loop(0, CHUNKS)(wait_hidden)
-    keep(0, 1)
 
 
 def advance_kernel(
-    hiddens, fc2s, bias2s, mixeds, grad_mixeds, states,
-    advanced, normed, scale, grad_mixed,
+    hiddens, fc2s, bias2s, mixeds, states,
+    advanced, normed, scale,
     hidden, fc2, bias2, mixed, state, total, sem, sem_hidden, sem_fc2,
 ):
-    wait = fetch(sem, (bias2s, bias2), (mixeds, mixed), (grad_mixeds, grad_mixed), (states, state))
+    wait = fetch(sem, (bias2s, bias2), (mixeds, mixed), (states, state))
     start_hidden, wait_hidden = chunk_copies(sem_hidden, lambda c: (hiddens.at[:, c], hidden.at[:, c]))
     start_fc2, wait_fc2 = chunk_copies(sem_fc2, lambda c: (fc2s.at[c, :], fc2.at[c, :]))
 
@@ -434,9 +433,9 @@
         start_hidden(n)
         start_fc2(n)
 
-    wait(0, 1, 2, 3)
-    for pair in range(GROUPS // 2):
-        rows = pair_rows(pair)
+    wait(0, 1, 2)
+    for batch in range(BATCHES):
+        rows = batch_rows(batch)
         normed[rows, :], scale[rows, :] = norm(state[rows, :].astype(F32))
     total[...] = mixed[...].astype(F32) + row(bias2)
 
@@ -449,18 +448,16 @@
     advanced[...] = total[...].astype(BF16)
 
 
-def finish_kernel(wire, normed, scale, grad_mixed, gains, sensitivity, gain, blocks, out, sem, sem_out):
-    wait = fetch(sem, (gains, gain))
+def finish_kernel(wire, normed, scale, grad_mixed, gain, sensitivity, blocks, out, sem_out):
     receive_blocks(wire, blocks)
-    wait(0)
     copies = []
-    for pair in range(GROUPS // 2):
-        rows = pair_rows(pair)
+    for batch in range(BATCHES):
+        rows = batch_rows(batch)
         grad = grad_mixed[rows, :].astype(F32)
-        grad_lowered = gather_blocks(blocks, pair) + grad
+        grad_lowered = gather_blocks(blocks, batch) + grad
         grad = grad + norm_backward(grad_lowered, row(gain), normed[rows, :], scale[rows, :])
         out[rows, :] = grad.astype(BF16)
-        copies.append(pltpu.make_async_copy(out.at[rows, :], sensitivity.at[rows, :], sem_out.at[pair]))
+        copies.append(pltpu.make_async_copy(out.at[rows, :], sensitivity.at[rows, :], sem_out.at[batch]))
         copies[-1].start()
     for c in copies:
         c.wait()
@@ -479,6 +476,7 @@
 
 
 LON_WIRE = near(LONS, COLS, LANES)
+FIELD = near(WIDTH, LANES)
 LAT_WIRE = near(LATS, WIRE, 128)
 BLOCKS = vmem(LONS, GROUPS, COLS, 128, dtype=F32)
 PEERS = vmem(LATS * STRIDE, 128, dtype=F32)
@@ -495,7 +493,7 @@
 TOKEN, UNITS = (TOKENS, FEATURES), (TOKENS, HIDDEN)
 VECTOR = vmem(FEATURES, dtype=F32)
 PARAMS = pltpu.CompilerParams(vmem_limit_bytes=48 * 1024 * 1024)
-KEPT = 8
+MATMUL = 2 * TOKENS * FEATURES * HIDDEN
 
 
 def place(space):
@@ -530,8 +528,83 @@
 
 def to_lon(wire, table):
     scratch = [PEERS, vmem(WIDTH, LANES)]
-    field = call(width_back_kernel, near(WIDTH, LANES), scratch, [exchange(wire, "lat"), table], "nh")
+    field = call(width_back_kernel, FIELD, scratch, [exchange(wire, "lat"), table], "nh")
     return exchange(field.reshape(LON_WIRE.shape), "lon")
+
+
+def begin(*operands):
+    return call(
+        begin_kernel,
+        LON_WIRE,
+        [vmem(*TOKEN), VECTOR, VECTOR, BLOCKS, sems(3)],
+        operands,
+        "fff",
+    )
+
+
+def keep(*arrays):
+    shapes = tuple(vmem(*k.shape, dtype=k.dtype) for k in arrays)
+    return call(keep_kernel, shapes, [sems(len(arrays))], arrays, "f" * len(arrays), MATMUL)
+
+
+def filtered(wire, *kept):
+    return call(
+        filter_kernel,
+        (LAT_WIRE, pltpu.HBM(POINTS, BF16), pltpu.HBM(POINTS, BF16)),
+        [vmem(*POINTS), vmem(*POINTS), *SPECTRAL, WIDE_BIAS, WIDE_BIAS, sems(2)],
+        [wire, *kept],
+        "nhhhhhh",
+    )
+
+
+def adjoint(wire, *operands):
+    return call(adjoint_kernel, LAT_WIRE, [*SPECTRAL], [wire, *operands], "nhhhhnn")
+
+
+def gradient(*operands):
+    return call(
+        gradient_kernel,
+        (pltpu.HBM(UNITS, BF16), vmem(*TOKEN, dtype=F32), vmem(*TOKEN), VECTOR, VECTOR, vmem(1, HIDDEN, dtype=F32)),
+        [vmem(*TOKEN), VECTOR, VECTOR, vmem(HIDDEN, FEATURES), vmem(*UNITS)]
+        + [sems(7), sems(CHUNKS), sems(CHUNKS)],
+        operands,
+        "ffffffff",
+        MATMUL,
+    )
+
+
+def token(*operands):
+    return call(
+        token_kernel,
+        (pltpu.HBM(UNITS, BF16), pltpu.HBM(TOKEN, BF16), vmem(*TOKEN), LON_WIRE),
+        [vmem(FEATURES, HIDDEN), vmem(*UNITS), vmem(*UNITS), vmem(*TOKEN), BLOCKS, vmem(*TOKEN)]
+        + [vmem(*TOKEN, dtype=F32), sems(1), sems(CHUNKS), sems(CHUNKS), sems(CHUNKS)],
+        operands,
+        "nhhhhhff",
+        2 * MATMUL,
+    )
+
+
+def advance(*operands):
+    return call(
+        advance_kernel,
+        (near(*TOKEN), vmem(*TOKEN, dtype=F32), vmem(TOKENS, 1, dtype=F32)),
+        [vmem(*UNITS), vmem(HIDDEN, FEATURES), VECTOR, vmem(*TOKEN), vmem(*TOKEN), vmem(*TOKEN, dtype=F32)]
+        + [sems(3), sems(CHUNKS), sems(CHUNKS)],
+        operands,
+        "fffff",
+        MATMUL,
+    )
+
+
+def finish(*operands):
+    return call(
+        finish_kernel,
+        pltpu.HBM(TOKEN, BF16),
+        [BLOCKS, vmem(*TOKEN), sems(BATCHES)],
+        operands,
+        "nhhhh",
+    )
 
 
 def shards(
@@ -540,78 +613,26 @@
 ):
     tokens = state.reshape(TOKEN)
     cot = cotangent.reshape(TOKEN)
-    matmul = 2 * TOKENS * FEATURES * HIDDEN
-    kept = [
-        *map(jnp.asarray, (*width_tables(), *height_tables())),
-        spec_weight1.reshape(2, BLOCK, BLOCK),
-        spec_bias1.reshape(2, BLOCK),
-        spec_weight2.reshape(2, BLOCK, BLOCK),
-        spec_bias2.reshape(2, BLOCK),
-    ]
-
-    lowered, wire, *kept = call(
-        begin_kernel,
-        (near(*TOKEN), LON_WIRE, *(vmem(*k.shape, dtype=k.dtype) for k in kept)),
-        [vmem(*TOKEN), VECTOR, VECTOR, BLOCKS, sems(8), sems(KEPT)],
-        [tokens, norm1_gain, norm1_bias, *kept],
-        "fff" + "f" * KEPT,
-    )
-    width_forward, width_inverse, height_forward, height_inverse, weight1, bias1, weight2, bias2 = kept
+    tables = map(jnp.asarray, (*width_tables(), *height_tables()))
+    weight1, weight2 = spec_weight1.reshape(2, BLOCK, BLOCK), spec_weight2.reshape(2, BLOCK, BLOCK)
+    bias1, bias2 = spec_bias1.reshape(2, BLOCK), spec_bias2.reshape(2, BLOCK)
+
+    wire = begin(tokens, norm1_gain, norm1_bias)
+    width_forward, width_inverse, height_forward, height_inverse, weight1, weight2, bias1, bias2, gain1 = keep(
+        *tables, weight1, weight2, bias1, bias2, norm1_gain
+    )
     wire = to_lat(wire, width_forward)
-    wire, slopes, squares = call(
-        filter_kernel,
-        (LAT_WIRE, pltpu.HBM(POINTS, BF16), pltpu.HBM(POINTS, BF16)),
-        [vmem(*POINTS), vmem(*POINTS), *SPECTRAL, WIDE_BIAS, WIDE_BIAS, sems(2)],
-        [wire, height_forward, height_inverse, weight1, bias1, weight2, bias2],
-        "nhhhhhh",
-    )
-    grad_hidden, base, cot = call(
-        gradient_kernel,
-        (pltpu.HBM(UNITS, F32), vmem(*TOKEN, dtype=F32), vmem(*TOKEN)),
-        [vmem(*TOKEN), vmem(*TOKEN), vmem(HIDDEN, FEATURES), vmem(*UNITS, dtype=F32)]
-        + [sems(3), sems(CHUNKS), sems(CHUNKS)],
-        [tokens, lowered, cot, fc2_weight],
-        "fnff",
-        matmul,
+    wire, slopes, squares = filtered(wire, height_forward, height_inverse, weight1, bias1, weight2, bias2)
+    grad_hidden, base, cot, gain2, shift2, fc1_bias = gradient(
+        cot, tokens, norm1_gain, norm1_bias, norm2_gain, norm2_bias, fc1_bias.reshape(1, -1), fc2_weight
     )
     wire = to_lon(wire, width_inverse)
-
-    hidden, mixed, grad_mixed, wire = call(
-        token_kernel,
-        (pltpu.HBM(UNITS, BF16), pltpu.HBM(TOKEN, BF16), pltpu.HBM(TOKEN, BF16), LON_WIRE),
-        [VECTOR, VECTOR, vmem(FEATURES, HIDDEN), vmem(1, HIDDEN, dtype=F32), vmem(*UNITS, dtype=F32)]
-        + [vmem(*UNITS), vmem(*TOKEN), vmem(*TOKEN), BLOCKS, vmem(*TOKEN), vmem(*TOKEN, dtype=F32)]
-        + [sems(3), sems(CHUNKS), sems(CHUNKS), sems(CHUNKS)],
-        [wire, base, cot, norm2_gain, norm2_bias, fc1_weight, fc1_bias.reshape(1, -1), grad_hidden],
-        "nhhfffff",
-        2 * matmul,
-    )
-
+    hidden, mixed, grad_mixed, wire = token(wire, base, cot, gain2, shift2, fc1_bias, fc1_weight, grad_hidden)
     wire = to_lat(wire, width_forward)
-    wire = call(
-        adjoint_kernel,
-        LAT_WIRE,
-        [*SPECTRAL],
-        [wire, height_forward, height_inverse, weight1, weight2, slopes, squares],
-        "nhhhhnn",
-    )
-    advanced, normed, scale, grad_mixed = call(
-        advance_kernel,
-        (near(*TOKEN), vmem(*TOKEN, dtype=F32), vmem(TOKENS, 1, dtype=F32), vmem(*TOKEN)),
-        [vmem(*UNITS), vmem(HIDDEN, FEATURES), VECTOR, vmem(*TOKEN), vmem(*TOKEN), vmem(*TOKEN, dtype=F32)]
-        + [sems(4), sems(CHUNKS), sems(CHUNKS)],
-        [hidden, fc2_weight, fc2_bias, mixed, grad_mixed, tokens],
-        "ffffff",
-        matmul,
-    )
+    wire = adjoint(wire, height_forward, height_inverse, weight1, weight2, slopes, squares)
+    advanced, normed, scale = advance(hidden, fc2_weight, fc2_bias, mixed, tokens)
     wire = to_lon(wire, width_inverse)
-    sensitivity = call(
-        finish_kernel,
-        pltpu.HBM(TOKEN, BF16),
-        [VECTOR, BLOCKS, vmem(*TOKEN), sems(1), sems(GROUPS // 2)],
-        [wire, normed, scale, grad_mixed, norm1_gain],
-        "nhhhf",
-    )
+    sensitivity = finish(wire, normed, scale, grad_mixed, gain1)
     return advanced.reshape(state.shape), sensitivity.reshape(state.shape)
 
 

time: 171 us -> 164 us (0.959)
  blocking collectives: 113 us -> 95.8 us
  waiting for transfers between devices: 9.1 us -> 17.3 us
  starting transfers between devices: 6.94 us -> 14.4 us
  Pallas kernels: 40.5 us -> 34.9 us
    all_to_all x6 -> x5, blocking collectives: 113 us -> 95.8 us  [exchange(): return lax.all_to_all(value, axis, split_axis=0, concat_axis=0, tiled=True)]
    all_to_all x2 -> x3, waiting for transfers between devices: 9.1 us -> 17.3 us  [exchange(): return lax.all_to_all(value, axis, split_axis=0, concat_axis=0, tiled=True)]
    all_to_all x2 -> x3, starting transfers between devices: 6.94 us -> 14.4 us  [exchange(): return lax.all_to_all(value, axis, split_axis=0, concat_axis=0, tiled=True)]
    pallas_call x11 -> x12, Pallas kernels: 40.5 us -> 34.9 us  [call(): pl.pallas_call(kernel, out_shape=out_shape, in_specs=[place(m) for m in s...]
  transfers between devices with their start and end apart: 2 -> 3, of which waited for: 2 -> 3; matrix products, arithmetic and copies ran while one was open for 0% -> 0% of each run, Pallas kernels for 6% -> 7%
where the time goes in v3:
time: 164 us; the launch traced here: 163 us
  blocking collectives  95.8 us (58%)
  Pallas kernels  34.9 us (21%)
  waiting for transfers between devices  17.3 us (11%)
  starting transfers between devices  14.4 us (9%)
    all_to_all x5, blocking collectives, exchange(): return lax.all_to_all(value, axis, split_axis=0, concat_axis=0, tiled=True)  95.8 us
    pallas_call x12, Pallas kernels, call(): pl.pallas_call(kernel, out_shape=out_shape, in_specs=[place(m) for m in s...  34.9 us
    all_to_all x3, waiting for transfers between devices, exchange(): return lax.all_to_all(value, axis, split_axis=0, concat_axis=0, tiled=True)  17.3 us
    all_to_all x3, starting transfers between devices, exchange(): return lax.all_to_all(value, axis, split_axis=0, concat_axis=0, tiled=True)  14.4 us
  transfers between devices with their start and end apart: 3, of which 3 were waited for; matrix products, arithmetic and copies ran while one was open for 0% of the time, Pallas kernels for 7%

profile of v3, /device:TPU:1, one launch (start us, length us, event | category | flops | bytes accessed | tf_op | source)
XLA Modules:
  0.0 163.4 jit_solution(3178714416361112152)
XLA Ops:
  0.6 2.5 %begin_kernel.1 = bf16[8,24,1152]{2,1,0:T(8,128)(2,1)} custom-call(bf16[288,768]{1,0:T(8,128)(2,1)} %bitcast.15, f32[768]{0:T(1024)} %gain1s.1, f32[768]{0:T(1024)} %shift1s.1), custom_call_target="tpu_custom_call" | custom-call | tf_op jit(solution)/shard_map/begin_kernel/pallas_call | solution.py:508
  3.1 7.5 %all-to-all-start = ((bf16[8,24,1152]{2,1,0:T(8,128)(2,1)}), bf16[8,24,1152]{2,1,0:T(8,128)(2,1)S(1)}, u32[]{:S(2)}, u32[]{:S(2)}) async-start(bf16[8,24,1152]{2,1,0:T(8,128)(2,1)} %begin_kernel.1), calls=%async_computation | async-start | bytes 884736 | tf_op jit(solution)/shard_map/all_to_all | solution.py:521
  10.6 1.4 keep_kernel.1
  12.0 8.1 %all-to-all-done = bf16[8,24,1152]{2,1,0:T(8,128)(2,1)S(1)} async-done(((bf16[8,24,1152]{2,1,0:T(8,128)(2,1)}), bf16[8,24,1152]{2,1,0:T(8,128)(2,1)S(1)}, u32[]{:S(2)}, u32[]{:S(2)}) %all-to-all-start) | async-done | bytes 442400 | tf_op jit(solution)/shard_map/all_to_all | solution.py:521
  20.1 0.4 width_kernel.2
  20.6 25.7 %all_to_all.40.wire = bf16[16,108,128]{2,1,0:T(8,128)(2,1)S(1)} all-to-all(bf16[16,108,128]{2,1,0:T(8,128)(2,1)S(1)} %width_kernel.2), channel_id=1, replica_groups=mesh['lat'=16,'lon'=8,'ens'=2] {'lat'}, dimensions={0} | all-to-all | bytes 884736 | tf_op jit(solution)/shard_map/all_to_all | solution.py:521
  46.3 5.1 %filter_kernel.1 = (bf16[16,108,128]{2,1,0:T(8,128)(2,1)S(1)}, bf16[6,384,256]{2,1,0:T(8,128)(2,1)}, bf16[6,384,256]{2,1,0:T(8,128)(2,1)}) custom-call(bf16[16,108,128]{2,1,0:T(8,128)(2,1)S(1)} %all_to_all.40.wire, bf16[2,384,192]{2,1,0:T(8,128)(2,1)S(1)} %get-tuple-element.28.forward, bf16[2,192,384]{2,1,0:T(8,128)(2,1)S(1)} %get-tuple-element.29.inverse, ...), custom_call_target="tpu_custom_call" | custom-call | tf_op jit(solution)/shard_map/filter_kernel/pallas_call | solution.py:508
  51.3 18.6 %all_to_all.41.wire = bf16[16,108,128]{2,1,0:T(8,128)(2,1)S(1)} all-to-all(bf16[16,108,128]{2,1,0:T(8,128)(2,1)S(1)} %get-tuple-element.34), channel_id=1, replica_groups=mesh['lat'=16,'lon'=8,'ens'=2] {'lat'}, dimensions={0} | all-to-all | bytes 884736 | tf_op jit(solution)/shard_map/all_to_all | solution.py:521
  69.9 1.3 width_back_kernel.2
  71.2 3.5 %all-to-all-start.3 = ((bf16[8,24,1152]{2,1,0:T(8,128)(2,1)}), bf16[8,24,1152]{2,1,0:T(8,128)(2,1)S(1)}, u32[]{:S(2)}, u32[]{:S(2)}) async-start(bf16[8,24,1152]{2,1,0:T(8,128)(2,1)} %bitcast.6), calls=%async_computation.3 | async-start | bytes 884736 | tf_op jit(solution)/shard_map/all_to_all | solution.py:521
  74.7 4.9 %gradient_kernel.1 = (bf16[288,3072]{1,0:T(8,128)(2,1)}, f32[288,768]{1,0:T(8,128)S(1)}, bf16[288,768]{1,0:T(8,128)(2,1)S(1)}, f32[768]{0:T(1024)S(1)}, f32[768]{0:T(1024)S(1)}, /*index=5*/f32[1,3072]{1,0:T(1,128)S(1)}) custom-call(bf16[288,768]{1,0:T(8,128)(2,1)} %bitcast.18, bf16[288,768]{1,0:T(8,128)(2,1)} %bitcast.16, f32[768]{0:T(1024)} %gain1s.1, ...), custom_call_target="tpu_custom_call" | custom-call | flops 1358954496 | tf_op jit(solution)/shard_map/gradient_kernel/pallas_call | solution.py:508
  79.6 4.6 %all-to-all-done.3.wire = bf16[8,24,1152]{2,1,0:T(8,128)(2,1)S(1)} async-done(((bf16[8,24,1152]{2,1,0:T(8,128)(2,1)}), bf16[8,24,1152]{2,1,0:T(8,128)(2,1)S(1)}, u32[]{:S(2)}, u32[]{:S(2)}) %all-to-all-start.3) | async-done | bytes 442400 | tf_op jit(solution)/shard_map/all_to_all | solution.py:521
  84.2 7.8 %token_kernel.1 = (bf16[288,3072]{1,0:T(8,128)(2,1)}, bf16[288,768]{1,0:T(8,128)(2,1)}, bf16[288,768]{1,0:T(8,128)(2,1)S(1)}, bf16[8,24,1152]{2,1,0:T(8,128)(2,1)S(1)}) custom-call(bf16[8,24,1152]{2,1,0:T(8,128)(2,1)S(1)} %all-to-all-done.3.wire, f32[288,768]{1,0:T(8,128)S(1)} %get-tuple-element.36.base, bf16[288,768]{1,0:T(8,128)(2,1)S(1)} %get-tuple-element.37.cotangent, ...), custom_call_target="tpu_custom_call" | custom-call | flops 2717908992 | tf_op jit(solution)/shard_map/token_kernel/pallas_call | solution.py:508
  92.1 0.0 copy-start
  92.1 0.0 copy-start.1
  92.1 12.8 %all_to_all.42 = bf16[8,24,1152]{2,1,0:T(8,128)(2,1)S(1)} all-to-all(bf16[8,24,1152]{2,1,0:T(8,128)(2,1)S(1)} %get-tuple-element.45), channel_id=1, replica_groups=mesh['lat'=16,'lon'=8,'ens'=2] {'lon'}, dimensions={0} | all-to-all | bytes 884736 | tf_op jit(solution)/shard_map/all_to_all | solution.py:521
  104.9 0.4 width_kernel.3
  105.3 20.0 %all_to_all.43.wire = bf16[16,108,128]{2,1,0:T(8,128)(2,1)S(1)} all-to-all(bf16[16,108,128]{2,1,0:T(8,128)(2,1)S(1)} %width_kernel.3), channel_id=1, replica_groups=mesh['lat'=16,'lon'=8,'ens'=2] {'lat'}, dimensions={0} | all-to-all | bytes 884736 | tf_op jit(solution)/shard_map/all_to_all | solution.py:521
  125.3 0.0 copy-done
  125.3 0.0 copy-done.1
  125.3 3.2 %adjoint_kernel.1 = bf16[16,108,128]{2,1,0:T(8,128)(2,1)S(1)} custom-call(bf16[16,108,128]{2,1,0:T(8,128)(2,1)S(1)} %all_to_all.43.wire, bf16[2,384,192]{2,1,0:T(8,128)(2,1)S(1)} %get-tuple-element.28.forward, bf16[2,192,384]{2,1,0:T(8,128)(2,1)S(1)} %get-tuple-element.29.inverse, f32[2,96,96]{2,1,0:T(8,128)S(1)} %get-tuple-element.30.weight1, ...), custom_call_target="tpu_custom_call" | custom-call | tf_op jit(solution)/shard_map/adjoint_kernel/pallas_call | solution.py:508
  128.5 18.7 %all_to_all.44.wire = bf16[16,108,128]{2,1,0:T(8,128)(2,1)S(1)} all-to-all(bf16[16,108,128]{2,1,0:T(8,128)(2,1)S(1)} %adjoint_kernel.1), channel_id=1, replica_groups=mesh['lat'=16,'lon'=8,'ens'=2] {'lat'}, dimensions={0} | all-to-all | bytes 884736 | tf_op jit(solution)/shard_map/all_to_all | solution.py:521
  147.2 1.3 width_back_kernel.3
  148.6 3.5 %all-to-all-start.7 = ((bf16[8,24,1152]{2,1,0:T(8,128)(2,1)}), bf16[8,24,1152]{2,1,0:T(8,128)(2,1)S(1)}, u32[]{:S(2)}, u32[]{:S(2)}) async-start(bf16[8,24,1152]{2,1,0:T(8,128)(2,1)} %bitcast.11), calls=%async_computation.7 | async-start | bytes 884736 | tf_op jit(solution)/shard_map/all_to_all | solution.py:521
  152.0 4.9 %advance_kernel.1 = (bf16[288,768]{1,0:T(8,128)(2,1)}, f32[288,768]{1,0:T(8,128)S(1)}, f32[288,1]{1,0:T(8,128)S(1)}) custom-call(bf16[288,3072]{1,0:T(8,128)(2,1)} %get-tuple-element.42.hiddens, bf16[3072,768]{1,0:T(8,128)(2,1)} %fc2s.3, f32[768]{0:T(1024)} %bias2s.1, bf16[288,768]{1,0:T(8,128)(2,1)} %get-tuple-element.43.mixeds, bf16[288,768]{1,0:T(8,128)(2,1)} %bitcast.17), custom_call_target="tpu_custom_call" | custom-call | flops 1358954496 | tf_op jit(solution)/shard_map/advance_kernel/pallas_call | solution.py:508
  157.0 4.6 %all-to-all-done.7.wire = bf16[8,24,1152]{2,1,0:T(8,128)(2,1)S(1)} async-done(((bf16[8,24,1152]{2,1,0:T(8,128)(2,1)}), bf16[8,24,1152]{2,1,0:T(8,128)(2,1)S(1)}, u32[]{:S(2)}, u32[]{:S(2)}) %all-to-all-start.7) | async-done | bytes 442400 | tf_op jit(solution)/shard_map/all_to_all | solution.py:521
  161.6 1.6 finish_kernel.1
Async XLA Ops:
  3.1 17.0 %all-to-all-start = ((bf16[8,24,1152]{2,1,0:T(8,128)(2,1)}), bf16[8,24,1152]{2,1,0:T(8,128)(2,1)S(1)}, u32[]{:S(2)}, u32[]{:S(2)}) async-start(bf16[8,24,1152]{2,1,0:T(8,128)(2,1)} %begin_kernel.1), calls=%async_computation | async-start | bytes 884736 | tf_op jit(solution)/shard_map/all_to_all | solution.py:521
  71.2 13.1 %all-to-all-start.3 = ((bf16[8,24,1152]{2,1,0:T(8,128)(2,1)}), bf16[8,24,1152]{2,1,0:T(8,128)(2,1)S(1)}, u32[]{:S(2)}, u32[]{:S(2)}) async-start(bf16[8,24,1152]{2,1,0:T(8,128)(2,1)} %bitcast.6), calls=%async_computation.3 | async-start | bytes 884736 | tf_op jit(solution)/shard_map/all_to_all | solution.py:521
  92.1 33.3 %copy-start = (bf16[6,384,256]{2,1,0:T(8,128)(2,1)S(1)}, bf16[6,384,256]{2,1,0:T(8,128)(2,1)}, u32[]{:S(2)}) copy-start(bf16[6,384,256]{2,1,0:T(8,128)(2,1)} %get-tuple-element.46.slopes) | copy-start | bytes 3538948
  92.1 33.2 %copy-start.1 = (bf16[6,384,256]{2,1,0:T(8,128)(2,1)S(1)}, bf16[6,384,256]{2,1,0:T(8,128)(2,1)}, u32[]{:S(2)}) copy-start(bf16[6,384,256]{2,1,0:T(8,128)(2,1)} %get-tuple-element.47.squares) | copy-start | bytes 3538948
  148.6 13.1 %all-to-all-start.7 = ((bf16[8,24,1152]{2,1,0:T(8,128)(2,1)}), bf16[8,24,1152]{2,1,0:T(8,128)(2,1)S(1)}, u32[]{:S(2)}, u32[]{:S(2)}) async-start(bf16[8,24,1152]{2,1,0:T(8,128)(2,1)} %bitcast.11), calls=%async_computation.7 | async-start | bytes 884736 | tf_op jit(solution)/shard_map/all_to_all | solution.py:521

commit v4 on v3

--- a/solution.py
+++ b/solution.py
@@ -21,7 +21,8 @@
 TILES = LANES // 128
 WIRE = TILES * GROUPS
 STRIDE = 109
-CHUNK = 1536
+CHUNK = 1024
+STEP = 256
 BATCH = 6
 BATCHES = GROUPS // BATCH
 CHUNKS = HIDDEN // CHUNK
@@ -180,12 +181,6 @@
         value = (normed * row(gain) + row(shift)).astype(BF16)
         scatter_blocks(blocks, batch, value.astype(F32))
     send_blocks(blocks, wire)
-
-
-def keep_kernel(*refs):
-    sem = refs[-1]
-    half = len(refs) // 2
-    fetch(sem, *zip(refs[:half], refs[half:-1], strict=True))(*range(half))
 
 
 def wire_out(scratch, wire):
@@ -344,19 +339,17 @@
     return lambda n: one(n).start(), lambda n: one(n).wait()
 
 
-def gradient_kernel(
-    cotangents, states, gain1s, shift1s, gain2s, shift2s, bias1s, fc2s,
-    grad_hiddens, base, cotangent, gain2, shift2, bias1,
-    state, gain1, shift1, fc2, grad_hidden, sem, sem_in, sem_out,
-):
+def gradient_kernel(cotangents, states, shift1s, fc2s, gain1s, *refs):
+    more, (grad_hiddens, base, cotangent), rest = refs[:HELD], refs[HELD : HELD + 3], refs[HELD + 3 :]
+    gain1, held, (state, shift1, fc2, grad_hidden, sem, sem_in, sem_out) = rest[0], rest[1 : HELD + 1], rest[HELD + 1 :]
     wait = fetch(
         sem, (cotangents, cotangent), (states, state), (gain1s, gain1), (shift1s, shift1),
-        (gain2s, gain2), (shift2s, shift2), (bias1s, bias1),
+        *zip(more, held, strict=True),
     )
     start_in, wait_in = chunk_copies(sem_in, lambda c: (fc2s.at[c, :], fc2.at[c, :]))
     start_out, wait_out = chunk_copies(sem_out, lambda c: (grad_hidden.at[:, c], grad_hiddens.at[:, c]))
     pl.loop(0, CHUNKS)(start_in)
-    wait(*range(7))
+    wait(*range(4 + HELD))
     for batch in range(BATCHES):
         rows = batch_rows(batch)
         value = state[rows, :].astype(F32)
@@ -373,19 +366,14 @@
 
 
 def token_kernel(
-    wire, base, cotangent, gain, shift, bias1, fc1s, grad_hiddens,
+    wire, base, cotangent, gain, shift, bias1, fc1s, grad_hidden,
     hiddens, mixeds, grad_mixed, wire_next,
-    fc1, grad_hidden, hidden, mixed, blocks, rows_in, grad_total, sem, sem_fc1, sem_grad, sem_hidden,
+    fc1, hidden, mixed, blocks, rows_in, grad_pre, grad_total, sem, sem_fc1, sem_hidden,
 ):
     start_fc1, wait_fc1 = chunk_copies(sem_fc1, lambda c: (fc1s.at[:, c], fc1.at[:, c]))
-    start_grad, wait_grad = chunk_copies(sem_grad, lambda c: (grad_hiddens.at[:, c], grad_hidden.at[:, c]))
     start_hidden, wait_hidden = chunk_copies(sem_hidden, lambda c: (hidden.at[:, c], hiddens.at[:, c]))
 
-    @pl.loop(0, CHUNKS)
-    def _(n):
-        start_fc1(n)
-        start_grad(n)
-
+    pl.loop(0, CHUNKS)(start_fc1)
     receive_blocks(wire, blocks)
     for batch in range(BATCHES):
         rows = batch_rows(batch)
@@ -394,18 +382,25 @@
         normed, _ = norm(value.astype(F32))
         rows_in[rows, :] = (normed * row(gain) + row(shift)).astype(BF16)
     keep = fetch(sem, (mixed, mixeds))
-    grad_total[...] = jnp.zeros_like(grad_total)
-
-    @pl.loop(0, CHUNKS)
-    def _(n):
-        wait_fc1(n)
-        hidden_pre = dot(rows_in[...], fc1[:, pieces(n)]) + bias1[:, pieces(n)]
+
+    def units(n):
+        return slice(STEP * n, STEP * n + STEP)
+
+    def before(n):
+        if STEP * n % CHUNK == 0:
+            wait_fc1(STEP * n // CHUNK)
+        return dot(rows_in[...], fc1[:, units(n)]) + bias1[:, units(n)]
+
+    hidden_pre = before(0)
+    for n in range(HIDDEN // STEP):
+        following = before(n + 1) if n + 1 < HIDDEN // STEP else None
         value, slope = gelu_pair(hidden_pre)
-        hidden[:, pieces(n)] = value.astype(BF16)
-        start_hidden(n)
-        wait_grad(n)
-        grad_pre = (grad_hidden[:, pieces(n)].astype(F32) * slope).astype(BF16)
-        grad_total[...] += dot_t(grad_pre, fc1[:, pieces(n)])
+        hidden[:, units(n)] = value.astype(BF16)
+        grad_pre[:, units(n)] = (grad_hidden[:, units(n)].astype(F32) * slope).astype(BF16)
+        if (STEP * n + STEP) % CHUNK == 0:
+            start_hidden(STEP * n // CHUNK)
+        hidden_pre = following
+    grad_total[...] = dot_t(grad_pre[...], fc1[...])
 
     for batch in range(BATCHES):
         rows = batch_rows(batch)
@@ -493,6 +488,7 @@
 TOKEN, UNITS = (TOKENS, FEATURES), (TOKENS, HIDDEN)
 VECTOR = vmem(FEATURES, dtype=F32)
 PARAMS = pltpu.CompilerParams(vmem_limit_bytes=48 * 1024 * 1024)
+HELD = 11
 MATMUL = 2 * TOKENS * FEATURES * HIDDEN
 
 
@@ -542,11 +538,6 @@
     )
 
 
-def keep(*arrays):
-    shapes = tuple(vmem(*k.shape, dtype=k.dtype) for k in arrays)
-    return call(keep_kernel, shapes, [sems(len(arrays))], arrays, "f" * len(arrays), MATMUL)
-
-
 def filtered(wire, *kept):
     return call(
         filter_kernel,
@@ -561,14 +552,14 @@
     return call(adjoint_kernel, LAT_WIRE, [*SPECTRAL], [wire, *operands], "nhhhhnn")
 
 
-def gradient(*operands):
+def gradient(cot, tokens, shift1, fc2, gain1, *arrays):
     return call(
         gradient_kernel,
-        (pltpu.HBM(UNITS, BF16), vmem(*TOKEN, dtype=F32), vmem(*TOKEN), VECTOR, VECTOR, vmem(1, HIDDEN, dtype=F32)),
-        [vmem(*TOKEN), VECTOR, VECTOR, vmem(HIDDEN, FEATURES), vmem(*UNITS)]
-        + [sems(7), sems(CHUNKS), sems(CHUNKS)],
-        operands,
-        "ffffffff",
+        (pltpu.HBM(UNITS, BF16), vmem(*TOKEN, dtype=F32), vmem(*TOKEN))
+        + tuple(vmem(*a.shape, dtype=a.dtype) for a in (gain1, *arrays)),
+        [vmem(*TOKEN), VECTOR, vmem(HIDDEN, FEATURES), vmem(*UNITS), sems(4 + HELD), sems(CHUNKS), sems(CHUNKS)],
+        [cot, tokens, shift1, fc2, gain1, *arrays],
+        "fffff" + "f" * len(arrays),
         MATMUL,
     )
 
@@ -577,10 +568,10 @@
     return call(
         token_kernel,
         (pltpu.HBM(UNITS, BF16), pltpu.HBM(TOKEN, BF16), vmem(*TOKEN), LON_WIRE),
-        [vmem(FEATURES, HIDDEN), vmem(*UNITS), vmem(*UNITS), vmem(*TOKEN), BLOCKS, vmem(*TOKEN)]
-        + [vmem(*TOKEN, dtype=F32), sems(1), sems(CHUNKS), sems(CHUNKS), sems(CHUNKS)],
+        [vmem(FEATURES, HIDDEN), vmem(*UNITS), vmem(*TOKEN), BLOCKS, vmem(*TOKEN)]
+        + [vmem(*UNITS), vmem(*TOKEN, dtype=F32), sems(1), sems(CHUNKS), sems(CHUNKS)],
         operands,
-        "nhhhhhff",
+        "nhhhhhfh",
         2 * MATMUL,
     )
 
@@ -618,14 +609,14 @@
     bias1, bias2 = spec_bias1.reshape(2, BLOCK), spec_bias2.reshape(2, BLOCK)
 
     wire = begin(tokens, norm1_gain, norm1_bias)
-    width_forward, width_inverse, height_forward, height_inverse, weight1, weight2, bias1, bias2, gain1 = keep(
-        *tables, weight1, weight2, bias1, bias2, norm1_gain
-    )
+    grad_hidden, base, cot, gain1, *held = gradient(
+        cot, tokens, norm1_bias, fc2_weight, norm1_gain,
+        *tables, weight1, weight2, bias1, bias2, norm2_gain, norm2_bias, fc1_bias.reshape(1, -1),
+    )
+    width_forward, width_inverse, height_forward, height_inverse, weight1, weight2, bias1, bias2 = held[:8]
+    gain2, shift2, fc1_bias = held[8:]
     wire = to_lat(wire, width_forward)
     wire, slopes, squares = filtered(wire, height_forward, height_inverse, weight1, bias1, weight2, bias2)
-    grad_hidden, base, cot, gain2, shift2, fc1_bias = gradient(
-        cot, tokens, norm1_gain, norm1_bias, norm2_gain, norm2_bias, fc1_bias.reshape(1, -1), fc2_weight
-    )
     wire = to_lon(wire, width_inverse)
     hidden, mixed, grad_mixed, wire = token(wire, base, cot, gain2, shift2, fc1_bias, fc1_weight, grad_hidden)
     wire = to_lat(wire, width_forward)

time: 164 us -> 162 us (0.988)
  blocking collectives: 95.8 us -> 109 us
  waiting for transfers between devices: 17.3 us -> 9.22 us
  starting transfers between devices: 14.4 us -> 10.9 us
  Pallas kernels: 34.9 us -> 31.9 us
    all_to_all x5 -> x6, blocking collectives: 95.8 us -> 109 us  [exchange(): return lax.all_to_all(value, axis, split_axis=0, concat_axis=0, tiled=True)]
    all_to_all x3 -> x2, waiting for transfers between devices: 17.3 us -> 9.22 us  [exchange(): return lax.all_to_all(value, axis, split_axis=0, concat_axis=0, tiled=True)]
    all_to_all x3 -> x2, starting transfers between devices: 14.4 us -> 10.9 us  [exchange(): return lax.all_to_all(value, axis, split_axis=0, concat_axis=0, tiled=True)]
    pallas_call x12 -> x11, Pallas kernels: 34.9 us -> 31.9 us  [call(): pl.pallas_call(kernel, out_shape=out_shape, in_specs=[place(m) for m in s...]
  transfers between devices with their start and end apart: 3 -> 2, of which waited for: 3 -> 2; matrix products, arithmetic and copies ran while one was open for 0% -> 0% of each run, Pallas kernels for 7% -> 6%
where the time goes in v4:
time: 162 us
  blocking collectives  109 us (67%)
  Pallas kernels  31.9 us (20%)
  starting transfers between devices  10.9 us (7%)
  waiting for transfers between devices  9.22 us (6%)
    all_to_all x6, blocking collectives, exchange(): return lax.all_to_all(value, axis, split_axis=0, concat_axis=0, tiled=True)  109 us
    pallas_call x11, Pallas kernels, call(): pl.pallas_call(kernel, out_shape=out_shape, in_specs=[place(m) for m in s...  31.9 us
    all_to_all x2, starting transfers between devices, exchange(): return lax.all_to_all(value, axis, split_axis=0, concat_axis=0, tiled=True)  10.9 us
    all_to_all x2, waiting for transfers between devices, exchange(): return lax.all_to_all(value, axis, split_axis=0, concat_axis=0, tiled=True)  9.22 us
  transfers between devices with their start and end apart: 2, of which 2 were waited for; matrix products, arithmetic and copies ran while one was open for 0% of the time, Pallas kernels for 6%

profile of v4, /device:TPU:1, one launch (start us, length us, event | category | flops | bytes accessed | tf_op | source)
XLA Modules:
  0.0 161.9 jit_solution(18108546334183958396)
XLA Ops:
  0.6 2.5 %begin_kernel.1 = bf16[8,24,1152]{2,1,0:T(8,128)(2,1)} custom-call(bf16[288,768]{1,0:T(8,128)(2,1)} %bitcast.16, f32[768]{0:T(1024)} %gain1s.1, f32[768]{0:T(1024)} %shift1s.1), custom_call_target="tpu_custom_call" | custom-call | tf_op jit(solution)/shard_map/begin_kernel/pallas_call | solution.py:504
  3.1 7.5 %all-to-all-start = ((bf16[8,24,1152]{2,1,0:T(8,128)(2,1)}), bf16[8,24,1152]{2,1,0:T(8,128)(2,1)S(1)}, u32[]{:S(2)}, u32[]{:S(2)}) async-start(bf16[8,24,1152]{2,1,0:T(8,128)(2,1)} %begin_kernel.1), calls=%async_computation | async-start | bytes 884736 | tf_op jit(solution)/shard_map/all_to_all | solution.py:517
  10.6 5.2 %gradient_kernel.1 = (bf16[288,3072]{1,0:T(8,128)(2,1)}, f32[288,768]{1,0:T(8,128)S(1)}, bf16[288,768]{1,0:T(8,128)(2,1)S(1)}, f32[768]{0:T(1024)S(1)}, bf16[2,1...) custom-call(bf16[288,768]{1,0:T(8,128)(2,1)} %bitcast.19, ...), custom_call_target="tpu_custom_call" | custom-call | flops 1358954496 | tf_op jit(solution)/shard_map/gradient_kernel/pallas_call | solution.py:504
  15.8 4.3 %all-to-all-done = bf16[8,24,1152]{2,1,0:T(8,128)(2,1)S(1)} async-done(((bf16[8,24,1152]{2,1,0:T(8,128)(2,1)}), bf16[8,24,1152]{2,1,0:T(8,128)(2,1)S(1)}, u32[]{:S(2)}, u32[]{:S(2)}) %all-to-all-start) | async-done | bytes 442400 | tf_op jit(solution)/shard_map/all_to_all | solution.py:517
  20.1 0.4 width_kernel.2
  20.6 25.7 %all_to_all.40.wire = bf16[16,108,128]{2,1,0:T(8,128)(2,1)S(1)} all-to-all(bf16[16,108,128]{2,1,0:T(8,128)(2,1)S(1)} %width_kernel.2), channel_id=1, replica_groups=mesh['lat'=16,'lon'=8,'ens'=2] {'lat'}, dimensions={0} | all-to-all | bytes 884736 | tf_op jit(solution)/shard_map/all_to_all | solution.py:517
  46.3 5.0 %filter_kernel.1 = (bf16[16,108,128]{2,1,0:T(8,128)(2,1)S(1)}, bf16[6,384,256]{2,1,0:T(8,128)(2,1)}, bf16[6,384,256]{2,1,0:T(8,128)(2,1)}) custom-call(bf16[16,108,128]{2,1,0:T(8,128)(2,1)S(1)} %all_to_all.40.wire, bf16[2,384,192]{2,1,0:T(8,128)(2,1)S(1)} %get-tuple-element.28.forward, bf16[2,192,384]{2,1,0:T(8,128)(2,1)S(1)} %get-tuple-element.29.inverse, ...), custom_call_target="tpu_custom_call" | custom-call | tf_op jit(solution)/shard_map/filter_kernel/pallas_call | solution.py:504
  51.3 0.0 copy-start.2
  51.3 18.7 %all_to_all.41.wire = bf16[16,108,128]{2,1,0:T(8,128)(2,1)S(1)} all-to-all(bf16[16,108,128]{2,1,0:T(8,128)(2,1)S(1)} %get-tuple-element.34), channel_id=1, replica_groups=mesh['lat'=16,'lon'=8,'ens'=2] {'lat'}, dimensions={0} | all-to-all | bytes 884736 | tf_op jit(solution)/shard_map/all_to_all | solution.py:517
  70.0 0.5 width_back_kernel.2
  70.5 13.1 %all_to_all.42.wire = bf16[8,24,1152]{2,1,0:T(8,128)(2,1)S(1)} all-to-all(bf16[8,24,1152]{2,1,0:T(8,128)(2,1)S(1)} %bitcast.15), channel_id=1, replica_groups=mesh['lat'=16,'lon'=8,'ens'=2] {'lon'}, dimensions={0} | all-to-all | bytes 884736 | tf_op jit(solution)/shard_map/all_to_all | solution.py:517
  83.7 0.0 copy-done.2
  83.7 7.0 %token_kernel.1 = (bf16[288,3072]{1,0:T(8,128)(2,1)}, bf16[288,768]{1,0:T(8,128)(2,1)}, bf16[288,768]{1,0:T(8,128)(2,1)S(1)}, bf16[8,24,1152]{2,1,0:T(8,128)(2,1)S(1)}) custom-call(bf16[8,24,1152]{2,1,0:T(8,128)(2,1)S(1)} %all_to_all.42.wire, f32[288,768]{1,0:T(8,128)S(1)} %get-tuple-element.36.base, bf16[288,768]{1,0:T(8,128)(2,1)S(1)} %get-tuple-element.37.cotangent, ...), custom_call_target="tpu_custom_call" | custom-call | flops 2717908992 | tf_op jit(solution)/shard_map/token_kernel/pallas_call | solution.py:504
  90.7 0.0 copy-start
  90.7 0.0 copy-start.1
  90.7 12.4 %all_to_all.43 = bf16[8,24,1152]{2,1,0:T(8,128)(2,1)S(1)} all-to-all(bf16[8,24,1152]{2,1,0:T(8,128)(2,1)S(1)} %get-tuple-element.45), channel_id=1, replica_groups=mesh['lat'=16,'lon'=8,'ens'=2] {'lon'}, dimensions={0} | all-to-all | bytes 884736 | tf_op jit(solution)/shard_map/all_to_all | solution.py:517
  103.2 0.4 width_kernel.3
  103.6 20.4 %all_to_all.44.wire = bf16[16,108,128]{2,1,0:T(8,128)(2,1)S(1)} all-to-all(bf16[16,108,128]{2,1,0:T(8,128)(2,1)S(1)} %width_kernel.3), channel_id=1, replica_groups=mesh['lat'=16,'lon'=8,'ens'=2] {'lat'}, dimensions={0} | all-to-all | bytes 884736 | tf_op jit(solution)/shard_map/all_to_all | solution.py:517
  124.0 0.0 copy-done
  124.0 0.0 copy-done.1
  124.0 3.2 %adjoint_kernel.1 = bf16[16,108,128]{2,1,0:T(8,128)(2,1)S(1)} custom-call(bf16[16,108,128]{2,1,0:T(8,128)(2,1)S(1)} %all_to_all.44.wire, bf16[2,384,192]{2,1,0:T(8,128)(2,1)S(1)} %get-tuple-element.28.forward, bf16[2,192,384]{2,1,0:T(8,128)(2,1)S(1)} %get-tuple-element.29.inverse, f32[2,96,96]{2,1,0:T(8,128)S(1)} %get-tuple-element.30.weight1, ...), custom_call_target="tpu_custom_call" | custom-call | tf_op jit(solution)/shard_map/adjoint_kernel/pallas_call | solution.py:504
  127.2 18.5 %all_to_all.45.wire = bf16[16,108,128]{2,1,0:T(8,128)(2,1)S(1)} all-to-all(bf16[16,108,128]{2,1,0:T(8,128)(2,1)S(1)} %adjoint_kernel.1), channel_id=1, replica_groups=mesh['lat'=16,'lon'=8,'ens'=2] {'lat'}, dimensions={0} | all-to-all | bytes 884736 | tf_op jit(solution)/shard_map/all_to_all | solution.py:517
  145.8 1.3 width_back_kernel.3
  147.1 3.5 %all-to-all-start.7 = ((bf16[8,24,1152]{2,1,0:T(8,128)(2,1)}), bf16[8,24,1152]{2,1,0:T(8,128)(2,1)S(1)}, u32[]{:S(2)}, u32[]{:S(2)}) async-start(bf16[8,24,1152]{2,1,0:T(8,128)(2,1)} %bitcast.11), calls=%async_computation.7 | async-start | bytes 884736 | tf_op jit(solution)/shard_map/all_to_all | solution.py:517
  150.6 4.7 %advance_kernel.1 = (bf16[288,768]{1,0:T(8,128)(2,1)}, f32[288,768]{1,0:T(8,128)S(1)}, f32[288,1]{1,0:T(8,128)S(1)}) custom-call(bf16[288,3072]{1,0:T(8,128)(2,1)} %get-tuple-element.42.hiddens, bf16[3072,768]{1,0:T(8,128)(2,1)} %fc2s.3, f32[768]{0:T(1024)} %bias2s.1, bf16[288,768]{1,0:T(8,128)(2,1)} %get-tuple-element.43.mixeds, bf16[288,768]{1,0:T(8,128)(2,1)} %bitcast.18), custom_call_target="tpu_custom_call" | custom-call | flops 1358954496 | tf_op jit(solution)/shard_map/advance_kernel/pallas_call | solution.py:504
  155.3 4.9 %all-to-all-done.7.wire = bf16[8,24,1152]{2,1,0:T(8,128)(2,1)S(1)} async-done(((bf16[8,24,1152]{2,1,0:T(8,128)(2,1)}), bf16[8,24,1152]{2,1,0:T(8,128)(2,1)S(1)}, u32[]{:S(2)}, u32[]{:S(2)}) %all-to-all-start.7) | async-done | bytes 442400 | tf_op jit(solution)/shard_map/all_to_all | solution.py:517
  160.2 1.6 finish_kernel.1
Async XLA Ops:
  3.1 17.0 %all-to-all-start = ((bf16[8,24,1152]{2,1,0:T(8,128)(2,1)}), bf16[8,24,1152]{2,1,0:T(8,128)(2,1)S(1)}, u32[]{:S(2)}, u32[]{:S(2)}) async-start(bf16[8,24,1152]{2,1,0:T(8,128)(2,1)} %begin_kernel.1), calls=%async_computation | async-start | bytes 884736 | tf_op jit(solution)/shard_map/all_to_all | solution.py:517
  51.3 32.4 %copy-start.2 = (bf16[288,3072]{1,0:T(8,128)(2,1)S(1)}, bf16[288,3072]{1,0:T(8,128)(2,1)}, u32[]{:S(2)}) copy-start(bf16[288,3072]{1,0:T(8,128)(2,1)} %get-tuple-element.41.grad_hidden) | copy-start | bytes 5308420
  90.7 33.3 %copy-start = (bf16[6,384,256]{2,1,0:T(8,128)(2,1)S(1)}, bf16[6,384,256]{2,1,0:T(8,128)(2,1)}, u32[]{:S(2)}) copy-start(bf16[6,384,256]{2,1,0:T(8,128)(2,1)} %get-tuple-element.46.slopes) | copy-start | bytes 3538948
  90.7 33.3 %copy-start.1 = (bf16[6,384,256]{2,1,0:T(8,128)(2,1)S(1)}, bf16[6,384,256]{2,1,0:T(8,128)(2,1)}, u32[]{:S(2)}) copy-start(bf16[6,384,256]{2,1,0:T(8,128)(2,1)} %get-tuple-element.47.squares) | copy-start | bytes 3538948
  147.1 13.1 %all-to-all-start.7 = ((bf16[8,24,1152]{2,1,0:T(8,128)(2,1)}), bf16[8,24,1152]{2,1,0:T(8,128)(2,1)S(1)}, u32[]{:S(2)}, u32[]{:S(2)}) async-start(bf16[8,24,1152]{2,1,0:T(8,128)(2,1)} %bitcast.11), calls=%async_computation.7 | async-start | bytes 884736 | tf_op jit(solution)/shard_map/all_to_all | solution.py:517

commit v5 on v4

--- a/solution.py
+++ b/solution.py
@@ -284,10 +284,11 @@
 
 
 def filter_kernel(
-    wire, forward, inverse, weight1, bias1, weight2, bias2,
-    wire_back, slopes_out, squares_out,
-    slopes, squares, scratch, columns, backs, square, w1, w2, c1, c2, sem,
+    wire, forward, inverse, weight1, bias1, weight2, bias2, fc1s,
+    wire_back, slopes_out, squares_out, fc1,
+    slopes, squares, scratch, columns, backs, square, w1, w2, c1, c2, sem, sem_token,
 ):
+    wait_token = fetch(sem_token, (fc1s, fc1))
     build_weight(weight1, square, w1)
     build_weight(weight2, square, w2)
     build_bias(bias1, c1)
@@ -308,6 +309,7 @@
     keep = fetch(sem, (slopes, slopes_out), (squares, squares_out))
     spectrum_out(backs, scratch, wire_back)
     keep(0, 1)
+    wait_token(0)
 
 
 def adjoint_kernel(
@@ -366,14 +368,12 @@
 
 
 def token_kernel(
-    wire, base, cotangent, gain, shift, bias1, fc1s, grad_hidden,
+    wire, base, cotangent, gain, shift, bias1, fc1, grad_hidden,
     hiddens, mixeds, grad_mixed, wire_next,
-    fc1, hidden, mixed, blocks, rows_in, grad_pre, grad_total, sem, sem_fc1, sem_hidden,
+    hidden, mixed, blocks, rows_in, grad_pre, grad_total, sem, sem_hidden,
 ):
-    start_fc1, wait_fc1 = chunk_copies(sem_fc1, lambda c: (fc1s.at[:, c], fc1.at[:, c]))
     start_hidden, wait_hidden = chunk_copies(sem_hidden, lambda c: (hidden.at[:, c], hiddens.at[:, c]))
 
-    pl.loop(0, CHUNKS)(start_fc1)
     receive_blocks(wire, blocks)
     for batch in range(BATCHES):
         rows = batch_rows(batch)
@@ -387,8 +387,6 @@
         return slice(STEP * n, STEP * n + STEP)
 
     def before(n):
-        if STEP * n % CHUNK == 0:
-            wait_fc1(STEP * n // CHUNK)
         return dot(rows_in[...], fc1[:, units(n)]) + bias1[:, units(n)]
 
     hidden_pre = before(0)
@@ -487,7 +485,7 @@
 WIDE_BIAS = vmem(1, 256, dtype=F32)
 TOKEN, UNITS = (TOKENS, FEATURES), (TOKENS, HIDDEN)
 VECTOR = vmem(FEATURES, dtype=F32)
-PARAMS = pltpu.CompilerParams(vmem_limit_bytes=48 * 1024 * 1024)
+PARAMS = pltpu.CompilerParams(vmem_limit_bytes=40 * 1024 * 1024)
 HELD = 11
 MATMUL = 2 * TOKENS * FEATURES * HIDDEN
 
@@ -538,13 +536,13 @@
     )
 
 
-def filtered(wire, *kept):
+def filtered(*operands):
     return call(
         filter_kernel,
-        (LAT_WIRE, pltpu.HBM(POINTS, BF16), pltpu.HBM(POINTS, BF16)),
-        [vmem(*POINTS), vmem(*POINTS), *SPECTRAL, WIDE_BIAS, WIDE_BIAS, sems(2)],
-        [wire, *kept],
-        "nhhhhhh",
+        (LAT_WIRE, pltpu.HBM(POINTS, BF16), pltpu.HBM(POINTS, BF16), vmem(FEATURES, HIDDEN)),
+        [vmem(*POINTS), vmem(*POINTS), *SPECTRAL, WIDE_BIAS, WIDE_BIAS, sems(2), sems(1)],
+        operands,
+        "nhhhhhhf",
     )
 
 
@@ -568,10 +566,10 @@
     return call(
         token_kernel,
         (pltpu.HBM(UNITS, BF16), pltpu.HBM(TOKEN, BF16), vmem(*TOKEN), LON_WIRE),
-        [vmem(FEATURES, HIDDEN), vmem(*UNITS), vmem(*TOKEN), BLOCKS, vmem(*TOKEN)]
-        + [vmem(*UNITS), vmem(*TOKEN, dtype=F32), sems(1), sems(CHUNKS), sems(CHUNKS)],
+        [vmem(*UNITS), vmem(*TOKEN), BLOCKS, vmem(*TOKEN)]
+        + [vmem(*UNITS), vmem(*TOKEN, dtype=F32), sems(1), sems(CHUNKS)],
         operands,
-        "nhhhhhfh",
+        "nhhhhhhh",
         2 * MATMUL,
     )
 
@@ -616,9 +614,11 @@
     width_forward, width_inverse, height_forward, height_inverse, weight1, weight2, bias1, bias2 = held[:8]
     gain2, shift2, fc1_bias = held[8:]
     wire = to_lat(wire, width_forward)
-    wire, slopes, squares = filtered(wire, height_forward, height_inverse, weight1, bias1, weight2, bias2)
+    wire, slopes, squares, fc1 = filtered(
+        wire, height_forward, height_inverse, weight1, bias1, weight2, bias2, fc1_weight
+    )
     wire = to_lon(wire, width_inverse)
-    hidden, mixed, grad_mixed, wire = token(wire, base, cot, gain2, shift2, fc1_bias, fc1_weight, grad_hidden)
+    hidden, mixed, grad_mixed, wire = token(wire, base, cot, gain2, shift2, fc1_bias, fc1, grad_hidden)
     wire = to_lat(wire, width_forward)
     wire = adjoint(wire, height_forward, height_inverse, weight1, weight2, slopes, squares)
     advanced, normed, scale = advance(hidden, fc2_weight, fc2_bias, mixed, tokens)

time: 162 us -> 161 us (level)
  no operation moved by 1% of the time
where the time goes in v5:
time: 161 us; the launch traced here: 160 us
  blocking collectives  109 us (68%)
  Pallas kernels  30.7 us (19%)
  starting transfers between devices  10.9 us (7%)
  waiting for transfers between devices  9.22 us (6%)
    all_to_all x6, blocking collectives, exchange(): return lax.all_to_all(value, axis, split_axis=0, concat_axis=0, tiled=True)  109 us
    pallas_call x11, Pallas kernels, call(): pl.pallas_call(kernel, out_shape=out_shape, in_specs=[place(m) for m in s...  30.7 us
    all_to_all x2, starting transfers between devices, exchange(): return lax.all_to_all(value, axis, split_axis=0, concat_axis=0, tiled=True)  10.9 us
    all_to_all x2, waiting for transfers between devices, exchange(): return lax.all_to_all(value, axis, split_axis=0, concat_axis=0, tiled=True)  9.22 us
  transfers between devices with their start and end apart: 2, of which 2 were waited for; matrix products, arithmetic and copies ran while one was open for 0% of the time, Pallas kernels for 6%

profile of v5, /device:TPU:1, one launch (start us, length us, event | category | flops | bytes accessed | tf_op | source)
XLA Modules:
  0.0 160.5 jit_solution(2502797084892988593)
XLA Ops:
  0.6 2.5 %begin_kernel.1 = bf16[8,24,1152]{2,1,0:T(8,128)(2,1)} custom-call(bf16[288,768]{1,0:T(8,128)(2,1)} %bitcast.16, f32[768]{0:T(1024)} %gain1s.1, f32[768]{0:T(1024)} %shift1s.1), custom_call_target="tpu_custom_call" | custom-call | tf_op jit(solution)/shard_map/begin_kernel/pallas_call | solution.py:502
  3.1 7.5 %all-to-all-start = ((bf16[8,24,1152]{2,1,0:T(8,128)(2,1)}), bf16[8,24,1152]{2,1,0:T(8,128)(2,1)S(1)}, u32[]{:S(2)}, u32[]{:S(2)}) async-start(bf16[8,24,1152]{2,1,0:T(8,128)(2,1)} %begin_kernel.1), calls=%async_computation | async-start | bytes 884736 | tf_op jit(solution)/shard_map/all_to_all | solution.py:515
  10.6 5.2 %gradient_kernel.1 = (bf16[288,3072]{1,0:T(8,128)(2,1)}, f32[288,768]{1,0:T(8,128)S(1)}, bf16[288,768]{1,0:T(8,128)(2,1)S(1)}, f32[768]{0:T(1024)S(1)}, bf16[2,1...) custom-call(bf16[288,768]{1,0:T(8,128)(2,1)} %bitcast.19, ...), custom_call_target="tpu_custom_call" | custom-call | flops 1358954496 | tf_op jit(solution)/shard_map/gradient_kernel/pallas_call | solution.py:502
  15.8 4.3 %all-to-all-done = bf16[8,24,1152]{2,1,0:T(8,128)(2,1)S(1)} async-done(((bf16[8,24,1152]{2,1,0:T(8,128)(2,1)}), bf16[8,24,1152]{2,1,0:T(8,128)(2,1)S(1)}, u32[]{:S(2)}, u32[]{:S(2)}) %all-to-all-start) | async-done | bytes 442400 | tf_op jit(solution)/shard_map/all_to_all | solution.py:515
  20.1 0.4 width_kernel.2
  20.6 25.7 %all_to_all.40.wire = bf16[16,108,128]{2,1,0:T(8,128)(2,1)S(1)} all-to-all(bf16[16,108,128]{2,1,0:T(8,128)(2,1)S(1)} %width_kernel.2), channel_id=1, replica_groups=mesh['lat'=16,'lon'=8,'ens'=2] {'lat'}, dimensions={0} | all-to-all | bytes 884736 | tf_op jit(solution)/shard_map/all_to_all | solution.py:515
  46.3 5.0 %filter_kernel.1 = (bf16[16,108,128]{2,1,0:T(8,128)(2,1)S(1)}, bf16[6,384,256]{2,1,0:T(8,128)(2,1)}, bf16[6,384,256]{2,1,0:T(8,128)(2,1)}, bf16[768,3072]{1,0:T(8,128)(2,1)S(1)}) custom-call(bf16[16,108,128]{2,1,0:T(8,128)(2,1)S(1)} %all_to_all.40.wire, bf16[2,384,192]{2,1,0:T(8,128)(2,1)S(1)} %get-tuple-element.29.forward, ...), custom_call_target="tpu_custom_call" | custom-call | tf_op jit(solution)/shard_map/filter_kernel/pallas_call | solution.py:502
  51.3 0.0 copy-start.2
  51.3 18.7 %all_to_all.41.wire = bf16[16,108,128]{2,1,0:T(8,128)(2,1)S(1)} all-to-all(bf16[16,108,128]{2,1,0:T(8,128)(2,1)S(1)} %get-tuple-element.35), channel_id=1, replica_groups=mesh['lat'=16,'lon'=8,'ens'=2] {'lat'}, dimensions={0} | all-to-all | bytes 884736 | tf_op jit(solution)/shard_map/all_to_all | solution.py:515
  70.0 0.5 width_back_kernel.2
  70.5 13.1 %all_to_all.42.wire = bf16[8,24,1152]{2,1,0:T(8,128)(2,1)S(1)} all-to-all(bf16[8,24,1152]{2,1,0:T(8,128)(2,1)S(1)} %bitcast.15), channel_id=1, replica_groups=mesh['lat'=16,'lon'=8,'ens'=2] {'lon'}, dimensions={0} | all-to-all | bytes 884736 | tf_op jit(solution)/shard_map/all_to_all | solution.py:515
  83.7 0.0 copy-done.2
  83.7 5.8 %token_kernel.1 = (bf16[288,3072]{1,0:T(8,128)(2,1)}, bf16[288,768]{1,0:T(8,128)(2,1)}, bf16[288,768]{1,0:T(8,128)(2,1)S(1)}, bf16[8,24,1152]{2,1,0:T(8,128)(2,1)S(1)}) custom-call(bf16[8,24,1152]{2,1,0:T(8,128)(2,1)S(1)} %all_to_all.42.wire, f32[288,768]{1,0:T(8,128)S(1)} %get-tuple-element.37.base, bf16[288,768]{1,0:T(8,128)(2,1)S(1)} %get-tuple-element.38.cotangent, ...), custom_call_target="tpu_custom_call" | custom-call | flops 2717908992 | tf_op jit(solution)/shard_map/token_kernel/pallas_call | solution.py:502
  89.5 0.0 copy-start
  89.5 0.0 copy-start.1
  89.5 12.3 %all_to_all.43 = bf16[8,24,1152]{2,1,0:T(8,128)(2,1)S(1)} all-to-all(bf16[8,24,1152]{2,1,0:T(8,128)(2,1)S(1)} %get-tuple-element.47), channel_id=1, replica_groups=mesh['lat'=16,'lon'=8,'ens'=2] {'lon'}, dimensions={0} | all-to-all | bytes 884736 | tf_op jit(solution)/shard_map/all_to_all | solution.py:515
  101.8 0.4 width_kernel.3
  102.2 20.1 %all_to_all.44.wire = bf16[16,108,128]{2,1,0:T(8,128)(2,1)S(1)} all-to-all(bf16[16,108,128]{2,1,0:T(8,128)(2,1)S(1)} %width_kernel.3), channel_id=1, replica_groups=mesh['lat'=16,'lon'=8,'ens'=2] {'lat'}, dimensions={0} | all-to-all | bytes 884736 | tf_op jit(solution)/shard_map/all_to_all | solution.py:515
  122.4 0.0 copy-done
  122.4 0.0 copy-done.1
  122.4 3.2 %adjoint_kernel.1 = bf16[16,108,128]{2,1,0:T(8,128)(2,1)S(1)} custom-call(bf16[16,108,128]{2,1,0:T(8,128)(2,1)S(1)} %all_to_all.44.wire, bf16[2,384,192]{2,1,0:T(8,128)(2,1)S(1)} %get-tuple-element.29.forward, bf16[2,192,384]{2,1,0:T(8,128)(2,1)S(1)} %get-tuple-element.30.inverse, f32[2,96,96]{2,1,0:T(8,128)S(1)} %get-tuple-element.31.weight1, ...), custom_call_target="tpu_custom_call" | custom-call | tf_op jit(solution)/shard_map/adjoint_kernel/pallas_call | solution.py:502
  125.6 18.8 %all_to_all.45.wire = bf16[16,108,128]{2,1,0:T(8,128)(2,1)S(1)} all-to-all(bf16[16,108,128]{2,1,0:T(8,128)(2,1)S(1)} %adjoint_kernel.1), channel_id=1, replica_groups=mesh['lat'=16,'lon'=8,'ens'=2] {'lat'}, dimensions={0} | all-to-all | bytes 884736 | tf_op jit(solution)/shard_map/all_to_all | solution.py:515
  144.4 1.3 width_back_kernel.3
  145.7 3.5 %all-to-all-start.7 = ((bf16[8,24,1152]{2,1,0:T(8,128)(2,1)}), bf16[8,24,1152]{2,1,0:T(8,128)(2,1)S(1)}, u32[]{:S(2)}, u32[]{:S(2)}) async-start(bf16[8,24,1152]{2,1,0:T(8,128)(2,1)} %bitcast.11), calls=%async_computation.7 | async-start | bytes 884736 | tf_op jit(solution)/shard_map/all_to_all | solution.py:515
  149.2 4.7 %advance_kernel.1 = (bf16[288,768]{1,0:T(8,128)(2,1)}, f32[288,768]{1,0:T(8,128)S(1)}, f32[288,1]{1,0:T(8,128)S(1)}) custom-call(bf16[288,3072]{1,0:T(8,128)(2,1)} %get-tuple-element.44.hiddens, bf16[3072,768]{1,0:T(8,128)(2,1)} %fc2s.3, f32[768]{0:T(1024)} %bias2s.1, bf16[288,768]{1,0:T(8,128)(2,1)} %get-tuple-element.45.mixeds, bf16[288,768]{1,0:T(8,128)(2,1)} %bitcast.18), custom_call_target="tpu_custom_call" | custom-call | flops 1358954496 | tf_op jit(solution)/shard_map/advance_kernel/pallas_call | solution.py:502
  153.9 4.9 %all-to-all-done.7.wire = bf16[8,24,1152]{2,1,0:T(8,128)(2,1)S(1)} async-done(((bf16[8,24,1152]{2,1,0:T(8,128)(2,1)}), bf16[8,24,1152]{2,1,0:T(8,128)(2,1)S(1)}, u32[]{:S(2)}, u32[]{:S(2)}) %all-to-all-start.7) | async-done | bytes 442400 | tf_op jit(solution)/shard_map/all_to_all | solution.py:515
  158.8 1.6 finish_kernel.1
Async XLA Ops:
  3.1 17.0 %all-to-all-start = ((bf16[8,24,1152]{2,1,0:T(8,128)(2,1)}), bf16[8,24,1152]{2,1,0:T(8,128)(2,1)S(1)}, u32[]{:S(2)}, u32[]{:S(2)}) async-start(bf16[8,24,1152]{2,1,0:T(8,128)(2,1)} %begin_kernel.1), calls=%async_computation | async-start | bytes 884736 | tf_op jit(solution)/shard_map/all_to_all | solution.py:515
  51.3 32.4 %copy-start.2 = (bf16[288,3072]{1,0:T(8,128)(2,1)S(1)}, bf16[288,3072]{1,0:T(8,128)(2,1)}, u32[]{:S(2)}) copy-start(bf16[288,3072]{1,0:T(8,128)(2,1)} %get-tuple-element.43.grad_hidden) | copy-start | bytes 5308420
  89.5 32.9 %copy-start = (bf16[6,384,256]{2,1,0:T(8,128)(2,1)S(1)}, bf16[6,384,256]{2,1,0:T(8,128)(2,1)}, u32[]{:S(2)}) copy-start(bf16[6,384,256]{2,1,0:T(8,128)(2,1)} %get-tuple-element.48.slopes) | copy-start | bytes 3538948
  89.5 32.9 %copy-start.1 = (bf16[6,384,256]{2,1,0:T(8,128)(2,1)S(1)}, bf16[6,384,256]{2,1,0:T(8,128)(2,1)}, u32[]{:S(2)}) copy-start(bf16[6,384,256]{2,1,0:T(8,128)(2,1)} %get-tuple-element.49.squares) | copy-start | bytes 3538948
  145.7 13.1 %all-to-all-start.7 = ((bf16[8,24,1152]{2,1,0:T(8,128)(2,1)}), bf16[8,24,1152]{2,1,0:T(8,128)(2,1)S(1)}, u32[]{:S(2)}, u32[]{:S(2)}) async-start(bf16[8,24,1152]{2,1,0:T(8,128)(2,1)} %bitcast.11), calls=%async_computation.7 | async-start | bytes 884736 | tf_op jit(solution)/shard_map/all_to_all | solution.py:515

commit v6 on v5

--- a/solution.py
+++ b/solution.py
@@ -472,7 +472,7 @@
 FIELD = near(WIDTH, LANES)
 LAT_WIRE = near(LATS, WIRE, 128)
 BLOCKS = vmem(LONS, GROUPS, COLS, 128, dtype=F32)
-PEERS = vmem(LATS * STRIDE, 128, dtype=F32)
+PEERS = vmem(LATS * STRIDE + 15, 128, dtype=F32)
 POINTS = (ROWS, 4 * HEIGHT, 256)
 SPECTRAL = (
     PEERS,

time: 161 us -> 161 us (level)
  no operation moved by 1% of the time
where the time goes in v6:
time: 161 us; the launch traced here: 160 us
  blocking collectives  109 us (68%)
  Pallas kernels  30.7 us (19%)
  starting transfers between devices  10.9 us (7%)
  waiting for transfers between devices  9.22 us (6%)
    all_to_all x6, blocking collectives, exchange(): return lax.all_to_all(value, axis, split_axis=0, concat_axis=0, tiled=True)  109 us
    pallas_call x11, Pallas kernels, call(): pl.pallas_call(kernel, out_shape=out_shape, in_specs=[place(m) for m in s...  30.7 us
    all_to_all x2, starting transfers between devices, exchange(): return lax.all_to_all(value, axis, split_axis=0, concat_axis=0, tiled=True)  10.9 us
    all_to_all x2, waiting for transfers between devices, exchange(): return lax.all_to_all(value, axis, split_axis=0, concat_axis=0, tiled=True)  9.22 us
  transfers between devices with their start and end apart: 2, of which 2 were waited for; matrix products, arithmetic and copies ran while one was open for 0% of the time, Pallas kernels for 6%

profile of v6, /device:TPU:1, one launch (start us, length us, event | category | flops | bytes accessed | tf_op | source)
XLA Modules:
  0.0 160.5 jit_solution(15966453818098006941)
XLA Ops:
  0.6 2.5 %begin_kernel.1 = bf16[8,24,1152]{2,1,0:T(8,128)(2,1)} custom-call(bf16[288,768]{1,0:T(8,128)(2,1)} %bitcast.16, f32[768]{0:T(1024)} %gain1s.1, f32[768]{0:T(1024)} %shift1s.1), custom_call_target="tpu_custom_call" | custom-call | tf_op jit(solution)/shard_map/begin_kernel/pallas_call | solution.py:502
  3.1 7.5 %all-to-all-start = ((bf16[8,24,1152]{2,1,0:T(8,128)(2,1)}), bf16[8,24,1152]{2,1,0:T(8,128)(2,1)S(1)}, u32[]{:S(2)}, u32[]{:S(2)}) async-start(bf16[8,24,1152]{2,1,0:T(8,128)(2,1)} %begin_kernel.1), calls=%async_computation | async-start | bytes 884736 | tf_op jit(solution)/shard_map/all_to_all | solution.py:515
  10.6 5.2 %gradient_kernel.1 = (bf16[288,3072]{1,0:T(8,128)(2,1)}, f32[288,768]{1,0:T(8,128)S(1)}, bf16[288,768]{1,0:T(8,128)(2,1)S(1)}, f32[768]{0:T(1024)S(1)}, bf16[2,1...) custom-call(bf16[288,768]{1,0:T(8,128)(2,1)} %bitcast.19, ...), custom_call_target="tpu_custom_call" | custom-call | flops 1358954496 | tf_op jit(solution)/shard_map/gradient_kernel/pallas_call | solution.py:502
  15.8 4.3 %all-to-all-done = bf16[8,24,1152]{2,1,0:T(8,128)(2,1)S(1)} async-done(((bf16[8,24,1152]{2,1,0:T(8,128)(2,1)}), bf16[8,24,1152]{2,1,0:T(8,128)(2,1)S(1)}, u32[]{:S(2)}, u32[]{:S(2)}) %all-to-all-start) | async-done | bytes 442400 | tf_op jit(solution)/shard_map/all_to_all | solution.py:515
  20.1 0.4 width_kernel.2
  20.6 25.7 %all_to_all.40.wire = bf16[16,108,128]{2,1,0:T(8,128)(2,1)S(1)} all-to-all(bf16[16,108,128]{2,1,0:T(8,128)(2,1)S(1)} %width_kernel.2), channel_id=1, replica_groups=mesh['lat'=16,'lon'=8,'ens'=2] {'lat'}, dimensions={0} | all-to-all | bytes 884736 | tf_op jit(solution)/shard_map/all_to_all | solution.py:515
  46.3 5.0 %filter_kernel.1 = (bf16[16,108,128]{2,1,0:T(8,128)(2,1)S(1)}, bf16[6,384,256]{2,1,0:T(8,128)(2,1)}, bf16[6,384,256]{2,1,0:T(8,128)(2,1)}, bf16[768,3072]{1,0:T(8,128)(2,1)S(1)}) custom-call(bf16[16,108,128]{2,1,0:T(8,128)(2,1)S(1)} %all_to_all.40.wire, bf16[2,384,192]{2,1,0:T(8,128)(2,1)S(1)} %get-tuple-element.29.forward, ...), custom_call_target="tpu_custom_call" | custom-call | tf_op jit(solution)/shard_map/filter_kernel/pallas_call | solution.py:502
  51.3 0.0 copy-start.2
  51.3 18.7 %all_to_all.41.wire = bf16[16,108,128]{2,1,0:T(8,128)(2,1)S(1)} all-to-all(bf16[16,108,128]{2,1,0:T(8,128)(2,1)S(1)} %get-tuple-element.35), channel_id=1, replica_groups=mesh['lat'=16,'lon'=8,'ens'=2] {'lat'}, dimensions={0} | all-to-all | bytes 884736 | tf_op jit(solution)/shard_map/all_to_all | solution.py:515
  70.0 0.5 width_back_kernel.2
  70.5 13.1 %all_to_all.42.wire = bf16[8,24,1152]{2,1,0:T(8,128)(2,1)S(1)} all-to-all(bf16[8,24,1152]{2,1,0:T(8,128)(2,1)S(1)} %bitcast.15), channel_id=1, replica_groups=mesh['lat'=16,'lon'=8,'ens'=2] {'lon'}, dimensions={0} | all-to-all | bytes 884736 | tf_op jit(solution)/shard_map/all_to_all | solution.py:515
  83.7 0.0 copy-done.2
  83.7 5.8 %token_kernel.1 = (bf16[288,3072]{1,0:T(8,128)(2,1)}, bf16[288,768]{1,0:T(8,128)(2,1)}, bf16[288,768]{1,0:T(8,128)(2,1)S(1)}, bf16[8,24,1152]{2,1,0:T(8,128)(2,1)S(1)}) custom-call(bf16[8,24,1152]{2,1,0:T(8,128)(2,1)S(1)} %all_to_all.42.wire, f32[288,768]{1,0:T(8,128)S(1)} %get-tuple-element.37.base, bf16[288,768]{1,0:T(8,128)(2,1)S(1)} %get-tuple-element.38.cotangent, ...), custom_call_target="tpu_custom_call" | custom-call | flops 2717908992 | tf_op jit(solution)/shard_map/token_kernel/pallas_call | solution.py:502
  89.5 0.0 copy-start
  89.5 0.0 copy-start.1
  89.5 12.3 %all_to_all.43 = bf16[8,24,1152]{2,1,0:T(8,128)(2,1)S(1)} all-to-all(bf16[8,24,1152]{2,1,0:T(8,128)(2,1)S(1)} %get-tuple-element.47), channel_id=1, replica_groups=mesh['lat'=16,'lon'=8,'ens'=2] {'lon'}, dimensions={0} | all-to-all | bytes 884736 | tf_op jit(solution)/shard_map/all_to_all | solution.py:515
  101.8 0.4 width_kernel.3
  102.2 20.1 %all_to_all.44.wire = bf16[16,108,128]{2,1,0:T(8,128)(2,1)S(1)} all-to-all(bf16[16,108,128]{2,1,0:T(8,128)(2,1)S(1)} %width_kernel.3), channel_id=1, replica_groups=mesh['lat'=16,'lon'=8,'ens'=2] {'lat'}, dimensions={0} | all-to-all | bytes 884736 | tf_op jit(solution)/shard_map/all_to_all | solution.py:515
  122.4 0.0 copy-done
  122.4 0.0 copy-done.1
  122.4 3.2 %adjoint_kernel.1 = bf16[16,108,128]{2,1,0:T(8,128)(2,1)S(1)} custom-call(bf16[16,108,128]{2,1,0:T(8,128)(2,1)S(1)} %all_to_all.44.wire, bf16[2,384,192]{2,1,0:T(8,128)(2,1)S(1)} %get-tuple-element.29.forward, bf16[2,192,384]{2,1,0:T(8,128)(2,1)S(1)} %get-tuple-element.30.inverse, f32[2,96,96]{2,1,0:T(8,128)S(1)} %get-tuple-element.31.weight1, ...), custom_call_target="tpu_custom_call" | custom-call | tf_op jit(solution)/shard_map/adjoint_kernel/pallas_call | solution.py:502
  125.6 18.8 %all_to_all.45.wire = bf16[16,108,128]{2,1,0:T(8,128)(2,1)S(1)} all-to-all(bf16[16,108,128]{2,1,0:T(8,128)(2,1)S(1)} %adjoint_kernel.1), channel_id=1, replica_groups=mesh['lat'=16,'lon'=8,'ens'=2] {'lat'}, dimensions={0} | all-to-all | bytes 884736 | tf_op jit(solution)/shard_map/all_to_all | solution.py:515
  144.4 1.3 width_back_kernel.3
  145.7 3.5 %all-to-all-start.7 = ((bf16[8,24,1152]{2,1,0:T(8,128)(2,1)}), bf16[8,24,1152]{2,1,0:T(8,128)(2,1)S(1)}, u32[]{:S(2)}, u32[]{:S(2)}) async-start(bf16[8,24,1152]{2,1,0:T(8,128)(2,1)} %bitcast.11), calls=%async_computation.7 | async-start | bytes 884736 | tf_op jit(solution)/shard_map/all_to_all | solution.py:515
  149.2 4.7 %advance_kernel.1 = (bf16[288,768]{1,0:T(8,128)(2,1)}, f32[288,768]{1,0:T(8,128)S(1)}, f32[288,1]{1,0:T(8,128)S(1)}) custom-call(bf16[288,3072]{1,0:T(8,128)(2,1)} %get-tuple-element.44.hiddens, bf16[3072,768]{1,0:T(8,128)(2,1)} %fc2s.3, f32[768]{0:T(1024)} %bias2s.1, bf16[288,768]{1,0:T(8,128)(2,1)} %get-tuple-element.45.mixeds, bf16[288,768]{1,0:T(8,128)(2,1)} %bitcast.18), custom_call_target="tpu_custom_call" | custom-call | flops 1358954496 | tf_op jit(solution)/shard_map/advance_kernel/pallas_call | solution.py:502
  153.9 4.9 %all-to-all-done.7.wire = bf16[8,24,1152]{2,1,0:T(8,128)(2,1)S(1)} async-done(((bf16[8,24,1152]{2,1,0:T(8,128)(2,1)}), bf16[8,24,1152]{2,1,0:T(8,128)(2,1)S(1)}, u32[]{:S(2)}, u32[]{:S(2)}) %all-to-all-start.7) | async-done | bytes 442400 | tf_op jit(solution)/shard_map/all_to_all | solution.py:515
  158.7 1.6 finish_kernel.1
Async XLA Ops:
  3.1 17.0 %all-to-all-start = ((bf16[8,24,1152]{2,1,0:T(8,128)(2,1)}), bf16[8,24,1152]{2,1,0:T(8,128)(2,1)S(1)}, u32[]{:S(2)}, u32[]{:S(2)}) async-start(bf16[8,24,1152]{2,1,0:T(8,128)(2,1)} %begin_kernel.1), calls=%async_computation | async-start | bytes 884736 | tf_op jit(solution)/shard_map/all_to_all | solution.py:515
  51.3 32.4 %copy-start.2 = (bf16[288,3072]{1,0:T(8,128)(2,1)S(1)}, bf16[288,3072]{1,0:T(8,128)(2,1)}, u32[]{:S(2)}) copy-start(bf16[288,3072]{1,0:T(8,128)(2,1)} %get-tuple-element.43.grad_hidden) | copy-start | bytes 5308420
  89.5 32.9 %copy-start = (bf16[6,384,256]{2,1,0:T(8,128)(2,1)S(1)}, bf16[6,384,256]{2,1,0:T(8,128)(2,1)}, u32[]{:S(2)}) copy-start(bf16[6,384,256]{2,1,0:T(8,128)(2,1)} %get-tuple-element.48.slopes) | copy-start | bytes 3538948
  89.5 32.9 %copy-start.1 = (bf16[6,384,256]{2,1,0:T(8,128)(2,1)S(1)}, bf16[6,384,256]{2,1,0:T(8,128)(2,1)}, u32[]{:S(2)}) copy-start(bf16[6,384,256]{2,1,0:T(8,128)(2,1)} %get-tuple-element.49.squares) | copy-start | bytes 3538948
  145.7 13.1 %all-to-all-start.7 = ((bf16[8,24,1152]{2,1,0:T(8,128)(2,1)}), bf16[8,24,1152]{2,1,0:T(8,128)(2,1)S(1)}, u32[]{:S(2)}, u32[]{:S(2)}) async-start(bf16[8,24,1152]{2,1,0:T(8,128)(2,1)} %bitcast.11), calls=%async_computation.7 | async-start | bytes 884736 | tf_op jit(solution)/shard_map/all_to_all | solution.py:515
